TPU v7x, 512 devices: a whole 4x4x16 slice. The times are simulated.
512 devices in a mesh: gx: 16 (over z), gy: 8 (over y, core), gz: 4 (over x).
Axes of the slice: x: 4, y: 4, z: 16, core: 2. Of those that a mesh axis runs over, the one named last changes fastest.
Arguments:
- nodal_warmth_degrees: float32 [3, 3, 3, 64, 32, 512], P(None, None, None, 'gx', 'gy', 'gz'), may hold values from -6 to 6
- thermal_transfer_coefficient: float32 [64, 32, 512], P('gx', 'gy', 'gz'), may hold values from 0.1 to 2
- taken_beam_fraction: float32 [64, 32, 512], P('gx', 'gy', 'gz'), may hold values from 0.3 to 3
- laid_tiers: int32 [16, 8, 4], P('gx', 'gy', 'gz'), may hold values from 64 to 128
- holding_brick_column: int32 [16, 8, 4, 2048, 1], P('gx', 'gy', 'gz'), may hold values from 0 to 15; in each aligned block of 2048 rows (0 to 2047, 2048 to 4095, ..., all dimensions but the last counted through in order) at most 256 rows name the same one
- piece_onto_solid_brick: int32 [16, 8, 4, 2048], P('gx', 'gy', 'gz'), may hold values from 0 to 255, as said below
- deformation_change: float32 [6, 8, 131072], P(None, None, ('gx', 'gy', 'gz')), may hold values from -0.06 to 0.06
- earlier_tension_state: float32 [6, 8, 131072], P(None, None, ('gx', 'gy', 'gz')), may hold values from -3 to 3
- plastic_onset_threshold: float32 [131072], P(('gx', 'gy', 'gz')), may hold values from 0.5 to 2
Outputs:
- temperature_new: float32 [3, 3, 3, 64, 32, 512], P(None, None, None, 'gx', 'gy', 'gz')
- stress_new: float32 [6, 8, 131072], P(None, None, ('gx', 'gy', 'gz'))
- forces: float32 [3, 8, 131072], P(None, None, ('gx', 'gy', 'gz'))
Inputs may be any that keep to these rules, and one draw needn't show every extreme that they name: `holding_brick_column`: the elements of one device hand at most 256 elements to one owner; in every draw some device hands exactly 256 to some owner. `piece_onto_solid_brick`: some mechanical cells may receive no element.
All inputs are finite; a program needn't handle non-finite values.
Results may differ from a plain program's by a relative error of at most 0.00022.
Values sent between devices are 32-bit elements; how exact they have to be, the bound alone decides.
No kernel may reach another device: no remote copies, remote signals or barrier semaphores. Data moves between devices by JAX's collectives and lax.ppermute only.
A program may use at most 64 MiB of HBM per device.

v0:
```python
import math

import jax
import jax.numpy as jnp
import numpy as np
from jax import lax
from jax.sharding import PartitionSpec as P

STEPS = 4


time_step = 0.003
penalty = 3.0
heat_power = 100.0
expansion = 0.02
shear_modulus = 100.0 / 2.6
lame_first = 30.0 / 0.52
hardening = 10.0
highest = lax.Precision.HIGHEST
nodal_weights = np.array([1.0 / 6.0, 2.0 / 3.0, 1.0 / 6.0], np.float32)


def padded(shard, sides, width):
    edges = {}
    for axis, dim in sides:
        size, length = (lax.axis_size(axis), shard.shape[dim])
        up = [(i, (i + 1) % size) for i in range(size - 1)]
        last = lax.slice_in_dim(shard, length - width, length, axis=dim)
        initial = lax.slice_in_dim(shard, 0, width, axis=dim)
        edges[dim] = (
            lax.ppermute(last, axis, up),
            lax.ppermute(initial, axis, [(b, a) for a, b in up]),
        )
    done = []
    for _, dim in sides:
        low, high = edges[dim]
        around = [(width, width) if d in done else (0, 0) for d in range(shard.ndim)]
        shard = jnp.concatenate([jnp.pad(low, around), shard, jnp.pad(high, around)], axis=dim)
        done.append(dim)
    return shard


def with_halo(cells, sides, width):
    for axis, dim in sides:
        count = lax.axis_size(axis)
        ends = count - 1
        head = lax.slice_in_dim(cells, 0, width, axis=dim)
        tail = lax.slice_in_dim(cells, cells.shape[dim] - width, cells.shape[dim], axis=dim)
        cells = jnp.concatenate(
            [
                lax.ppermute(tail, axis, [(i, (i + 1) % count) for i in range(ends)]),
                cells,
                lax.ppermute(head, axis, [((i + 1) % count, i) for i in range(ends)]),
            ],
            axis=dim,
        )
    return cells


def in_blocks(shard, dim, length):
    shape = shard.shape
    pieces = shard.reshape(*shape[:dim], length, shape[dim] // length, *shape[dim + 1 :])
    return jnp.moveaxis(pieces, dim, 0)


def sent_and_summed(shard, axis, dim):
    length = lax.axis_size(axis)
    pieces = lax.all_to_all(in_blocks(shard, dim, length), axis, 0, 0, tiled=True)
    return jnp.sum(pieces, axis=0)


def sent_together(arrays, axis, dim, along):
    columns = [a.reshape(*a.shape[:along], -1) for a in arrays]
    both = jnp.concatenate(columns, axis=along)
    out, at, done = (sent_and_summed(both, axis, dim), 0, [])
    for a, column in zip(arrays, columns):
        piece = out[..., at : at + column.shape[along]]
        done.append(piece.reshape(*piece.shape[:along], *a.shape[along:]))
        at += column.shape[along]
    return tuple(done)


def lumped_line():
    stiff = np.array([[7.0, -8.0, 1.0], [-8.0, 16.0, -8.0], [1.0, -8.0, 7.0]], np.float32) / 3.0
    return stiff / nodal_weights[:, None]


def gauss_spots():
    half = 0.5 / math.sqrt(3.0)
    return [0.5 - half, 0.5 + half]


def gauss_values():
    rows = []
    for point in gauss_spots():
        rows.append(
            [
                2.0 * (point - 0.5) * (point - 1.0),
                -4.0 * point * (point - 1.0),
                2.0 * point * (point - 0.5),
            ]
        )
    return np.array(rows, np.float32)


def gradient_table():
    spots = gauss_spots()
    table = np.zeros((3, 8, 8), np.float32)
    for node in range(8):
        corner = [node // 4, node // 2 % 2, node % 2]
        for point in range(8):
            place = [spots[point // 4], spots[point // 2 % 2], spots[point % 2]]
            values = [place[k] if corner[k] else 1.0 - place[k] for k in range(3)]
            slopes = [1.0 if corner[k] else -1.0 for k in range(3)]
            table[0, node, point] = slopes[0] * values[1] * values[2] / 8.0
            table[1, node, point] = values[0] * slopes[1] * values[2] / 8.0
            table[2, node, point] = values[0] * values[1] * slopes[2] / 8.0
    return table


def window(array, lead, axis, offset):
    index = [slice(None)] * lead
    for k in range(3):
        move = offset if k == axis else 0
        index.append(slice(1 + move, array.shape[lead + k] - 1 + move))
    return array[tuple(index)]


def node_terms(anchor, count, centre, near, far):
    places = (jnp.arange(count) + anchor).astype(jnp.float32)[None, :] + 0.5 * jnp.arange(3).astype(
        jnp.float32
    )[:, None]
    offset = places - centre
    radius = jnp.where(offset >= 0.0, near, far)
    return -3.0 * (offset / radius) ** 2


def volume_rate(core, kcore):
    line = jnp.asarray(lumped_line())
    rate = jnp.einsum("ai,ibcxyz->abcxyz", line, core, precision=highest)
    rate = rate + jnp.einsum("bi,aicxyz->abcxyz", line, core, precision=highest)
    rate = rate + jnp.einsum("ci,abixyz->abcxyz", line, core, precision=highest)
    return -kcore * rate


def heat_source(acore, shape, anchor, step_forward, extent):
    length, width, height = extent
    xterm = node_terms(
        anchor[0], shape[3], length * 0.5 + step_forward * length / 16.0, length / 8.0, length / 4.0
    )
    yterm = node_terms(anchor[1], shape[4], width * 0.5, width / 4.0, width / 4.0)
    zterm = node_terms(anchor[2], shape[5], height * 0.75, height / 8.0, height / 8.0)
    total = (
        xterm[:, None, None, :, None, None]
        + yterm[None, :, None, None, :, None]
        + zterm[None, None, :, None, None, :]
    )
    return heat_power * (2.0 / 3.0) * jnp.exp(total) * acore


def advance_solution(
    nodal_quantity_entries, diffusivity, mask, absorb_heat, anchor, step_forward, extent
):
    core = window(nodal_quantity_entries, 3, 0, 0)
    kcore = window(diffusivity, 0, 0, 0)
    mcore = window(mask, 0, 0, 0)
    acore = window(absorb_heat, 0, 0, 0)
    rate = volume_rate(core, kcore)
    for axis in range(3):
        for offset, own, other in ((1, 2, 0), (-1, 0, 2)):
            beside = window(nodal_quantity_entries, 3, axis, offset)
            kbeside = window(diffusivity, 0, axis, offset)
            mbeside = window(mask, 0, axis, offset)
            couple = (
                penalty
                * 2.0
                * kcore
                * kbeside
                / jnp.maximum(kcore + kbeside, 1.0)
                * mcore
                * mbeside
            )
            jump = jnp.take(core, own, axis=axis) - jnp.take(beside, other, axis=axis)
            flux = couple * jump / float(nodal_weights[own])
            rate = rate.at[(slice(None),) * axis + (own,)].add(-flux)
    source = heat_source(acore, core.shape, anchor, step_forward, extent)
    return core + time_step * mcore * (rate + source)


def gauss_point_change(change):
    table = jnp.asarray(gauss_values())
    value = jnp.einsum("pa,abcxyz->pbcxyz", table, change, precision=highest)
    value = jnp.einsum("qb,pbcxyz->pqcxyz", table, value, precision=highest)
    value = jnp.einsum("rc,pqcxyz->pqrxyz", table, value, precision=highest)
    return value


def mechanics(deformation_change, earlier_tension_state, plastic_onset_threshold, thermal):
    normal_component = deformation_change[0:3] - expansion * thermal[None]
    volume = normal_component[0] + normal_component[1] + normal_component[2]
    trial_normal = (
        earlier_tension_state[0:3]
        + lame_first * volume[None]
        + 2.0 * shear_modulus * normal_component
    )
    trial_shear = earlier_tension_state[3:6] + 2.0 * shear_modulus * deformation_change[3:6]
    pressure = (trial_normal[0] + trial_normal[1] + trial_normal[2]) / 3.0
    dev_normal = trial_normal - pressure[None]
    squares = jnp.sum(dev_normal * dev_normal, axis=0) + 2.0 * jnp.sum(
        trial_shear * trial_shear, axis=0
    )
    equivalent = jnp.sqrt(1.5 * squares)
    limit = plastic_onset_threshold[None, :]
    plastic = jnp.maximum(equivalent - limit, 0.0) / (3.0 * shear_modulus + hardening)
    factor = 1.0 - 3.0 * shear_modulus * plastic / jnp.maximum(equivalent, limit)
    new_normal = pressure[None] + factor[None] * dev_normal
    new_shear = factor[None] * trial_shear
    stress_new = jnp.concatenate([new_normal, new_shear], axis=0)
    rows = [[0, 5, 4], [5, 1, 3], [4, 3, 2]]
    tensor = jnp.stack([jnp.stack([stress_new[k] for k in row], axis=0) for row in rows], axis=0)
    forces = jnp.einsum("dig,cdgm->cim", jnp.asarray(gradient_table()), tensor, precision=highest)
    return (stress_new, forces)


def ghost(nodal_quantity_entries):
    return padded(nodal_quantity_entries, (("gx", 3), ("gy", 4), ("gz", 5)), 1)


def local(
    nodal_warmth_degrees,
    thermal_transfer_coefficient,
    taken_beam_fraction,
    laid_tiers,
    holding_brick_column,
    piece_onto_solid_brick,
    deformation_change,
    earlier_tension_state,
    plastic_onset_threshold,
):
    size_x, size_y, size_z = thermal_transfer_coefficient.shape
    extent = (
        size_x * lax.axis_size("gx"),
        size_y * lax.axis_size("gy"),
        size_z * lax.axis_size("gz"),
    )
    start_x = lax.axis_index("gx") * size_x
    start_y = lax.axis_index("gy") * size_y
    start_z = lax.axis_index("gz") * size_z
    mask = (jnp.arange(size_z)[None, None, :] < laid_tiers[0, 0, 0]).astype(jnp.float32)
    mask = jnp.broadcast_to(mask, thermal_transfer_coefficient.shape)
    depth = 1
    diffusivity, masked_values, absorb_heat = (
        with_halo(thermal_transfer_coefficient, (("gx", 0), ("gy", 1), ("gz", 2)), depth),
        with_halo(mask, (("gx", 0), ("gy", 1), ("gz", 2)), depth),
        with_halo(taken_beam_fraction, (("gx", 0), ("gy", 1), ("gz", 2)), depth),
    )
    nodal_quantity_entries = nodal_warmth_degrees
    for step_forward in range(STEPS):
        nodal_quantity_entries = advance_solution(
            ghost(nodal_quantity_entries),
            diffusivity,
            masked_values,
            absorb_heat,
            (start_x, start_y, start_z),
            step_forward,
            extent,
        )
    mesh_piece_sequence = size_x * size_y * size_z
    change_amount_entry = gauss_point_change(nodal_quantity_entries - nodal_warmth_degrees).reshape(
        8, mesh_piece_sequence
    )
    weights = mask.reshape(mesh_piece_sequence)
    target_owner = holding_brick_column.reshape(mesh_piece_sequence)
    target_cell = piece_onto_solid_brick.reshape(mesh_piece_sequence)
    owners = lax.axis_size("gx")
    cells = deformation_change.shape[2]
    local_sums = (
        jnp.zeros((owners, 8, cells), jnp.float32)
        .at[target_owner, :, target_cell]
        .add(change_amount_entry.T * weights[:, None])
    )
    local_counts = (
        jnp.zeros((owners, cells), jnp.float32).at[target_owner, target_cell].add(weights)
    )
    summed, counted = sent_together((local_sums, local_counts), "gx", 0, 1)
    sums = summed[0]
    counts = counted[0]
    thermal = sums / jnp.maximum(counts, 1.0)[None, :]
    stress_new, forces = mechanics(
        deformation_change, earlier_tension_state, plastic_onset_threshold, thermal
    )
    return (nodal_quantity_entries, stress_new, forces)


def solution(mesh):
    placed = (
        P(None, None, None, "gx", "gy", "gz"),
        P("gx", "gy", "gz"),
        P("gx", "gy", "gz"),
        P("gx", "gy", "gz"),
        P("gx", "gy", "gz", None, None),
        P("gx", "gy", "gz", None),
        P(None, None, ("gx", "gy", "gz")),
        P(None, None, ("gx", "gy", "gz")),
        P(("gx", "gy", "gz")),
    )
    return jax.shard_map(
        local,
        mesh=mesh,
        in_specs=placed,
        out_specs=(
            P(None, None, None, "gx", "gy", "gz"),
            P(None, None, ("gx", "gy", "gz")),
            P(None, None, ("gx", "gy", "gz")),
        ),
        check_vma=False,
    )
```

profile of v0, /device:TPU:14, one launch (start us, length us, event | category | flops | bytes accessed | tf_op | source)
XLA Modules:
  0.0 205.5 jit_solution(11309395098199805089)
XLA Ops:
  2.7 4.5 %collective-permute-start.4 = (f32[1,4,128]{2,1,0:T(4,128)S(1)}, f32[1,4,128]{2,1,0:T(4,128)S(1)}, u32[]{:S(2)}, u32[]{:S(2)}) collective-permute-start(f32[1,4,128]{2,1,0:T(4,128)S(1)} %slice.1240), channel_id=1, source_target_pairs={{0,32},{32,64},{64,96},{96,128},{128,160},{160,192},{192,224},{224... | collective-permute-start | bytes 6152 | tf_op jit(solution)/shard_map/ppermute | solution.py:51
  8.0 3.8 %collective-permute-start.3 = (f32[1,4,128]{2,1,0:T(4,128)S(1)}, f32[1,4,128]{2,1,0:T(4,128)S(1)}, u32[]{:S(2)}, u32[]{:S(2)}) collective-permute-start(f32[1,4,128]{2,1,0:T(4,128)S(1)} %get-tuple-element.433), channel_id=1, source_target_pairs={{0,32},{32,64},{64,96},{96,128},{128,160},{160,192},{192,224},{224... | collective-permute-start | bytes 6152 | tf_op jit(solution)/shard_map/ppermute | solution.py:51
  22.1 11.2 %scatter_custom_fusion.1 = f32[4096]{0:T(1024)S(1)} fusion(s32[2048]{0:T(1024)S(1)} %broadcast_select_fusion, f32[2048]{0:T(1024)S(1)} %bitcast.721, f32[]{:T(128)} %constant.696.clone.1), kind=kCustom, calls=%fused_computation.428 | custom fusion | flops 2048 | bytes 16388
  33.4 5.2 %collective-permute-start.5 = (f32[3,3,3,1,4,128]{5,4,3,2,1,0:T(4,128)S(1)}, f32[3,3,3,1,4,128]{5,4,3,2,1,0:T(4,128)S(1)}, u32[]{:S(2)}, u32[]{:S(2)}) collective-permute-start(f32[3,3,3,1,4,128]{5,4,3,2,1,0:T(4,128)S(1)} %get-tuple-element.400), channel_id=1, source_target_pairs={{0,32},{32,64},{64,96},{96,128},{128,160},{160,192},{192,224},{224... | collective-permute-start | bytes 165896 | tf_op jit(solution)/shard_map/ppermute | solution.py:31
  40.6 2.5 %collective-permute-start.6 = (f32[6,1,128]{2,1,0:T(1,128)S(1)}, f32[6,1,128]{2,1,0:T(1,128)S(1)}, u32[]{:S(2)}, u32[]{:S(2)}) collective-permute-start(f32[6,1,128]{2,1,0:T(1,128)S(1)} %get-tuple-element.421), channel_id=1, source_target_pairs={{4,0},{8,4},{12,8},{16,12},{20,16},{24,20},{28,24},{5,1},{9,5},{13... | collective-permute-start | bytes 9224 | tf_op jit(solution)/shard_map/ppermute | solution.py:53
  45.1 3.6 %collective-permute-start.10 = (f32[6,1,128]{2,1,0:T(1,128)S(1)}, f32[6,1,128]{2,1,0:T(1,128)S(1)}, u32[]{:S(2)}, u32[]{:S(2)}) collective-permute-start(f32[6,1,128]{2,1,0:T(1,128)S(1)} %get-tuple-element.422), channel_id=1, source_target_pairs={{0,4},{4,8},{8,12},{12,16},{16,20},{20,24},{24,28},{1,5},{5,9},{9,... | collective-permute-start | bytes 9224 | tf_op jit(solution)/shard_map/ppermute | solution.py:51
  53.4 3.0 %collective-permute-done.15 = f32[6,6,1]{2,1,0:T(8,128)S(1)} collective-permute-done((f32[6,6,1]{2,1,0:T(8,128)S(1)}, f32[6,6,1]{2,1,0:T(8,128)S(1)}, u32[]{:S(2)}, u32[]{:S(2)}) %collective-permute-start.15) | collective-permute-done | bytes 176 | tf_op jit(solution)/shard_map/ppermute | solution.py:51
  56.5 2.7 %collective-permute-start.12 = (f32[6,6,1]{2,1,0:T(8,128)S(1)}, f32[6,6,1]{2,1,0:T(8,128)S(1)}, u32[]{:S(2)}, u32[]{:S(2)}) collective-permute-start(f32[6,6,1]{2,1,0:T(8,128)S(1)} %get-tuple-element.415), channel_id=1, source_target_pairs={{1,0},{2,1},{3,2},{5,4},{6,5},{7,6},{9,8},{10,9},{11,10},{13,12},{... | collective-permute-start | bytes 440 | tf_op jit(solution)/shard_map/ppermute | solution.py:53
  59.2 3.8 %collective-permute-start.13 = (f32[6,6,1]{2,1,0:T(8,128)S(1)}, f32[6,6,1]{2,1,0:T(8,128)S(1)}, u32[]{:S(2)}, u32[]{:S(2)}) collective-permute-start(f32[6,6,1]{2,1,0:T(8,128)S(1)} %get-tuple-element.417), channel_id=1, source_target_pairs={{1,0},{2,1},{3,2},{5,4},{6,5},{7,6},{9,8},{10,9},{11,10},{13,12},{... | collective-permute-start | bytes 440 | tf_op jit(solution)/shard_map/ppermute | solution.py:53
  65.2 3.5 %collective-permute-start.14 = (f32[3,3,3,4,4,1]{5,4,3,0,1,2:T(4,128)S(1)}, f32[3,3,3,4,4,1]{5,4,3,0,1,2:T(4,128)S(1)}, u32[]{:S(2)}, u32[]{:S(2)}) collective-permute-start(f32[3,3,3,4,4,1]{5,4,3,0,1,2:T(4,128)S(1)} %get-tuple-element.395), channel_id=1, source_target_pairs={{1,0},{2,1},{3,2},{5,4},{6,5},{7,6},{9,8},{10,9},{11,10},{13,12},{... | collective-permute-start | bytes 5192 | tf_op jit(solution)/shard_map/ppermute | solution.py:32
  70.6 3.4 %collective-permute-done.14 = f32[3,3,3,4,4,1]{5,4,3,0,1,2:T(4,128)S(1)} collective-permute-done((f32[3,3,3,4,4,1]{5,4,3,0,1,2:T(4,128)S(1)}, f32[3,3,3,4,4,1]{5,4,3,0,1,2:T(4,128)S(1)}, u32[]{:S(2)}, u32[]{:S(2)}) %collective-permute-start.14) | collective-permute-done | bytes 1760 | tf_op jit(solution)/shard_map/ppermute | solution.py:32
  74.3 4.0 %collective-permute-done.17 = f32[3,3,3,4,4,1]{5,4,3,0,1,2:T(4,128)S(1)} collective-permute-done((f32[3,3,3,4,4,1]{5,4,3,0,1,2:T(4,128)S(1)}, f32[3,3,3,4,4,1]{5,4,3,0,1,2:T(4,128)S(1)}, u32[]{:S(2)}, u32[]{:S(2)}) %collective-permute-start.17) | collective-permute-done | bytes 1760 | tf_op jit(solution)/shard_map/ppermute | solution.py:31
  82.6 5.6 %collective-permute-start.19 = (f32[3,3,3,1,4,128]{5,4,3,2,1,0:T(4,128)S(1)}, f32[3,3,3,1,4,128]{5,4,3,2,1,0:T(4,128)S(1)}, u32[]{:S(2)}, u32[]{:S(2)}) collective-permute-start(f32[3,3,3,1,4,128]{5,4,3,2,1,0:T(4,128)S(1)} %get-tuple-element.392), channel_id=1, source_target_pairs={{0,32},{32,64},{64,96},{96,128},{128,160},{160,192},{192,224},{224... | collective-permute-start | bytes 165896 | tf_op jit(solution)/shard_map/ppermute | solution.py:31
  92.5 2.7 %collective-permute-start.22 = (f32[3,3,3,4,4,1]{5,4,3,0,1,2:T(4,128)S(1)}, f32[3,3,3,4,4,1]{5,4,3,0,1,2:T(4,128)S(1)}, u32[]{:S(2)}, u32[]{:S(2)}) collective-permute-start(f32[3,3,3,4,4,1]{5,4,3,0,1,2:T(4,128)S(1)} %get-tuple-element.389), channel_id=1, source_target_pairs={{1,0},{2,1},{3,2},{5,4},{6,5},{7,6},{9,8},{10,9},{11,10},{13,12},{... | collective-permute-start | bytes 5192 | tf_op jit(solution)/shard_map/ppermute | solution.py:32
  97.3 3.5 %collective-permute-done.22 = f32[3,3,3,4,4,1]{5,4,3,0,1,2:T(4,128)S(1)} collective-permute-done((f32[3,3,3,4,4,1]{5,4,3,0,1,2:T(4,128)S(1)}, f32[3,3,3,4,4,1]{5,4,3,0,1,2:T(4,128)S(1)}, u32[]{:S(2)}, u32[]{:S(2)}) %collective-permute-start.22) | collective-permute-done | bytes 1760 | tf_op jit(solution)/shard_map/ppermute | solution.py:32
  101.0 4.4 %collective-permute-done.23 = f32[3,3,3,4,4,1]{5,4,3,0,1,2:T(4,128)S(1)} collective-permute-done((f32[3,3,3,4,4,1]{5,4,3,0,1,2:T(4,128)S(1)}, f32[3,3,3,4,4,1]{5,4,3,0,1,2:T(4,128)S(1)}, u32[]{:S(2)}, u32[]{:S(2)}) %collective-permute-start.23) | collective-permute-done | bytes 1760 | tf_op jit(solution)/shard_map/ppermute | solution.py:31
  108.2 3.9 %collective-permute-start.25 = (f32[3,3,3,1,4,128]{5,4,3,2,1,0:T(4,128)S(1)}, f32[3,3,3,1,4,128]{5,4,3,2,1,0:T(4,128)S(1)}, u32[]{:S(2)}, u32[]{:S(2)}) collective-permute-start(f32[3,3,3,1,4,128]{5,4,3,2,1,0:T(4,128)S(1)} %get-tuple-element.386), channel_id=1, source_target_pairs={{0,32},{32,64},{64,96},{96,128},{128,160},{160,192},{192,224},{224... | collective-permute-start | bytes 165896 | tf_op jit(solution)/shard_map/ppermute | solution.py:31
  121.5 3.4 %collective-permute-done.28 = f32[3,3,3,4,4,1]{5,4,3,0,1,2:T(4,128)S(1)} collective-permute-done((f32[3,3,3,4,4,1]{5,4,3,0,1,2:T(4,128)S(1)}, f32[3,3,3,4,4,1]{5,4,3,0,1,2:T(4,128)S(1)}, u32[]{:S(2)}, u32[]{:S(2)}) %collective-permute-start.28) | collective-permute-done | bytes 1760 | tf_op jit(solution)/shard_map/ppermute | solution.py:32
  125.2 4.6 %collective-permute-done.29 = f32[3,3,3,4,4,1]{5,4,3,0,1,2:T(4,128)S(1)} collective-permute-done((f32[3,3,3,4,4,1]{5,4,3,0,1,2:T(4,128)S(1)}, f32[3,3,3,4,4,1]{5,4,3,0,1,2:T(4,128)S(1)}, u32[]{:S(2)}, u32[]{:S(2)}) %collective-permute-start.29) | collective-permute-done | bytes 1760 | tf_op jit(solution)/shard_map/ppermute | solution.py:31
  133.7 6.4 %collective-permute-start.31 = (f32[3,3,3,1,4,128]{5,4,3,2,1,0:T(4,128)S(1)}, f32[3,3,3,1,4,128]{5,4,3,2,1,0:T(4,128)S(1)}, u32[]{:S(2)}, u32[]{:S(2)}) collective-permute-start(f32[3,3,3,1,4,128]{5,4,3,2,1,0:T(4,128)S(1)} %get-tuple-element.380), channel_id=1, source_target_pairs={{0,32},{32,64},{64,96},{96,128},{128,160},{160,192},{192,224},{224... | collective-permute-start | bytes 165896 | tf_op jit(solution)/shard_map/ppermute | solution.py:31
  148.4 2.9 %collective-permute-done.34 = f32[3,3,3,4,4,1]{5,4,3,0,2,1:T(4,128)S(1)} collective-permute-done((f32[3,3,3,4,4,1]{5,4,3,0,2,1:T(4,128)S(1)}, f32[3,3,3,4,4,1]{5,4,3,0,2,1:T(4,128)S(1)}, u32[]{:S(2)}, u32[]{:S(2)}) %collective-permute-start.34) | collective-permute-done | bytes 1760 | tf_op jit(solution)/shard_map/ppermute | solution.py:32
  151.5 4.5 %collective-permute-done.35 = f32[3,3,3,4,4,1]{5,4,3,2,1,0:T(4,128)S(1)} collective-permute-done((f32[3,3,3,4,4,1]{5,4,3,2,1,0:T(4,128)S(1)}, f32[3,3,3,4,4,1]{5,4,3,2,1,0:T(4,128)S(1)}, u32[]{:S(2)}, u32[]{:S(2)}) %collective-permute-start.35) | collective-permute-done | bytes 1760 | tf_op jit(solution)/shard_map/ppermute | solution.py:31
  159.2 12.0 %scatter_custom_fusion = f32[4096,8]{1,0:T(8,128)S(1)} fusion(s32[2048]{0:T(1024)S(1)} %broadcast_select_fusion, f32[2048,8]{1,0:T(8,128)S(1)} %copy.488, f32[]{:T(128)} %constant.696.clone.1), kind=kCustom, calls=%fused_computation.5 | custom fusion | flops 16384 | bytes 131076
  172.0 31.7 %all_to_all.5 = f32[16,1,2304]{2,1,0:T(1,128)S(1)} all-to-all(f32[16,1,2304]{2,1,0:T(1,128)S(1)} %copy.490), channel_id=1, replica_groups=mesh['gx'=16,'gy'=8,'gz'=4] {'gx'}, dimensions={0} | all-to-all | bytes 294912 | tf_op jit(solution)/shard_map/all_to_all | solution.py:68
  (217 shorter events, 66.0 us)
Async XLA Ops:
  1.4 37.2 %collective-permute-start.1 = (f32[1,4,128]{2,1,0:T(4,128)S(1)}, f32[1,4,128]{2,1,0:T(4,128)S(1)}, u32[]{:S(2)}, u32[]{:S(2)}) collective-permute-start(f32[1,4,128]{2,1,0:T(4,128)S(1)} %slice.1240), channel_id=1, source_target_pairs={{32,0},{64,32},{96,64},{128,96},{160,128},{192,160},{224,192},{256... | collective-permute-start | bytes 6152 | tf_op jit(solution)/shard_map/ppermute | solution.py:53
  2.7 37.8 %collective-permute-start.4 = (f32[1,4,128]{2,1,0:T(4,128)S(1)}, f32[1,4,128]{2,1,0:T(4,128)S(1)}, u32[]{:S(2)}, u32[]{:S(2)}) collective-permute-start(f32[1,4,128]{2,1,0:T(4,128)S(1)} %slice.1240), channel_id=1, source_target_pairs={{0,32},{32,64},{64,96},{96,128},{128,160},{160,192},{192,224},{224... | collective-permute-start | bytes 6152 | tf_op jit(solution)/shard_map/ppermute | solution.py:51
  8.0 25.4 %collective-permute-start.3 = (f32[1,4,128]{2,1,0:T(4,128)S(1)}, f32[1,4,128]{2,1,0:T(4,128)S(1)}, u32[]{:S(2)}, u32[]{:S(2)}) collective-permute-start(f32[1,4,128]{2,1,0:T(4,128)S(1)} %get-tuple-element.433), channel_id=1, source_target_pairs={{0,32},{32,64},{64,96},{96,128},{128,160},{160,192},{192,224},{224... | collective-permute-start | bytes 6152 | tf_op jit(solution)/shard_map/ppermute | solution.py:51
  11.8 28.7 %collective-permute-start = (f32[1,4,128]{2,1,0:T(4,128)S(1)}, f32[1,4,128]{2,1,0:T(4,128)S(1)}, u32[]{:S(2)}, u32[]{:S(2)}) collective-permute-start(f32[1,4,128]{2,1,0:T(4,128)S(1)} %get-tuple-element.434), channel_id=1, source_target_pairs={{32,0},{64,32},{96,64},{128,96},{160,128},{192,160},{224,192},{256... | collective-permute-start | bytes 6152 | tf_op jit(solution)/shard_map/ppermute | solution.py:53
  14.0 54.9 %collective-permute-start.2 = (f32[3,3,3,1,4,128]{5,4,3,2,1,0:T(4,128)S(1)}, f32[3,3,3,1,4,128]{5,4,3,2,1,0:T(4,128)S(1)}, u32[]{:S(2)}, u32[]{:S(2)}) collective-permute-start(f32[3,3,3,1,4,128]{5,4,3,2,1,0:T(4,128)S(1)} %get-tuple-element.401), channel_id=1, source_target_pairs={{32,0},{64,32},{96,64},{128,96},{160,128},{192,160},{224,192},{256... | collective-permute-start | bytes 165896 | tf_op jit(solution)/shard_map/ppermute | solution.py:32
  33.4 36.9 %collective-permute-start.5 = (f32[3,3,3,1,4,128]{5,4,3,2,1,0:T(4,128)S(1)}, f32[3,3,3,1,4,128]{5,4,3,2,1,0:T(4,128)S(1)}, u32[]{:S(2)}, u32[]{:S(2)}) collective-permute-start(f32[3,3,3,1,4,128]{5,4,3,2,1,0:T(4,128)S(1)} %get-tuple-element.400), channel_id=1, source_target_pairs={{0,32},{32,64},{64,96},{96,128},{128,160},{160,192},{192,224},{224... | collective-permute-start | bytes 165896 | tf_op jit(solution)/shard_map/ppermute | solution.py:31
  38.6 31.6 %collective-permute-start.8 = (f32[3,3,3,4,1,128]{5,4,3,0,1,2:T(1,128)S(1)}, f32[3,3,3,4,1,128]{5,4,3,0,1,2:T(1,128)S(1)}, u32[]{:S(2)}, u32[]{:S(2)}) collective-permute-start(f32[3,3,3,4,1,128]{5,4,3,0,1,2:T(1,128)S(1)} %get-tuple-element.399), channel_id=1, source_target_pairs={{4,0},{8,4},{12,8},{16,12},{20,16},{24,20},{28,24},{5,1},{9,5},{13... | collective-permute-start | bytes 165896 | tf_op jit(solution)/shard_map/ppermute | solution.py:32
  65.2 8.8 %collective-permute-start.14 = (f32[3,3,3,4,4,1]{5,4,3,0,1,2:T(4,128)S(1)}, f32[3,3,3,4,4,1]{5,4,3,0,1,2:T(4,128)S(1)}, u32[]{:S(2)}, u32[]{:S(2)}) collective-permute-start(f32[3,3,3,4,4,1]{5,4,3,0,1,2:T(4,128)S(1)} %get-tuple-element.395), channel_id=1, source_target_pairs={{1,0},{2,1},{3,2},{5,4},{6,5},{7,6},{9,8},{10,9},{11,10},{13,12},{... | collective-permute-start | bytes 5192 | tf_op jit(solution)/shard_map/ppermute | solution.py:32
  68.8 9.4 %collective-permute-start.17 = (f32[3,3,3,4,4,1]{5,4,3,0,1,2:T(4,128)S(1)}, f32[3,3,3,4,4,1]{5,4,3,0,1,2:T(4,128)S(1)}, u32[]{:S(2)}, u32[]{:S(2)}) collective-permute-start(f32[3,3,3,4,4,1]{5,4,3,0,1,2:T(4,128)S(1)} %get-tuple-element.394), channel_id=1, source_target_pairs={{0,1},{1,2},{2,3},{4,5},{5,6},{6,7},{8,9},{9,10},{10,11},{12,13},{... | collective-permute-start | bytes 5192 | tf_op jit(solution)/shard_map/ppermute | solution.py:31
  81.3 14.1 %collective-permute-start.18 = (f32[3,3,3,1,4,128]{5,4,3,2,1,0:T(4,128)S(1)}, f32[3,3,3,1,4,128]{5,4,3,2,1,0:T(4,128)S(1)}, u32[]{:S(2)}, u32[]{:S(2)}) collective-permute-start(f32[3,3,3,1,4,128]{5,4,3,2,1,0:T(4,128)S(1)} %get-tuple-element.393), channel_id=1, source_target_pairs={{32,0},{64,32},{96,64},{128,96},{160,128},{192,160},{224,192},{256... | collective-permute-start | bytes 165896 | tf_op jit(solution)/shard_map/ppermute | solution.py:32
  82.6 14.4 %collective-permute-start.19 = (f32[3,3,3,1,4,128]{5,4,3,2,1,0:T(4,128)S(1)}, f32[3,3,3,1,4,128]{5,4,3,2,1,0:T(4,128)S(1)}, u32[]{:S(2)}, u32[]{:S(2)}) collective-permute-start(f32[3,3,3,1,4,128]{5,4,3,2,1,0:T(4,128)S(1)} %get-tuple-element.392), channel_id=1, source_target_pairs={{0,32},{32,64},{64,96},{96,128},{128,160},{160,192},{192,224},{224... | collective-permute-start | bytes 165896 | tf_op jit(solution)/shard_map/ppermute | solution.py:31
  88.1 8.8 %collective-permute-start.20 = (f32[3,3,3,4,1,128]{5,4,3,0,1,2:T(1,128)S(1)}, f32[3,3,3,4,1,128]{5,4,3,0,1,2:T(1,128)S(1)}, u32[]{:S(2)}, u32[]{:S(2)}) collective-permute-start(f32[3,3,3,4,1,128]{5,4,3,0,1,2:T(1,128)S(1)} %get-tuple-element.391), channel_id=1, source_target_pairs={{4,0},{8,4},{12,8},{16,12},{20,16},{24,20},{28,24},{5,1},{9,5},{13... | collective-permute-start | bytes 165896 | tf_op jit(solution)/shard_map/ppermute | solution.py:32
  90.1 7.1 %collective-permute-start.21 = (f32[3,3,3,4,1,128]{5,4,3,0,1,2:T(1,128)S(1)}, f32[3,3,3,4,1,128]{5,4,3,0,1,2:T(1,128)S(1)}, u32[]{:S(2)}, u32[]{:S(2)}) collective-permute-start(f32[3,3,3,4,1,128]{5,4,3,0,1,2:T(1,128)S(1)} %get-tuple-element.390), channel_id=1, source_target_pairs={{0,4},{4,8},{8,12},{12,16},{16,20},{20,24},{24,28},{1,5},{5,9},{9,... | collective-permute-start | bytes 165896 | tf_op jit(solution)/shard_map/ppermute | solution.py:31
  92.5 8.3 %collective-permute-start.22 = (f32[3,3,3,4,4,1]{5,4,3,0,1,2:T(4,128)S(1)}, f32[3,3,3,4,4,1]{5,4,3,0,1,2:T(4,128)S(1)}, u32[]{:S(2)}, u32[]{:S(2)}) collective-permute-start(f32[3,3,3,4,4,1]{5,4,3,0,1,2:T(4,128)S(1)} %get-tuple-element.389), channel_id=1, source_target_pairs={{1,0},{2,1},{3,2},{5,4},{6,5},{7,6},{9,8},{10,9},{11,10},{13,12},{... | collective-permute-start | bytes 5192 | tf_op jit(solution)/shard_map/ppermute | solution.py:32
  95.3 10.1 %collective-permute-start.23 = (f32[3,3,3,4,4,1]{5,4,3,0,1,2:T(4,128)S(1)}, f32[3,3,3,4,4,1]{5,4,3,0,1,2:T(4,128)S(1)}, u32[]{:S(2)}, u32[]{:S(2)}) collective-permute-start(f32[3,3,3,4,4,1]{5,4,3,0,1,2:T(4,128)S(1)} %get-tuple-element.388), channel_id=1, source_target_pairs={{0,1},{1,2},{2,3},{4,5},{5,6},{6,7},{8,9},{9,10},{10,11},{12,13},{... | collective-permute-start | bytes 5192 | tf_op jit(solution)/shard_map/ppermute | solution.py:31
  108.2 11.5 %collective-permute-start.25 = (f32[3,3,3,1,4,128]{5,4,3,2,1,0:T(4,128)S(1)}, f32[3,3,3,1,4,128]{5,4,3,2,1,0:T(4,128)S(1)}, u32[]{:S(2)}, u32[]{:S(2)}) collective-permute-start(f32[3,3,3,1,4,128]{5,4,3,2,1,0:T(4,128)S(1)} %get-tuple-element.386), channel_id=1, source_target_pairs={{0,32},{32,64},{64,96},{96,128},{128,160},{160,192},{192,224},{224... | collective-permute-start | bytes 165896 | tf_op jit(solution)/shard_map/ppermute | solution.py:31
  112.1 8.9 %collective-permute-start.24 = (f32[3,3,3,1,4,128]{5,4,3,2,1,0:T(4,128)S(1)}, f32[3,3,3,1,4,128]{5,4,3,2,1,0:T(4,128)S(1)}, u32[]{:S(2)}, u32[]{:S(2)}) collective-permute-start(f32[3,3,3,1,4,128]{5,4,3,2,1,0:T(4,128)S(1)} %get-tuple-element.387), channel_id=1, source_target_pairs={{32,0},{64,32},{96,64},{128,96},{160,128},{192,160},{224,192},{256... | collective-permute-start | bytes 165896 | tf_op jit(solution)/shard_map/ppermute | solution.py:32
  113.4 7.7 %collective-permute-start.26 = (f32[3,3,3,4,1,128]{5,4,3,0,1,2:T(1,128)S(1)}, f32[3,3,3,4,1,128]{5,4,3,0,1,2:T(1,128)S(1)}, u32[]{:S(2)}, u32[]{:S(2)}) collective-permute-start(f32[3,3,3,4,1,128]{5,4,3,0,1,2:T(1,128)S(1)} %get-tuple-element.385), channel_id=1, source_target_pairs={{4,0},{8,4},{12,8},{16,12},{20,16},{24,20},{28,24},{5,1},{9,5},{13... | collective-permute-start | bytes 165896 | tf_op jit(solution)/shard_map/ppermute | solution.py:32
  117.7 7.2 %collective-permute-start.28 = (f32[3,3,3,4,4,1]{5,4,3,0,1,2:T(4,128)S(1)}, f32[3,3,3,4,4,1]{5,4,3,0,1,2:T(4,128)S(1)}, u32[]{:S(2)}, u32[]{:S(2)}) collective-permute-start(f32[3,3,3,4,4,1]{5,4,3,0,1,2:T(4,128)S(1)} %get-tuple-element.383), channel_id=1, source_target_pairs={{1,0},{2,1},{3,2},{5,4},{6,5},{7,6},{9,8},{10,9},{11,10},{13,12},{... | collective-permute-start | bytes 5192 | tf_op jit(solution)/shard_map/ppermute | solution.py:32
  119.6 10.1 %collective-permute-start.29 = (f32[3,3,3,4,4,1]{5,4,3,0,1,2:T(4,128)S(1)}, f32[3,3,3,4,4,1]{5,4,3,0,1,2:T(4,128)S(1)}, u32[]{:S(2)}, u32[]{:S(2)}) collective-permute-start(f32[3,3,3,4,4,1]{5,4,3,0,1,2:T(4,128)S(1)} %get-tuple-element.382), channel_id=1, source_target_pairs={{0,1},{1,2},{2,3},{4,5},{5,6},{6,7},{8,9},{9,10},{10,11},{12,13},{... | collective-permute-start | bytes 5192 | tf_op jit(solution)/shard_map/ppermute | solution.py:31
  132.4 13.9 %collective-permute-start.30 = (f32[3,3,3,1,4,128]{5,4,3,2,1,0:T(4,128)S(1)}, f32[3,3,3,1,4,128]{5,4,3,2,1,0:T(4,128)S(1)}, u32[]{:S(2)}, u32[]{:S(2)}) collective-permute-start(f32[3,3,3,1,4,128]{5,4,3,2,1,0:T(4,128)S(1)} %get-tuple-element.381), channel_id=1, source_target_pairs={{32,0},{64,32},{96,64},{128,96},{160,128},{192,160},{224,192},{256... | collective-permute-start | bytes 165896 | tf_op jit(solution)/shard_map/ppermute | solution.py:32
  133.7 14.2 %collective-permute-start.31 = (f32[3,3,3,1,4,128]{5,4,3,2,1,0:T(4,128)S(1)}, f32[3,3,3,1,4,128]{5,4,3,2,1,0:T(4,128)S(1)}, u32[]{:S(2)}, u32[]{:S(2)}) collective-permute-start(f32[3,3,3,1,4,128]{5,4,3,2,1,0:T(4,128)S(1)} %get-tuple-element.380), channel_id=1, source_target_pairs={{0,32},{32,64},{64,96},{96,128},{128,160},{160,192},{192,224},{224... | collective-permute-start | bytes 165896 | tf_op jit(solution)/shard_map/ppermute | solution.py:31
  140.1 7.8 %collective-permute-start.32 = (f32[3,3,3,4,1,128]{5,4,3,2,0,1:T(1,128)S(1)}, f32[3,3,3,4,1,128]{5,4,3,2,0,1:T(1,128)S(1)}, u32[]{:S(2)}, u32[]{:S(2)}) collective-permute-start(f32[3,3,3,4,1,128]{5,4,3,2,0,1:T(1,128)S(1)} %copy.504), channel_id=1, source_target_pairs={{4,0},{8,4},{12,8},{16,12},{20,16},{24,20},{28,24},{5,1},{9,5},{13... | collective-permute-start | bytes 165896 | tf_op jit(solution)/shard_map/ppermute | solution.py:32
  146.3 9.8 %collective-permute-start.35 = (f32[3,3,3,4,4,1]{5,4,3,2,1,0:T(4,128)S(1)}, f32[3,3,3,4,4,1]{5,4,3,2,1,0:T(4,128)S(1)}, u32[]{:S(2)}, u32[]{:S(2)}) collective-permute-start(f32[3,3,3,4,4,1]{5,4,3,2,1,0:T(4,128)S(1)} %get-tuple-element.374), channel_id=1, source_target_pairs={{0,1},{1,2},{2,3},{4,5},{5,6},{6,7},{8,9},{9,10},{10,11},{12,13},{... | collective-permute-start | bytes 5192 | tf_op jit(solution)/shard_map/ppermute | solution.py:31
  (25 other events, 384.6 us)
where the time goes:
time: 207 us; the launch traced here: 206 us
  starting transfers between devices  88.2 us (43%)
  waiting for transfers between devices  33.7 us (16%)
  blocking collectives  31.7 us (15%)
  other arithmetic  30.1 us (15%)
  matrix products  13.2 us (6%)
  local copies, waits for them, and re-layouts  5.84 us (3%)
  between operations  2.79 us (1%)
    ppermute x12, starting transfers between devices, padded(): lax.ppermute(last, axis, up)  35.8 us
    all_to_all x1, blocking collectives, sent_and_summed(): lax.all_to_all(in_blocks(shard, dim, length), axis, 0, 0, tiled=True)  31.7 us
    unnamed x5, other arithmetic  23.4 us
    ppermute x12, starting transfers between devices, padded(): lax.ppermute(initial, axis, [(b, a) for a, b in up])  22.5 us
    ppermute x12, waiting for transfers between devices, padded(): lax.ppermute(last, axis, up)  17.5 us
    ppermute x6, starting transfers between devices, with_halo(): lax.ppermute(tail, axis, [(i, (i + 1) % count) for i in range(ends)])  16.4 us
    ppermute x6, starting transfers between devices, with_halo(): lax.ppermute(head, axis, [((i + 1) % count, i) for i in range(ends)])  13.5 us
    ppermute x12, waiting for transfers between devices, padded(): lax.ppermute(initial, axis, [(b, a) for a, b in up])  13.1 us
  transfers between devices with their start and end apart: 36, of which 9 were waited for; matrix products, arithmetic and copies ran while one was open for 11% of the time, Pallas kernels for 0%

commit v1 on v0

v1 whole, which is shorter than its diff:
```python
import functools
import math

import jax
import jax.numpy as jnp
import numpy as np
from jax import lax
from jax.experimental import pallas as pl
from jax.experimental.pallas import tpu as pltpu
from jax.sharding import PartitionSpec as P

STEPS = 4
DT = 0.003
PENALTY = 3.0
HEAT = 100.0 * (2.0 / 3.0)
EXPANSION = 0.02
MU = 100.0 / 2.6
LAME = 30.0 / 0.52
HARD = 10.0
NX, NY, NZ = 64, 32, 512
PX, PY, PZ = 4, 4, 128
OWNERS, CELLS = 16, 256
F32 = jnp.float32

LAM = (0.0, 12.0, 24.0)
XROWS = 480
YROWS = 928
CORNERS = [(side, xd, d) for side in (0, 1) for xd in (1, 2, 3) for d in range(1, 5 - xd)]


def mode(i, j, l):
    return 9 * i + 3 * j + l


def call(kernel, outs, args, scratch=(), smem=(), near=()):
    args = [
        pltpu.with_memory_space_constraint(a, pltpu.VMEM) if n in near else a
        for n, a in enumerate(args)
    ]
    specs = [
        pl.BlockSpec(memory_space=pltpu.SMEM if n in smem else pltpu.VMEM) for n in range(len(args))
    ]
    return pl.pallas_call(
        kernel,
        out_shape=outs,
        in_specs=specs,
        out_specs=jax.tree.map(lambda _: pl.BlockSpec(memory_space=pltpu.VMEM), outs),
        scratch_shapes=list(scratch),
    )(*args)


def lane_iota(rows):
    return lax.broadcasted_iota(jnp.int32, (rows, 128), 1)


def row_iota(rows):
    return lax.broadcasted_iota(jnp.int32, (rows, 128), 0)


def modal(a, b, c):
    s = a + c
    return (s + 4.0 * b) * (1.0 / 6.0), (c - a) * 0.5, (s - 2.0 * b) * (1.0 / 3.0)


def modal_grid(values):
    for stride in (9, 3, 1):
        out = [None] * 27
        for base in range(27):
            if base // stride % 3 == 0:
                ids = [base + stride * t for t in range(3)]
                for q, r in zip(ids, modal(*[values[q] for q in ids])):
                    out[q] = r
        values = out
    return values


def nodal_grid(values):
    for stride in (9, 3, 1):
        out = [None] * 27
        for base in range(27):
            if base // stride % 3 == 0:
                al, be, ga = (values[base + stride * t] for t in range(3))
                e = al + ga
                out[base], out[base + stride], out[base + 2 * stride] = e - be, al - 0.5 * ga, e + be
        values = out
    return values


def prep_kernel(t_ref, k_ref, a_ref, lay_ref, cols_ref, zpay_ref):
    layers = lay_ref[0]
    m = (lane_iota(8) < layers).astype(F32)
    lane = lane_iota(32)
    for h in range(2):
        rows = slice(8 * h, 8 * h + 8)
        modes = modal_grid([t_ref[n, rows, :] for n in range(27)])
        modes.append(k_ref[rows, :] * m)
        modes.append(a_ref[rows, :] * m * (DT * HEAT))
        for n, v in enumerate(modes):
            cols_ref[pl.ds(8 * h * 32 + n, 8, stride=32), :] = v
    zero = jnp.zeros((3, 128), F32)
    acc = jnp.zeros((32, 128), F32)
    for c in range(16):
        cols_ref[c * 32 + 29 : c * 32 + 32, :] = zero
    for c in range(16):
        x, y = c // 4, c % 4
        start = y * 32 + x * 8
        v = pltpu.roll(cols_ref[c * 32 : c * 32 + 32, :], (4 + start) % 128, axis=1)
        acc = jnp.where((lane >= start) & (lane < start + 8), v, acc)
    zpay_ref[...] = acc


def by_parity(axis, write, first, second):
    even = lax.axis_index(axis) % 2 == 0

    @pl.when(even)
    def _():
        write(first, second)

    @pl.when(jnp.logical_not(even))
    def _():
        write(second, first)


def face_rows(cols_ref, c, axis, sign):
    base = c * 32
    if axis == 0:
        parts = [cols_ref[base + 9 * i : base + 9 * i + 9, :] for i in range(3)]
        return [parts[0] + parts[2] + sign * parts[1]]
    out = []
    for i in range(3):
        parts = [cols_ref[base + 9 * i + 3 * j : base + 9 * i + 3 * j + 3, :] for j in range(3)]
        out.append(parts[0] + parts[2] + sign * parts[1])
    return out


def put_faces(dst, at, cols_ref, c, axis, sign):
    row = at
    for part in face_rows(cols_ref, c, axis, sign):
        dst[row : row + part.shape[0], :] = part
        row += part.shape[0]
    dst[row : row + 1, :] = cols_ref[c * 32 + 27 : c * 32 + 28, :]
    dst[row + 1 : at + 16, :] = jnp.zeros((at + 15 - row, 128), F32)


def xpay_kernel(cols_ref, za_ref, zb_ref, first_ref, second_ref, h_ref):
    even = lax.axis_index("gz") % 2 == 0
    idx = lane_iota(32) % 8
    za, zb = za_ref[...], zb_ref[...]
    upper = jnp.where(even, za, zb)
    lower = jnp.where(even, zb, za)
    own = jnp.where(idx < 4, lower, upper)
    h_ref[...] = own

    def write(upper_ref, lower_ref):
        for d in range(1, 4):
            for y in range(4):
                at = ((d - 1) * 4 + y) * 32
                upper_ref[at : at + 32, :] = cols_ref[((4 - d) * 4 + y) * 32 : ((4 - d) * 4 + y) * 32 + 32, :]
                lower_ref[at : at + 32, :] = cols_ref[((d - 1) * 4 + y) * 32 : ((d - 1) * 4 + y) * 32 + 32, :]
        for y in range(4):
            put_faces(upper_ref, 384 + 16 * y, cols_ref, y, 0, 1.0)
            put_faces(lower_ref, 384 + 16 * y, cols_ref, 12 + y, 0, -1.0)
        upper_ref[448:480, :] = own
        lower_ref[448:480, :] = own

    by_parity("gx", write, first_ref, second_ref)


def ypay_kernel(cols_ref, xa_ref, xb_ref, h_ref, first_ref, second_ref):
    even = lax.axis_index("gx") % 2 == 0

    def halo(side, at, rows):
        a, b = xa_ref[at : at + rows, :], xb_ref[at : at + rows, :]
        return jnp.where(even, b, a) if side == 0 else jnp.where(even, a, b)

    def write(upper_ref, lower_ref):
        for x in range(4):
            for d in range(1, 4):
                at = ((d - 1) * 4 + x) * 32
                upper_ref[at : at + 32, :] = cols_ref[(x * 4 + 4 - d) * 32 : (x * 4 + 4 - d) * 32 + 32, :]
                lower_ref[at : at + 32, :] = cols_ref[(x * 4 + d - 1) * 32 : (x * 4 + d - 1) * 32 + 32, :]
            put_faces(upper_ref, 384 + 16 * x, cols_ref, x * 4, 1, 1.0)
            put_faces(lower_ref, 384 + 16 * x, cols_ref, x * 4 + 3, 1, -1.0)
        for n, (side, xd, d) in enumerate(CORNERS):
            at = 448 + 32 * n
            upper_ref[at : at + 32, :] = halo(side, ((xd - 1) * 4 + 4 - d) * 32, 32)
            lower_ref[at : at + 32, :] = halo(side, ((xd - 1) * 4 + d - 1) * 32, 32)
        for n, block in enumerate((halo(0, 448, 32), h_ref[...], halo(1, 448, 32))):
            upper_ref[832 + 32 * n : 864 + 32 * n, :] = block
            lower_ref[832 + 32 * n : 864 + 32 * n, :] = block

    by_parity("gy", write, first_ref, second_ref)


def couple(k1, k2):
    return (2.0 * PENALTY * DT) * k1 * k2 / jnp.maximum(k1 + k2, 1.0)


def roll_lanes(v, shift):
    return pltpu.roll(v, shift, axis=1)


def wide(v, n):
    return v if n == 8 else jnp.concatenate([v, v], axis=0)


def shift_rows(v, up):
    n = v.shape[0]
    amount, edge = (7, 7) if up else (1, 0)
    if n == 8:
        return pltpu.roll(v, amount, axis=0)
    a, b = pltpu.roll(v[0:8], amount, axis=0), pltpu.roll(v[8:16], amount, axis=0)
    take = row_iota(8) == edge
    return jnp.concatenate([jnp.where(take, b, a), jnp.where(take, a, b)], axis=0)


def line_faces(values, stride):
    out = []
    for base in range(27):
        if base // stride % 3 == 0:
            e = values[base] + values[base + 2 * stride]
            out.append((e - values[base + stride], e + values[base + stride]))
    return out


def slot(y):
    return (y + 2) % 16


def advance(values, kappa, heats, yz, fluxes):
    factor = {}
    for total in sorted({LAM[i] + LAM[j] + LAM[l] for i in range(3) for j in range(3) for l in range(3)}):
        factor[total] = 1.0 - kappa * total if total else None
    terms = []
    for lines in fluxes:
        per = []
        for low, high in lines:
            gain, both = low - high, low + high
            per.append((gain, -3.0 * both, 2.0 * gain))
        terms.append(per)
    out = []
    for i in range(3):
        for j in range(3):
            for l in range(3):
                v = values[mode(i, j, l)]
                f = factor[LAM[i] + LAM[j] + LAM[l]]
                v = v if f is None else v * f
                v = v + heats[i] * yz[3 * j + l]
                v = v + (terms[0][3 * j + l][i] + terms[1][3 * i + l][j]) + terms[2][3 * i + j][l]
                out.append(v)
    return out


def gauss_exp(offset, near, far):
    scaled = offset * jnp.where(offset >= 0.0, 1.0 / near, 1.0 / far)
    return jnp.exp(-3.0 * (scaled * scaled))


def main_kernel(
    cols_ref, h_ref, xa_ref, xb_ref, ya_ref, yb_ref, own_ref, cell_ref, lay_ref,
    t_out, pay_out,
    m0, m1, h0, h1, cx, cy, czu, czd, ch, yz, yzh, gs, q_ref, old, inc, amat, bmat, csum,
):
    gx, gy, gz = lax.axis_index("gx"), lax.axis_index("gy"), lax.axis_index("gz")
    even_x, even_y = gx % 2 == 0, gy % 2 == 0
    lane8 = lane_iota(8)
    idx8 = lane8 % 8

    zeros8 = jnp.zeros((8, 128), F32)

    def clear(n, _):
        m0[pl.ds(pl.multiple_of(n * 64, 64), 64), :] = jnp.zeros((64, 128), F32)
        return 0

    lax.fori_loop(0, 96, clear, 0)

    def place(x, y, block):
        m0[pl.ds((x + 4) * 512 + slot(y), 32, stride=16), :] = block

    def xhalo(side, at, rows):
        a, b = xa_ref[at : at + rows, :], xb_ref[at : at + rows, :]
        return jnp.where(even_x, b, a) if side == 0 else jnp.where(even_x, a, b)

    def yhalo(side, at, rows):
        a, b = ya_ref[at : at + rows, :], yb_ref[at : at + rows, :]
        return jnp.where(even_y, b, a) if side == 0 else jnp.where(even_y, a, b)

    for c in range(16):
        place(c // 4, c % 4, cols_ref[c * 32 : c * 32 + 32, :])
    for side in (0, 1):
        for d in range(1, 4):
            x = -d if side == 0 else 3 + d
            for y in range(4):
                place(x, y, xhalo(side, ((d - 1) * 4 + y) * 32, 32))
        x = -4 if side == 0 else 7
        for y in range(4):
            block = xhalo(side, 384 + 16 * y, 16)
            at = (x + 4) * 512 + slot(y)
            m0[pl.ds(at, 8, stride=16), :] = block[0:8]
            m0[pl.ds(at + 8 * 16, 1), :] = block[8:9]
            m0[pl.ds(at + 27 * 16, 1), :] = block[9:10]
    for side in (0, 1):
        for x in range(4):
            for d in range(1, 4):
                place(x, -d if side == 0 else 3 + d, yhalo(side, ((d - 1) * 4 + x) * 32, 32))
            block = yhalo(side, 384 + 16 * x, 16)
            at = (x + 4) * 512 + slot(-4 if side == 0 else 7)
            for i in range(3):
                for l in range(3):
                    m0[pl.ds(at + mode(i, 0, l) * 16, 1), :] = block[3 * i + l : 3 * i + l + 1]
            m0[pl.ds(at + 27 * 16, 1), :] = block[9:10]
        for n, (xside, xd, d) in enumerate(CORNERS):
            x = -xd if xside == 0 else 3 + xd
            place(x, -d if side == 0 else 3 + d, yhalo(side, 448 + 32 * n, 32))

    def clear_h(n, _):
        h0[pl.ds(pl.multiple_of(n * 64, 64), 64), :] = jnp.zeros((64, 128), F32)
        return 0

    lax.fori_loop(0, 8, clear_h, 0)
    lane32 = lane_iota(32)
    for yb in range(3):
        if yb == 1:
            blocks = [xhalo(0, 448, 32), h_ref[...], xhalo(1, 448, 32)]
        else:
            blocks = [yhalo(yb // 2, 832 + 32 * n, 32) for n in range(3)]
        for y in range(4):
            rolled = [roll_lanes(b, (32 * n - 32 * y) % 128) if (n - y) % 4 else b for n, b in enumerate(blocks)]
            v = jnp.where(lane32 < 32, rolled[0], jnp.where(lane32 < 64, rolled[1], rolled[2]))
            v = jnp.where(lane32 < 96, v, 0.0)
            h0[pl.ds(slot(4 * yb - 4 + y), 32, stride=16), :] = v

    lane16 = lane_iota(16)
    idx16 = lane16 % 8
    kh = h0[27 * 16 : 28 * 16, :]
    gk_src = jnp.where(idx16 == 5, roll_lanes(kh, 2), kh)
    ch[0:16, :] = couple(kh, roll_lanes(kh, 120))
    ch[16:32, :] = couple(kh, shift_rows(kh, True))
    ch[32:48, :] = jnp.where((idx16 == 3) | (idx16 == 7), 0.0, couple(kh, roll_lanes(kh, 127)))

    def kof(xi):
        return m0[pl.ds(pl.multiple_of(xi * 512 + 27 * 16, 16), 16), :]

    def couplings(xi, k):
        at = pl.multiple_of(xi * 16, 16)
        knext = kof(jnp.minimum(xi + 1, 11))
        gk = roll_lanes(gk_src, 123 - xi * 8)
        cx[pl.ds(at, 16), :] = couple(k, knext)
        cy[pl.ds(at, 16), :] = couple(k, shift_rows(k, True))
        czu[pl.ds(at, 16), :] = couple(k, jnp.where(lane16 == 127, gk, roll_lanes(k, 127)))
        czd[pl.ds(at, 16), :] = couple(k, gk)
        return knext

    lax.fori_loop(0, 11, couplings, kof(0))

    def line_modes(base, centre, near, far):
        return modal(*[gauss_exp(base + 0.5 * n - centre, near, far) for n in range(3)])

    s16 = row_iota(16)
    ypos = (gy * PY + jnp.where(s16 < 12, s16 - 2, s16 - 18)).astype(F32)
    ymodes = line_modes(ypos, NY * 0.5, NY / 4.0, NY / 4.0)
    zpos = (gz * PZ + lane16).astype(F32)
    zmodes = line_modes(zpos, NZ * 0.75, NZ / 8.0, NZ / 8.0)
    zhpos = (gz * PZ + jnp.where(idx16 < 4, idx16 - 4, idx16 + 124)).astype(F32)
    zhmodes = line_modes(zhpos, NZ * 0.75, NZ / 8.0, NZ / 8.0)
    for j in range(3):
        for l in range(3):
            at = (3 * j + l) * 16
            yz[at : at + 16, :] = ymodes[j] * zmodes[l]
            yzh[at : at + 16, :] = ymodes[j] * zhmodes[l]

    def rows_of(ref, xi, n):
        return [ref[pl.ds(pl.multiple_of(xi * 512 + 16 * m, 8), n), :] for m in range(27)]

    def at_x(ref, xi, n):
        return ref[pl.ds(pl.multiple_of(xi * 16, 8), n), :]

    def table(ref, n):
        return [ref[16 * t : 16 * t + n, :] for t in range(9)]

    s8 = row_iota(8)

    def pair(ref, p, m):
        a = ref[pl.ds((4 + 2 * p) * 512 + 16 * m, 8), :]
        b = ref[pl.ds((5 + 2 * p) * 512 + 16 * m, 8), :]
        return jnp.where(s8 < 4, pltpu.roll(a, 6, axis=0), pltpu.roll(b, 2, axis=0))

    low_modes = [mode(i, j, l) for i in range(2) for j in range(2) for l in range(2)]
    for g, m in enumerate(low_modes):
        for p in range(2):
            old[16 * g + 8 * p : 16 * g + 8 * p + 8, :] = pair(m0, p, m)

    groups = [
        [(1, 3, 8), (3, 9, 16), (9, 11, 8)],
        [(2, 4, 8), (4, 8, 16), (8, 10, 8)],
        [(3, 9, 8)],
        [(4, 8, 8)],
    ]
    src, dst, hsrc, hdst = m0, m1, h0, h1
    for step in range(STEPS):
        last = step == STEPS - 1
        centre_x = NX * 0.5 + step * NX / 16.0
        hn = 16 if step < 2 else 8
        hv = [hsrc[16 * m : 16 * m + hn, :] for m in range(27)]
        lane_h = lane_iota(hn)
        idx_h = lane_h % 8
        hz = line_faces(hv, 1)
        for t, (low, high) in enumerate(hz):
            gs[16 * t : 16 * t + hn, :] = jnp.where(idx_h == 5, roll_lanes(high, 2), low)
        if not last:
            for t in range(9):
                q_ref[8 * t : 8 * t + 8, :] = zeros8

        for first, end, n in groups[step]:
            lane_n = lane_iota(n)

            def xflux(here, there, xi, n=n):
                c = at_x(cx, xi, n)
                return tuple(c * (a[1] - b[0]) for a, b in zip(line_faces(here, 9), line_faces(there, 9)))

            def body(xi, carry, n=n, src=src, dst=dst, step=step, last=last, lane_n=lane_n, centre_x=centre_x):
                left = carry
                values = rows_of(src, xi, n)
                following = rows_of(src, xi + 1, n)
                right = xflux(values, following, xi, n)
                kappa = DT * src_k(xi, n)
                heat = src_a(xi, n)
                base = (gx * PX + xi - 4).astype(F32) - centre_x
                splat = jnp.full((8, 128), base, F32)
                xm = modal(*[gauss_exp(splat + 0.5 * t, NX / 8.0, NX / 4.0) for t in range(3)])
                heats = [heat * wide(v, n) for v in xm]
                c = at_x(cy, xi, n)
                yf = []
                for low, high in line_faces(values, 3):
                    up = c * (high - shift_rows(low, True))
                    yf.append((shift_rows(up, False), up))
                cu, cd = at_x(czu, xi, n), at_x(czd, xi, n)
                zf = []
                shift = 123 - xi * 8
                mine = (lane8 == xi * 8 + 4) | (lane8 == xi * 8 + 5)
                for t, (low, high) in enumerate(line_faces(values, 1)):
                    g = roll_lanes(gs[16 * t : 16 * t + n, :], shift)
                    up = cu * (high - jnp.where(lane_n == 127, g, roll_lanes(low, 127)))
                    down = jnp.where(lane_n == 0, cd * (g - low), roll_lanes(up, 1))
                    zf.append((down, up))
                    if not last:
                        back = roll_lanes(jnp.where(lane8 == 127, up[0:8], down[0:8]), xi * 8 + 5)
                        q_ref[8 * t : 8 * t + 8, :] = jnp.where(mine, back, q_ref[8 * t : 8 * t + 8, :])
                out = advance(values, kappa, heats, table(yz, n), (list(zip(left, right)), yf, zf))
                for m, v in enumerate(out):
                    dst[pl.ds(pl.multiple_of(xi * 512 + 16 * m, 8), n), :] = v
                return right

            def src_k(xi, n):
                return m0[pl.ds(pl.multiple_of(xi * 512 + 27 * 16, 8), n), :]

            def src_a(xi, n):
                return m0[pl.ds(pl.multiple_of(xi * 512 + 28 * 16, 8), n), :]

            left = xflux(rows_of(src, first - 1, n), rows_of(src, first, n), first - 1, n)
            lax.fori_loop(first, end, body, left)

        if not last:
            n = 16 if step == 0 else 8
            hv = [v[0:n] for v in hv]
            idx_n = lane_iota(n) % 8
            xpos = (gx * PX + lane_iota(8) // 8 - 4).astype(F32) - centre_x
            xm = modal(*[gauss_exp(xpos + 0.5 * t, NX / 8.0, NX / 4.0) for t in range(3)])
            heat = h0[28 * 16 : 28 * 16 + n, :]
            heats = [heat * wide(v, n) for v in xm]
            c = ch[0:n, :]
            xf = []
            for low, high in line_faces(hv, 9):
                up = c * (high - roll_lanes(low, 120))
                xf.append((roll_lanes(up, 8), up))
            c = ch[16 : 16 + n, :]
            yf = []
            for low, high in line_faces(hv, 3):
                up = c * (high - shift_rows(low, True))
                yf.append((shift_rows(up, False), up))
            c = ch[32 : 32 + n, :]
            zf = []
            for t, (low, high) in enumerate(line_faces(hv, 1)):
                up = c * (high - roll_lanes(low, 127))
                q = wide(q_ref[8 * t : 8 * t + 8, :], n)
                down = jnp.where(idx_n == 4, q, roll_lanes(up, 1))
                zf.append((down, jnp.where(idx_n == 3, roll_lanes(q, 126), up)))
            kappa = DT * h0[27 * 16 : 27 * 16 + n, :]
            out = advance(hv, kappa, heats, table(yzh, n), (xf, yf, zf))
            for m, v in enumerate(out):
                hdst[16 * m : 16 * m + n, :] = v
        src, dst, hsrc, hdst = dst, src, hdst, hsrc

    live = (lane8 < lay_ref[0]).astype(F32)
    for p in range(2):
        modes = [pair(src, p, m) for m in range(27)]
        for g, m in enumerate(low_modes):
            at = 16 * g + 8 * p
            inc[at : at + 8, :] = (modes[m] - old[at : at + 8, :]) * live
        for n, v in enumerate(nodal_grid(modes)):
            t_out[n, 8 * p : 8 * p + 8, :] = v

    ones = row_iota(16)
    for c in range(16):
        lanes = slice(128 * c, 128 * c + 128)
        v = inc[pl.ds(c, 8, stride=16), :]
        hi = v.astype(jnp.bfloat16).astype(F32)
        lo = v - hi
        owner = jnp.broadcast_to(own_ref[c : c + 1, :], (8, 128))
        picks = [owner == o for o in range(OWNERS)]
        amat[0:128, lanes] = jnp.concatenate([jnp.where(k, hi, 0.0) for k in picks], axis=0).astype(jnp.bfloat16)
        amat[128:256, lanes] = jnp.concatenate([jnp.where(k, lo, 0.0) for k in picks], axis=0).astype(jnp.bfloat16)
        owner16 = jnp.broadcast_to(own_ref[c : c + 1, :], (16, 128))
        amat[256:272, lanes] = jnp.where(owner16 == ones, wide(live, 16), 0.0).astype(jnp.bfloat16)
        cell = jnp.broadcast_to(cell_ref[c : c + 1, :], (CELLS, 128))
        hit = cell == row_iota(CELLS)
        bmat[:, lanes] = jnp.where(hit, 1.0, 0.0).astype(jnp.bfloat16)
    total = lax.dot_general(
        amat[...], bmat[...], (((1,), (1,)), ((), ())), preferred_element_type=F32
    )
    csum[0:128, :] = (total[0:128] + total[128:256])[:, 0:128]
    csum[128:256, :] = (total[0:128] + total[128:256])[:, 128:256]
    for h in range(2):
        for g in range(8):
            pay_out[pl.ds(2 * g + h, 16, stride=18), :] = csum[pl.ds(128 * h + g, 16, stride=8), :]
        pay_out[pl.ds(16 + h, 16, stride=18), :] = total[256:272, 128 * h : 128 * h + 128]


def gradient_table():
    spots = [0.5 - 0.5 / math.sqrt(3.0), 0.5 + 0.5 / math.sqrt(3.0)]
    out = np.zeros((3, 8, 8), np.float32)
    for node in range(8):
        corner = [node // 4, node // 2 % 2, node % 2]
        for point in range(8):
            place = [spots[point // 4], spots[point // 2 % 2], spots[point % 2]]
            values = [place[k] if corner[k] else 1.0 - place[k] for k in range(3)]
            slopes = [1.0 if corner[k] else -1.0 for k in range(3)]
            out[0, node, point] = slopes[0] * values[1] * values[2] / 8.0
            out[1, node, point] = values[0] * slopes[1] * values[2] / 8.0
            out[2, node, point] = values[0] * values[1] * slopes[2] / 8.0
    return out


def column(values):
    rows = row_iota(8)
    out = jnp.full((8, 128), float(values[7]), F32)
    for r in range(7):
        out = jnp.where(rows == r, float(values[r]), out)
    return out


def mechanics_kernel(got_ref, de_ref, st_ref, lim_ref, stress_out, force_out):
    sums = got_ref[0:18, :]
    for s in range(1, OWNERS):
        sums = sums + got_ref[18 * s : 18 * s + 18, :]
    root = 1.0 / math.sqrt(3.0)
    rows = row_iota(8)
    signs = [jnp.where(rows // w % 2 == 0, -root, root) for w in (4, 2, 1)]
    table = gradient_table()
    cols = [[column(table[d, :, g]) for g in range(8)] for d in range(3)]
    for h in range(2):
        lanes = slice(128 * h, 128 * h + 128)
        inv = 1.0 / jnp.maximum(sums[16 + h : 17 + h], 1.0)

        def row(m):
            return jnp.broadcast_to(sums[2 * m + h : 2 * m + h + 1] * inv, (8, 128))

        z = [row(2 * n) + signs[2] * row(2 * n + 1) for n in range(4)]
        y = [z[2 * n] + signs[1] * z[2 * n + 1] for n in range(2)]
        strain = EXPANSION * (y[0] + signs[0] * y[1])
        normal = [de_ref[k, :, lanes] - strain for k in range(3)]
        volume = normal[0] + normal[1] + normal[2]
        trial = [st_ref[k, :, lanes] + LAME * volume + 2.0 * MU * normal[k] for k in range(3)]
        shear = [st_ref[k, :, lanes] + 2.0 * MU * de_ref[k, :, lanes] for k in range(3, 6)]
        pressure = (trial[0] + trial[1] + trial[2]) * (1.0 / 3.0)
        dev = [t - pressure for t in trial]
        squares = dev[0] * dev[0] + dev[1] * dev[1] + dev[2] * dev[2]
        squares = squares + 2.0 * (shear[0] * shear[0] + shear[1] * shear[1] + shear[2] * shear[2])
        equivalent = jnp.sqrt(1.5 * squares)
        limit = jnp.broadcast_to(lim_ref[0:1, lanes], (8, 128))
        plastic = jnp.maximum(equivalent - limit, 0.0) * (1.0 / (3.0 * MU + HARD))
        factor = 1.0 - (3.0 * MU) * plastic / jnp.maximum(equivalent, limit)
        stress = [pressure + factor * d for d in dev] + [factor * s for s in shear]
        for k in range(6):
            stress_out[k, :, lanes] = stress[k]
        index = [[0, 5, 4], [5, 1, 3], [4, 3, 2]]
        forces = [jnp.zeros((8, 128), F32)] * 3
        for g in range(8):
            at = [jnp.broadcast_to(s[g : g + 1], (8, 128)) for s in stress]
            for c in range(3):
                for d in range(3):
                    forces[c] = forces[c] + cols[d][g] * at[index[c][d]]
        for c in range(3):
            force_out[c, :, lanes] = forces[c]


def swap(first, second, axis, count):
    even = [(i, i ^ 1) for i in range(count)]
    odd = [(i, i + 1 if i % 2 else i - 1) for i in range(1, count - 1)]
    return lax.ppermute(first, axis, even), lax.ppermute(second, axis, odd)


def local(temps, cond, absorb, layers, owner, cell, de, st, lim):
    rows = lambda n: pltpu.VMEM((n, 128), F32)
    sx, sy, sz = (lax.axis_size(a) for a in ("gx", "gy", "gz"))
    temps = temps.reshape(27, 16, 128)
    layers = layers.reshape(1)
    cols, zpay = call(
        prep_kernel,
        (rows(512), rows(32)),
        (temps, cond.reshape(16, 128), absorb.reshape(16, 128), layers),
        smem=(3,),
    )
    za, zb = swap(zpay, zpay, "gz", sz)
    xf, xs, hown = call(xpay_kernel, (rows(XROWS), rows(XROWS), rows(32)), (cols, za, zb), near=(0, 1, 2))
    xa, xb = swap(xf, xs, "gx", sx)
    yf, ys = call(ypay_kernel, (rows(YROWS), rows(YROWS)), (cols, xa, xb, hown), near=(0, 1, 2, 3))
    ya, yb = swap(yf, ys, "gy", sy)
    vm = lambda n: pltpu.VMEM((n, 128), F32)
    t_new, pay = call(
        main_kernel,
        (jax.ShapeDtypeStruct((27, 16, 128), F32), rows(OWNERS * 18)),
        (cols, hown, xa, xb, ya, yb, owner.reshape(16, 128), cell.reshape(16, 128), layers),
        scratch=[
            vm(6144), vm(6144), vm(512), vm(512),
            vm(192), vm(192), vm(192), vm(192), vm(48), vm(144), vm(144), vm(144), vm(72), vm(128), vm(128),
            pltpu.VMEM((272, 2048), jnp.bfloat16), pltpu.VMEM((256, 2048), jnp.bfloat16), vm(256),
        ],
        smem=(8,),
        near=(0, 1, 2, 3, 4, 5),
    )
    got = lax.all_to_all(pay.reshape(OWNERS, 1, 2304), "gx", 0, 0, tiled=True)
    stress, forces = call(
        mechanics_kernel,
        (jax.ShapeDtypeStruct((6, 8, 256), F32), jax.ShapeDtypeStruct((3, 8, 256), F32)),
        (got.reshape(OWNERS * 18, 128), de, st, lim.reshape(1, 256)),
        near=(0,),
    )
    return t_new.reshape(3, 3, 3, 4, 4, 128), stress, forces


def solution(mesh):
    cells = P(None, None, ("gx", "gy", "gz"))
    temps = P(None, None, None, "gx", "gy", "gz")
    block = P("gx", "gy", "gz")
    return jax.shard_map(
        local,
        mesh=mesh,
        in_specs=(
            temps, block, block, block, P("gx", "gy", "gz", None, None), P("gx", "gy", "gz", None),
            cells, cells, P(("gx", "gy", "gz")),
        ),
        out_specs=(temps, cells, cells),
        check_vma=False,
    )
```

time: 207 us -> 78.7 us (0.38)
  the two profiles are of different devices: /device:TPU:14 before, /device:TPU:42 now
where the time goes in v1:
time: 78.7 us; the launch traced here: 78.3 us
  blocking collectives  30.1 us (38%)
  starting transfers between devices  17.4 us (22%)
  waiting for transfers between devices  15.4 us (20%)
  Pallas kernels  14 us (18%)
  between operations  1.36 us (2%)
    all_to_all x1, blocking collectives, local(): got = lax.all_to_all(pay.reshape(OWNERS, 1, 2304), 'gx', 0, 0, tiled=True)  30.1 us
    ppermute x6, starting transfers between devices, swap(): return (lax.ppermute(first, axis, even), lax.ppermute(second, axis, odd))  17.4 us
    ppermute x6, waiting for transfers between devices, swap(): return (lax.ppermute(first, axis, even), lax.ppermute(second, axis, odd))  15.4 us
    pallas_call x5, Pallas kernels, call(): pl.pallas_call(kernel, out_shape=outs, in_specs=specs, out_specs=jax.tree...  14 us
  transfers between devices with their start and end apart: 6, of which 5 were waited for; matrix products, arithmetic and copies ran while one was open for 0% of the time, Pallas kernels for 0%

profile of v1, /device:TPU:42, one launch (start us, length us, event | category | flops | bytes accessed | tf_op | source)
XLA Modules:
  0.0 78.3 jit_solution(9020979625397792323)
XLA Ops:
  1.3 1.3 %shard_map.112 = (f32[512,128]{1,0:T(8,128)S(1)}, f32[32,128]{1,0:T(8,128)S(1)}) custom-call(f32[27,16,128]{2,1,0:T(8,128)} %bitcast.14, f32[16,128]{1,0:T(8,128)} %bitcast.17, f32[16,128]{1,0:T(8,128)} %bitcast.18, s32[1]{0:T(128)} %bitcast.10.lay_ref), custom_call_target="tpu_custom_call" | custom-call | tf_op jit(solution)/shard_map/pallas_call | solution.py:43
  2.5 3.4 %collective-permute-start.1 = (f32[32,128]{1,0:T(8,128)S(1)}, f32[32,128]{1,0:T(8,128)S(1)}, u32[]{:S(2)}, u32[]{:S(2)}) collective-permute-start(f32[32,128]{1,0:T(8,128)S(1)} %get-tuple-element.15), channel_id=1, source_target_pairs={{1,2},{2,1},{5,6},{6,5},{9,10},{10,9},{13,14},{14,13},{17,18},{18,... | collective-permute-start | bytes 49160 | tf_op jit(solution)/shard_map/ppermute | solution.py:600
  5.9 1.9 %collective-permute-start = (f32[32,128]{1,0:T(8,128)S(1)}, f32[32,128]{1,0:T(8,128)S(1)}, u32[]{:S(2)}, u32[]{:S(2)}) collective-permute-start(f32[32,128]{1,0:T(8,128)S(1)} %get-tuple-element.15), channel_id=1, source_target_pairs={{0,1},{1,0},{2,3},{3,2},{4,5},{5,4},{6,7},{7,6},{8,9},{9,8},{10,11... | collective-permute-start | bytes 49160 | tf_op jit(solution)/shard_map/ppermute | solution.py:600
  7.9 0.3 collective-permute-done.1.zb_ref
  8.2 3.4 %collective-permute-done.za_ref = f32[32,128]{1,0:T(8,128)S(1)} collective-permute-done((f32[32,128]{1,0:T(8,128)S(1)}, f32[32,128]{1,0:T(8,128)S(1)}, u32[]{:S(2)}, u32[]{:S(2)}) %collective-permute-start) | collective-permute-done | bytes 16416 | tf_op jit(solution)/shard_map/ppermute | solution.py:600
  11.6 2.0 %collective-permute-start.2 = (f32[480,128]{1,0:T(8,128)S(1)}, f32[480,128]{1,0:T(8,128)S(1)}, u32[]{:S(2)}, u32[]{:S(2)}) collective-permute-start(f32[480,128]{1,0:T(8,128)S(1)} %get-tuple-element.17), channel_id=1, source_target_pairs={{0,32},{32,0},{64,96},{96,64},{128,160},{160,128},{192,224},{224,1... | collective-permute-start | bytes 737288 | tf_op jit(solution)/shard_map/ppermute | solution.py:600
  13.7 5.6 %collective-permute-start.3 = (f32[480,128]{1,0:T(8,128)S(1)}, f32[480,128]{1,0:T(8,128)S(1)}, u32[]{:S(2)}, u32[]{:S(2)}) collective-permute-start(f32[480,128]{1,0:T(8,128)S(1)} %get-tuple-element.18), channel_id=1, source_target_pairs={{32,64},{64,32},{96,128},{128,96},{160,192},{192,160},{224,256},{2... | collective-permute-start | bytes 737288 | tf_op jit(solution)/shard_map/ppermute | solution.py:600
  19.3 0.5 collective-permute-done.2.xa_ref
  19.8 3.7 %collective-permute-done.3.xb_ref = f32[480,128]{1,0:T(8,128)S(1)} collective-permute-done((f32[480,128]{1,0:T(8,128)S(1)}, f32[480,128]{1,0:T(8,128)S(1)}, u32[]{:S(2)}, u32[]{:S(2)}) %collective-permute-start.3) | collective-permute-done | bytes 245792 | tf_op jit(solution)/shard_map/ppermute | solution.py:600
  23.5 0.1 shard_map.114
  23.6 1.9 %collective-permute-start.4 = (f32[928,128]{1,0:T(8,128)S(1)}, f32[928,128]{1,0:T(8,128)S(1)}, u32[]{:S(2)}, u32[]{:S(2)}) collective-permute-start(f32[928,128]{1,0:T(8,128)S(1)} %get-tuple-element.19), channel_id=1, source_target_pairs={{0,4},{4,0},{8,12},{12,8},{16,20},{20,16},{24,28},{28,24},{1,5},{5... | collective-permute-start | bytes 1425416 | tf_op jit(solution)/shard_map/ppermute | solution.py:600
  25.5 2.5 %collective-permute-start.5 = (f32[928,128]{1,0:T(8,128)S(1)}, f32[928,128]{1,0:T(8,128)S(1)}, u32[]{:S(2)}, u32[]{:S(2)}) collective-permute-start(f32[928,128]{1,0:T(8,128)S(1)} %get-tuple-element.20), channel_id=1, source_target_pairs={{4,8},{8,4},{12,16},{16,12},{20,24},{24,20},{5,9},{9,5},{13,17},{1... | collective-permute-start | bytes 1425416 | tf_op jit(solution)/shard_map/ppermute | solution.py:600
  28.0 0.0 collective-permute-done.4.ya_ref
  28.0 7.5 %collective-permute-done.5.yb_ref = f32[928,128]{1,0:T(8,128)S(1)} collective-permute-done((f32[928,128]{1,0:T(8,128)S(1)}, f32[928,128]{1,0:T(8,128)S(1)}, u32[]{:S(2)}, u32[]{:S(2)}) %collective-permute-start.5) | collective-permute-done | bytes 475168 | tf_op jit(solution)/shard_map/ppermute | solution.py:600
  35.5 11.1 %shard_map.115 = (f32[27,16,128]{2,1,0:T(8,128)}, f32[288,128]{1,0:T(8,128)S(1)}) custom-call(f32[512,128]{1,0:T(8,128)S(1)} %get-tuple-element.14.cols_ref, f32[32,128]{1,0:T(8,128)S(1)} %get-tuple-element.16.h_ref, f32[480,128]{1,0:T(8,128)S(1)} %collective-permute-done.2.xa_ref, f32[480,128]{1,0:T(8,128)S(1)} %collective-permute-done.3.xb_ref, ...), custom_call_target="tpu_custom_call" | custom-call | tf_op jit(solution)/shard_map/pallas_call | solution.py:43
  46.6 30.1 %all_to_all.5 = f32[16,1,2304]{2,1,0:T(1,128)S(1)} all-to-all(f32[16,1,2304]{2,1,0:T(1,128)S(1)} %bitcast.13), channel_id=1, replica_groups=mesh['gx'=16,'gy'=8,'gz'=4] {'gx'}, dimensions={0} | all-to-all | bytes 294912 | tf_op jit(solution)/shard_map/all_to_all | solution.py:632
  76.7 1.6 %shard_map.116 = (f32[6,8,256]{2,1,0:T(8,128)}, f32[3,8,256]{2,1,0:T(8,128)}) custom-call(f32[288,128]{1,0:T(8,128)S(1)} %bitcast.12, f32[6,8,256]{2,1,0:T(8,128)} %de_ref.1, f32[6,8,256]{2,1,0:T(8,128)} %st_ref.1, f32[1,256]{1,0:T(1,128)} %bitcast.19), custom_call_target="tpu_custom_call" | custom-call | tf_op jit(solution)/shard_map/pallas_call | solution.py:43
  (1 shorter events, 0.0 us)
Async XLA Ops:
  2.5 5.6 %collective-permute-start.1 = (f32[32,128]{1,0:T(8,128)S(1)}, f32[32,128]{1,0:T(8,128)S(1)}, u32[]{:S(2)}, u32[]{:S(2)}) collective-permute-start(f32[32,128]{1,0:T(8,128)S(1)} %get-tuple-element.15), channel_id=1, source_target_pairs={{1,2},{2,1},{5,6},{6,5},{9,10},{10,9},{13,14},{14,13},{17,18},{18,... | collective-permute-start | bytes 49160 | tf_op jit(solution)/shard_map/ppermute | solution.py:600
  5.9 5.6 %collective-permute-start = (f32[32,128]{1,0:T(8,128)S(1)}, f32[32,128]{1,0:T(8,128)S(1)}, u32[]{:S(2)}, u32[]{:S(2)}) collective-permute-start(f32[32,128]{1,0:T(8,128)S(1)} %get-tuple-element.15), channel_id=1, source_target_pairs={{0,1},{1,0},{2,3},{3,2},{4,5},{5,4},{6,7},{7,6},{8,9},{9,8},{10,11... | collective-permute-start | bytes 49160 | tf_op jit(solution)/shard_map/ppermute | solution.py:600
  11.6 8.2 %collective-permute-start.2 = (f32[480,128]{1,0:T(8,128)S(1)}, f32[480,128]{1,0:T(8,128)S(1)}, u32[]{:S(2)}, u32[]{:S(2)}) collective-permute-start(f32[480,128]{1,0:T(8,128)S(1)} %get-tuple-element.17), channel_id=1, source_target_pairs={{0,32},{32,0},{64,96},{96,64},{128,160},{160,128},{192,224},{224,1... | collective-permute-start | bytes 737288 | tf_op jit(solution)/shard_map/ppermute | solution.py:600
  13.7 9.9 %collective-permute-start.3 = (f32[480,128]{1,0:T(8,128)S(1)}, f32[480,128]{1,0:T(8,128)S(1)}, u32[]{:S(2)}, u32[]{:S(2)}) collective-permute-start(f32[480,128]{1,0:T(8,128)S(1)} %get-tuple-element.18), channel_id=1, source_target_pairs={{32,64},{64,32},{96,128},{128,96},{160,192},{192,160},{224,256},{2... | collective-permute-start | bytes 737288 | tf_op jit(solution)/shard_map/ppermute | solution.py:600
  23.6 4.4 %collective-permute-start.4 = (f32[928,128]{1,0:T(8,128)S(1)}, f32[928,128]{1,0:T(8,128)S(1)}, u32[]{:S(2)}, u32[]{:S(2)}) collective-permute-start(f32[928,128]{1,0:T(8,128)S(1)} %get-tuple-element.19), channel_id=1, source_target_pairs={{0,4},{4,0},{8,12},{12,8},{16,20},{20,16},{24,28},{28,24},{1,5},{5... | collective-permute-start | bytes 1425416 | tf_op jit(solution)/shard_map/ppermute | solution.py:600
  25.5 10.0 %collective-permute-start.5 = (f32[928,128]{1,0:T(8,128)S(1)}, f32[928,128]{1,0:T(8,128)S(1)}, u32[]{:S(2)}, u32[]{:S(2)}) collective-permute-start(f32[928,128]{1,0:T(8,128)S(1)} %get-tuple-element.20), channel_id=1, source_target_pairs={{4,8},{8,4},{12,16},{16,12},{20,24},{24,20},{5,9},{9,5},{13,17},{1... | collective-permute-start | bytes 1425416 | tf_op jit(solution)/shard_map/ppermute | solution.py:600

commit v2 on v1

--- a/solution.py
+++ b/solution.py
@@ -8,6 +8,7 @@
 from jax.experimental import pallas as pl
 from jax.experimental.pallas import tpu as pltpu
 from jax.sharding import PartitionSpec as P
+
 
 STEPS = 4
 DT = 0.003
@@ -23,30 +24,50 @@
 F32 = jnp.float32
 
 LAM = (0.0, 12.0, 24.0)
-XROWS = 480
-YROWS = 928
-CORNERS = [(side, xd, d) for side in (0, 1) for xd in (1, 2, 3) for d in range(1, 5 - xd)]
+ROWS = 29
+
+XFULL = {(d, y): ((d - 1) * 4 + y) * ROWS for d in (1, 2, 3) for y in range(4)}
+XFACE = [12 * ROWS + 10 * y for y in range(4)]
+XH = 12 * ROWS + 40
+XROWS = 424
+YFULL = {(d, x): ((d - 1) * 4 + x) * ROWS for d in (1, 2, 3) for x in range(4)}
+YFACE = [12 * ROWS + 10 * x for x in range(4)]
+NEAR = [(side, xd, d) for side in (0, 1) for xd in (1, 2) for d in range(1, 4 - xd)]
+EDGE = [(side, xd, 4 - xd) for side in (0, 1) for xd in (1, 2, 3)]
+YNEAR = [12 * ROWS + 40 + ROWS * n for n in range(6)]
+YEDGE = [18 * ROWS + 40 + 16 * n for n in range(6)]
+YH = [18 * ROWS + 136, 19 * ROWS + 136]
+YROWS = 720
 
 
 def mode(i, j, l):
     return 9 * i + 3 * j + l
 
 
-def call(kernel, outs, args, scratch=(), smem=(), near=()):
-    args = [
-        pltpu.with_memory_space_constraint(a, pltpu.VMEM) if n in near else a
-        for n, a in enumerate(args)
-    ]
-    specs = [
-        pl.BlockSpec(memory_space=pltpu.SMEM if n in smem else pltpu.VMEM) for n in range(len(args))
-    ]
+def call(kernel, outs, args, scratch=(), far=(), aliases=None):
+    def place(n, a):
+        return a if a.size == 1 else pltpu.with_memory_space_constraint(a, pltpu.HBM if n in far else pltpu.VMEM)
+
     return pl.pallas_call(
         kernel,
         out_shape=outs,
-        in_specs=specs,
-        out_specs=jax.tree.map(lambda _: pl.BlockSpec(memory_space=pltpu.VMEM), outs),
+        in_specs=[
+            pl.BlockSpec(memory_space=pltpu.SMEM if a.size == 1 else pltpu.HBM if n in far else pltpu.VMEM)
+            for n, a in enumerate(args)
+        ],
+        out_specs=tuple(pl.BlockSpec(memory_space=o.memory_space) for o in outs),
+        input_output_aliases=aliases or {},
+        compiler_params=pltpu.CompilerParams(vmem_limit_bytes=24 << 20),
         scratch_shapes=list(scratch),
-    )(*args)
+    )(*[place(n, a) for n, a in enumerate(args)])
+
+
+def fetch(pairs, sems):
+    copies = [pltpu.make_async_copy(a, b, sems.at[n]) for n, (a, b) in enumerate(pairs)]
+    for c in copies:
+        c.start()
+    for c in copies:
+        c.wait()
 
 
 def lane_iota(rows):
@@ -86,9 +107,10 @@
     return values
 
 
-def prep_kernel(t_ref, k_ref, a_ref, lay_ref, cols_ref, zpay_ref):
-    layers = lay_ref[0]
-    m = (lane_iota(8) < layers).astype(F32)
+def prep_kernel(t_in, k_in, a_in, lay_ref, cols_ref, zpay_ref, live_ref, t_ref, k_ref, a_ref, sems):
+    fetch(((t_in, t_ref), (k_in, k_ref), (a_in, a_ref)), sems)
+    m = (lane_iota(8) < lay_ref[0, 0, 0]).astype(F32)
+    live_ref[...] = m
     lane = lane_iota(32)
     for h in range(2):
         rows = slice(8 * h, 8 * h + 8)
@@ -139,7 +161,11 @@
         dst[row : row + part.shape[0], :] = part
         row += part.shape[0]
     dst[row : row + 1, :] = cols_ref[c * 32 + 27 : c * 32 + 28, :]
-    dst[row + 1 : at + 16, :] = jnp.zeros((at + 15 - row, 128), F32)
+
+
+def xhalo_block(even, xa_ref, xb_ref, side, at, rows):
+    a, b = xa_ref[at : at + rows, :], xb_ref[at : at + rows, :]
+    return jnp.where(even, b, a) if side == 0 else jnp.where(even, a, b)
 
 
 def xpay_kernel(cols_ref, za_ref, zb_ref, first_ref, second_ref, h_ref):
@@ -152,42 +178,50 @@
     h_ref[...] = own
 
     def write(upper_ref, lower_ref):
-        for d in range(1, 4):
-            for y in range(4):
-                at = ((d - 1) * 4 + y) * 32
-                upper_ref[at : at + 32, :] = cols_ref[((4 - d) * 4 + y) * 32 : ((4 - d) * 4 + y) * 32 + 32, :]
-                lower_ref[at : at + 32, :] = cols_ref[((d - 1) * 4 + y) * 32 : ((d - 1) * 4 + y) * 32 + 32, :]
+        for (d, y), at in XFULL.items():
+            up, down = ((4 - d) * 4 + y) * 32, ((d - 1) * 4 + y) * 32
+            upper_ref[at : at + ROWS, :] = cols_ref[up : up + ROWS, :]
+            lower_ref[at : at + ROWS, :] = cols_ref[down : down + ROWS, :]
         for y in range(4):
-            put_faces(upper_ref, 384 + 16 * y, cols_ref, y, 0, 1.0)
-            put_faces(lower_ref, 384 + 16 * y, cols_ref, 12 + y, 0, -1.0)
-        upper_ref[448:480, :] = own
-        lower_ref[448:480, :] = own
+            put_faces(upper_ref, XFACE[y], cols_ref, y, 0, 1.0)
+            put_faces(lower_ref, XFACE[y], cols_ref, 12 + y, 0, -1.0)
+        for ref in (upper_ref, lower_ref):
+            ref[XH : XH + ROWS, :] = own[0:ROWS]
 
     by_parity("gx", write, first_ref, second_ref)
 
 
 def ypay_kernel(cols_ref, xa_ref, xb_ref, h_ref, first_ref, second_ref):
-    even = lax.axis_index("gx") % 2 == 0
-
-    def halo(side, at, rows):
-        a, b = xa_ref[at : at + rows, :], xb_ref[at : at + rows, :]
-        return jnp.where(even, b, a) if side == 0 else jnp.where(even, a, b)
+    halo = functools.partial(xhalo_block, lax.axis_index("gx") % 2 == 0, xa_ref, xb_ref)
+
+    def corner(side, at, ysign):
+        xsign = 1.0 if side == 0 else -1.0
+        c = [halo(side, at + 9 * i, 9) for i in range(3)]
+        xface = c[0] + c[2] + xsign * c[1]
+        yface = [v[0:3] + v[6:9] + ysign * v[3:6] for v in c[1:]]
+        return (xface[0:3] - xsign * yface[0] - yface[1], xface[3:9], yface[0], yface[1], halo(side, at + 27, 1))
 
     def write(upper_ref, lower_ref):
+        for (d, x), at in YFULL.items():
+            up, down = (x * 4 + 4 - d) * 32, (x * 4 + d - 1) * 32
+            upper_ref[at : at + ROWS, :] = cols_ref[up : up + ROWS, :]
+            lower_ref[at : at + ROWS, :] = cols_ref[down : down + ROWS, :]
         for x in range(4):
-            for d in range(1, 4):
-                at = ((d - 1) * 4 + x) * 32
-                upper_ref[at : at + 32, :] = cols_ref[(x * 4 + 4 - d) * 32 : (x * 4 + 4 - d) * 32 + 32, :]
-                lower_ref[at : at + 32, :] = cols_ref[(x * 4 + d - 1) * 32 : (x * 4 + d - 1) * 32 + 32, :]
-            put_faces(upper_ref, 384 + 16 * x, cols_ref, x * 4, 1, 1.0)
-            put_faces(lower_ref, 384 + 16 * x, cols_ref, x * 4 + 3, 1, -1.0)
-        for n, (side, xd, d) in enumerate(CORNERS):
-            at = 448 + 32 * n
-            upper_ref[at : at + 32, :] = halo(side, ((xd - 1) * 4 + 4 - d) * 32, 32)
-            lower_ref[at : at + 32, :] = halo(side, ((xd - 1) * 4 + d - 1) * 32, 32)
-        for n, block in enumerate((halo(0, 448, 32), h_ref[...], halo(1, 448, 32))):
-            upper_ref[832 + 32 * n : 864 + 32 * n, :] = block
-            lower_ref[832 + 32 * n : 864 + 32 * n, :] = block
+            put_faces(upper_ref, YFACE[x], cols_ref, x * 4, 1, 1.0)
+            put_faces(lower_ref, YFACE[x], cols_ref, x * 4 + 3, 1, -1.0)
+        for (side, xd, d), at in zip(NEAR, YNEAR):
+            upper_ref[at : at + ROWS, :] = halo(side, XFULL[xd, 4 - d], ROWS)
+            lower_ref[at : at + ROWS, :] = halo(side, XFULL[xd, d - 1], ROWS)
+        for (side, xd, d), at in zip(EDGE, YEDGE):
+            for ref, y, sign in ((upper_ref, 4 - d, 1.0), (lower_ref, d - 1, -1.0)):
+                row = at
+                for part in corner(side, XFULL[xd, y], sign):
+                    ref[row : row + part.shape[0], :] = part
+                    row += part.shape[0]
+        beside = jnp.where(lane_iota(ROWS) // 8 % 4 < 2, halo(1, XH, ROWS), halo(0, XH, ROWS))
+        for ref in (upper_ref, lower_ref):
+            ref[YH[0] : YH[0] + ROWS, :] = h_ref[0:ROWS, :]
+            ref[YH[1] : YH[1] + ROWS, :] = beside
 
     by_parity("gy", write, first_ref, second_ref)
 
@@ -256,106 +290,66 @@
     return jnp.exp(-3.0 * (scaled * scaled))
 
 
-def main_kernel(
-    cols_ref, h_ref, xa_ref, xb_ref, ya_ref, yb_ref, own_ref, cell_ref, lay_ref,
-    t_out, pay_out,
-    m0, m1, h0, h1, cx, cy, czu, czd, ch, yz, yzh, gs, q_ref, old, inc, amat, bmat, csum,
+def place(m0, x, y, block):
+    m0[pl.ds((x + 4) * 512 + slot(y), ROWS, stride=16), :] = block
+
+
+def place_h(h0, row, y, blocks):
+    lane = lane_iota(ROWS)
+    rolled = [roll_lanes(b, (32 * n - 32 * y) % 128) if (n - y) % 4 else b for n, b in enumerate(blocks)]
+    v = jnp.where(lane < 32, rolled[0], jnp.where(lane < 64, rolled[1], rolled[2]))
+    h0[pl.ds(row, ROWS, stride=16), :] = jnp.where(lane < 96, v, 0.0)
+
+
+def pair(ref, p, m):
+    a = ref[pl.ds((4 + 2 * p) * 512 + 16 * m, 8), :]
+    b = ref[pl.ds((5 + 2 * p) * 512 + 16 * m, 8), :]
+    return jnp.where(row_iota(8) < 4, pltpu.roll(a, 6, axis=0), pltpu.roll(b, 2, axis=0))
+
+
+LOW = [mode(i, j, l) for i in range(2) for j in range(2) for l in range(2)]
+
+
+def line_modes(base, centre, near, far):
+    return modal(*[gauss_exp(base + 0.5 * n - centre, near, far) for n in range(3)])
+
+
+def pre_kernel(
+    cols_ref, h_ref, xa_ref, xb_ref, own_in, cell_in,
+    m0, h0, yz, yzh, xtab, xhtab, old, bmat, own_out,
+    cell_ref, sems,
 ):
     gx, gy, gz = lax.axis_index("gx"), lax.axis_index("gy"), lax.axis_index("gz")
-    even_x, even_y = gx % 2 == 0, gy % 2 == 0
-    lane8 = lane_iota(8)
-    idx8 = lane8 % 8
-
-    zeros8 = jnp.zeros((8, 128), F32)
+    even_x = gx % 2 == 0
+    fetch(((own_in, own_out), (cell_in, cell_ref)), sems)
 
     def clear(n, _):
-        m0[pl.ds(pl.multiple_of(n * 64, 64), 64), :] = jnp.zeros((64, 128), F32)
+        m0[pl.ds(pl.multiple_of(n * 128, 128), 128), :] = jnp.zeros((128, 128), F32)
         return 0
 
-    lax.fori_loop(0, 96, clear, 0)
-
-    def place(x, y, block):
-        m0[pl.ds((x + 4) * 512 + slot(y), 32, stride=16), :] = block
-
-    def xhalo(side, at, rows):
-        a, b = xa_ref[at : at + rows, :], xb_ref[at : at + rows, :]
-        return jnp.where(even_x, b, a) if side == 0 else jnp.where(even_x, a, b)
-
-    def yhalo(side, at, rows):
-        a, b = ya_ref[at : at + rows, :], yb_ref[at : at + rows, :]
-        return jnp.where(even_y, b, a) if side == 0 else jnp.where(even_y, a, b)
-
+    lax.fori_loop(0, 48, clear, 0)
+    h0[...] = jnp.zeros((512, 128), F32)
+    xhalo = functools.partial(xhalo_block, even_x, xa_ref, xb_ref)
     for c in range(16):
-        place(c // 4, c % 4, cols_ref[c * 32 : c * 32 + 32, :])
+        place(m0, c // 4, c % 4, cols_ref[c * 32 : c * 32 + ROWS, :])
     for side in (0, 1):
         for d in range(1, 4):
             x = -d if side == 0 else 3 + d
             for y in range(4):
-                place(x, y, xhalo(side, ((d - 1) * 4 + y) * 32, 32))
+                place(m0, x, y, xhalo(side, XFULL[d, y], ROWS))
         x = -4 if side == 0 else 7
         for y in range(4):
-            block = xhalo(side, 384 + 16 * y, 16)
+            block = xhalo(side, XFACE[y], 10)
             at = (x + 4) * 512 + slot(y)
             m0[pl.ds(at, 8, stride=16), :] = block[0:8]
             m0[pl.ds(at + 8 * 16, 1), :] = block[8:9]
             m0[pl.ds(at + 27 * 16, 1), :] = block[9:10]
-    for side in (0, 1):
-        for x in range(4):
-            for d in range(1, 4):
-                place(x, -d if side == 0 else 3 + d, yhalo(side, ((d - 1) * 4 + x) * 32, 32))
-            block = yhalo(side, 384 + 16 * x, 16)
-            at = (x + 4) * 512 + slot(-4 if side == 0 else 7)
-            for i in range(3):
-                for l in range(3):
-                    m0[pl.ds(at + mode(i, 0, l) * 16, 1), :] = block[3 * i + l : 3 * i + l + 1]
-            m0[pl.ds(at + 27 * 16, 1), :] = block[9:10]
-        for n, (xside, xd, d) in enumerate(CORNERS):
-            x = -xd if xside == 0 else 3 + xd
-            place(x, -d if side == 0 else 3 + d, yhalo(side, 448 + 32 * n, 32))
-
-    def clear_h(n, _):
-        h0[pl.ds(pl.multiple_of(n * 64, 64), 64), :] = jnp.zeros((64, 128), F32)
-        return 0
-
-    lax.fori_loop(0, 8, clear_h, 0)
-    lane32 = lane_iota(32)
-    for yb in range(3):
-        if yb == 1:
-            blocks = [xhalo(0, 448, 32), h_ref[...], xhalo(1, 448, 32)]
-        else:
-            blocks = [yhalo(yb // 2, 832 + 32 * n, 32) for n in range(3)]
-        for y in range(4):
-            rolled = [roll_lanes(b, (32 * n - 32 * y) % 128) if (n - y) % 4 else b for n, b in enumerate(blocks)]
-            v = jnp.where(lane32 < 32, rolled[0], jnp.where(lane32 < 64, rolled[1], rolled[2]))
-            v = jnp.where(lane32 < 96, v, 0.0)
-            h0[pl.ds(slot(4 * yb - 4 + y), 32, stride=16), :] = v
+    blocks = [xhalo(0, XH, ROWS), h_ref[0:ROWS, :], xhalo(1, XH, ROWS)]
+    for y in range(4):
+        place_h(h0, slot(y), y, blocks)
 
     lane16 = lane_iota(16)
     idx16 = lane16 % 8
-    kh = h0[27 * 16 : 28 * 16, :]
-    gk_src = jnp.where(idx16 == 5, roll_lanes(kh, 2), kh)
-    ch[0:16, :] = couple(kh, roll_lanes(kh, 120))
-    ch[16:32, :] = couple(kh, shift_rows(kh, True))
-    ch[32:48, :] = jnp.where((idx16 == 3) | (idx16 == 7), 0.0, couple(kh, roll_lanes(kh, 127)))
-
-    def kof(xi):
-        return m0[pl.ds(pl.multiple_of(xi * 512 + 27 * 16, 16), 16), :]
-
-    def couplings(xi, k):
-        at = pl.multiple_of(xi * 16, 16)
-        knext = kof(jnp.minimum(xi + 1, 11))
-        gk = roll_lanes(gk_src, 123 - xi * 8)
-        cx[pl.ds(at, 16), :] = couple(k, knext)
-        cy[pl.ds(at, 16), :] = couple(k, shift_rows(k, True))
-        czu[pl.ds(at, 16), :] = couple(k, jnp.where(lane16 == 127, gk, roll_lanes(k, 127)))
-        czd[pl.ds(at, 16), :] = couple(k, gk)
-        return knext
-
-    lax.fori_loop(0, 11, couplings, kof(0))
-
-    def line_modes(base, centre, near, far):
-        return modal(*[gauss_exp(base + 0.5 * n - centre, near, far) for n in range(3)])
-
     s16 = row_iota(16)
     ypos = (gy * PY + jnp.where(s16 < 12, s16 - 2, s16 - 18)).astype(F32)
     ymodes = line_modes(ypos, NY * 0.5, NY / 4.0, NY / 4.0)
@@ -368,6 +362,82 @@
             at = (3 * j + l) * 16
             yz[at : at + 16, :] = ymodes[j] * zmodes[l]
             yzh[at : at + 16, :] = ymodes[j] * zhmodes[l]
+    for step in range(STEPS):
+        centre = NX * 0.5 + step * NX / 16.0
+        for t, v in enumerate(line_modes((gx * PX + s16 - 4).astype(F32), centre, NX / 8.0, NX / 4.0)):
+            xtab[(3 * step + t) * 16 : (3 * step + t) * 16 + 16, :] = v
+        for t, v in enumerate(line_modes((gx * PX + lane_iota(8) // 8 - 4).astype(F32), centre, NX / 8.0, NX / 4.0)):
+            xhtab[(3 * step + t) * 8 : (3 * step + t) * 8 + 8, :] = v
+
+    for g, m in enumerate(LOW):
+        for p in range(2):
+            old[16 * g + 8 * p : 16 * g + 8 * p + 8, :] = pair(m0, p, m)
+    for c in range(16):
+        cell = jnp.broadcast_to(cell_ref[c : c + 1, :], (CELLS, 128))
+        hit = cell == row_iota(CELLS)
+        bmat[:, 128 * c : 128 * c + 128] = jnp.where(hit, 1.0, 0.0).astype(jnp.bfloat16)
+
+
+def main_kernel(
+    m0_in, h0_in, yz, yzh, xtab, xhtab, old, bmat, xa_ref, xb_ref, ya_ref, yb_ref, h_ref, own_ref, live_ref,
+    t_hbm, pay_out, m0, h0,
+    t_out, sem, m1, h1, cx, cy, czu, czd, ch, gs, q_ref, inc, amat, csum,
+):
+    del m0_in, h0_in
+    even_y = lax.axis_index("gy") % 2 == 0
+    lane8 = lane_iota(8)
+    zeros8 = jnp.zeros((8, 128), F32)
+
+    def yhalo(side, at, rows):
+        a, b = ya_ref[at : at + rows, :], yb_ref[at : at + rows, :]
+        return jnp.where(even_y, b, a) if side == 0 else jnp.where(even_y, a, b)
+
+    for side in (0, 1):
+        out = [-d if side == 0 else 3 + d for d in range(5)]
+        for (d, x), at in YFULL.items():
+            place(m0, x, out[d], yhalo(side, at, ROWS))
+        for x in range(4):
+            block = yhalo(side, YFACE[x], 10)
+            at = (x + 4) * 512 + slot(out[4])
+            for i in range(3):
+                for l in range(3):
+                    m0[pl.ds(at + mode(i, 0, l) * 16, 1), :] = block[3 * i + l : 3 * i + l + 1]
+            m0[pl.ds(at + 27 * 16, 1), :] = block[9:10]
+        for (xside, xd, d), at in zip(NEAR, YNEAR):
+            place(m0, -xd if xside == 0 else 3 + xd, out[d], yhalo(side, at, ROWS))
+        for (xside, xd, d), at in zip(EDGE, YEDGE):
+            block = yhalo(side, at, 16)
+            to = ((-xd if xside == 0 else 3 + xd) + 4) * 512 + slot(out[d])
+            m0[pl.ds(to, 8, stride=16), :] = block[0:8]
+            for row, m in enumerate((8, 9, 10, 11, 18, 19, 20, 27), 8):
+                m0[pl.ds(to + 16 * m, 1), :] = block[row : row + 1]
+        beside = yhalo(side, YH[1], ROWS)
+        blocks = [beside, yhalo(side, YH[0], ROWS), beside]
+        for y in range(4):
+            place_h(h0, slot(8 * side - 4 + y), y, blocks)
+
+    lane16 = lane_iota(16)
+    idx16 = lane16 % 8
+    kh = h0[27 * 16 : 28 * 16, :]
+    gk_src = jnp.where(idx16 == 5, roll_lanes(kh, 2), kh)
+    ch[0:16, :] = couple(kh, roll_lanes(kh, 120))
+    ch[16:32, :] = couple(kh, shift_rows(kh, True))
+    ch[32:48, :] = jnp.where((idx16 == 3) | (idx16 == 7), 0.0, couple(kh, roll_lanes(kh, 127)))
+
+    def kof(xi, n):
+        return m0[xi * 512 + 27 * 16 : xi * 512 + 27 * 16 + n, :]
+
+    for xi in range(11):
+        n = 16 if 2 <= xi < 9 else 8
+        at = slice(xi * 16, xi * 16 + n)
+        k = kof(xi, n)
+        cx[at, :] = couple(k, kof(xi + 1, n))
+        if xi == 0:
+            continue
+        gk = roll_lanes(gk_src[0:n], (123 - xi * 8) % 128)
+        cy[at, :] = couple(k, shift_rows(k, True))
+        czu[at, :] = couple(k, jnp.where(lane_iota(n) == 127, gk, roll_lanes(k, 127)))
+        czd[at, :] = couple(k, gk)
 
     def rows_of(ref, xi, n):
         return [ref[pl.ds(pl.multiple_of(xi * 512 + 16 * m, 8), n), :] for m in range(27)]
@@ -377,18 +447,6 @@
 
     def table(ref, n):
         return [ref[16 * t : 16 * t + n, :] for t in range(9)]
-
-    s8 = row_iota(8)
-
-    def pair(ref, p, m):
-        a = ref[pl.ds((4 + 2 * p) * 512 + 16 * m, 8), :]
-        b = ref[pl.ds((5 + 2 * p) * 512 + 16 * m, 8), :]
-        return jnp.where(s8 < 4, pltpu.roll(a, 6, axis=0), pltpu.roll(b, 2, axis=0))
-
-    low_modes = [mode(i, j, l) for i in range(2) for j in range(2) for l in range(2)]
-    for g, m in enumerate(low_modes):
-        for p in range(2):
-            old[16 * g + 8 * p : 16 * g + 8 * p + 8, :] = pair(m0, p, m)
 
     groups = [
         [(1, 3, 8), (3, 9, 16), (9, 11, 8)],
@@ -399,7 +457,6 @@
     src, dst, hsrc, hdst = m0, m1, h0, h1
     for step in range(STEPS):
         last = step == STEPS - 1
-        centre_x = NX * 0.5 + step * NX / 16.0
         hn = 16 if step < 2 else 8
         hv = [hsrc[16 * m : 16 * m + hn, :] for m in range(27)]
         lane_h = lane_iota(hn)
@@ -418,17 +475,15 @@
                 c = at_x(cx, xi, n)
                 return tuple(c * (a[1] - b[0]) for a, b in zip(line_faces(here, 9), line_faces(there, 9)))
 
-            def body(xi, carry, n=n, src=src, dst=dst, step=step, last=last, lane_n=lane_n, centre_x=centre_x):
+            def body(xi, carry, n=n, src=src, dst=dst, step=step, last=last, lane_n=lane_n):
                 left = carry
                 values = rows_of(src, xi, n)
                 following = rows_of(src, xi + 1, n)
                 right = xflux(values, following, xi, n)
                 kappa = DT * src_k(xi, n)
                 heat = src_a(xi, n)
-                base = (gx * PX + xi - 4).astype(F32) - centre_x
-                splat = jnp.full((8, 128), base, F32)
-                xm = modal(*[gauss_exp(splat + 0.5 * t, NX / 8.0, NX / 4.0) for t in range(3)])
-                heats = [heat * wide(v, n) for v in xm]
+                xm = [xtab[pl.ds((3 * step + t) * 16 + xi, 1), :] for t in range(3)]
+                heats = [heat * jnp.broadcast_to(v, (n, 128)) for v in xm]
                 c = at_x(cy, xi, n)
                 yf = []
                 for low, high in line_faces(values, 3):
@@ -458,14 +513,16 @@
                 return m0[pl.ds(pl.multiple_of(xi * 512 + 28 * 16, 8), n), :]
 
             left = xflux(rows_of(src, first - 1, n), rows_of(src, first, n), first - 1, n)
-            lax.fori_loop(first, end, body, left)
+            if end - first == 2:
+                body(first + 1, body(first, left))
+            else:
+                lax.fori_loop(0, (end - first) // 2, lambda t, c: body(first + 2 * t + 1, body(first + 2 * t, c)), left)
 
         if not last:
             n = 16 if step == 0 else 8
             hv = [v[0:n] for v in hv]
             idx_n = lane_iota(n) % 8
-            xpos = (gx * PX + lane_iota(8) // 8 - 4).astype(F32) - centre_x
-            xm = modal(*[gauss_exp(xpos + 0.5 * t, NX / 8.0, NX / 4.0) for t in range(3)])
+            xm = [xhtab[(3 * step + t) * 8 : (3 * step + t) * 8 + 8, :] for t in range(3)]
             heat = h0[28 * 16 : 28 * 16 + n, :]
             heats = [heat * wide(v, n) for v in xm]
             c = ch[0:n, :]
@@ -491,14 +548,17 @@
                 hdst[16 * m : 16 * m + n, :] = v
         src, dst, hsrc, hdst = dst, src, hdst, hsrc
 
-    live = (lane8 < lay_ref[0]).astype(F32)
+    live = live_ref[...]
     for p in range(2):
         modes = [pair(src, p, m) for m in range(27)]
-        for g, m in enumerate(low_modes):
+        for g, m in enumerate(LOW):
             at = 16 * g + 8 * p
             inc[at : at + 8, :] = (modes[m] - old[at : at + 8, :]) * live
         for n, v in enumerate(nodal_grid(modes)):
             t_out[n, 8 * p : 8 * p + 8, :] = v
+
+    out_copy = pltpu.make_async_copy(t_out, t_hbm, sem)
+    out_copy.start()
 
     ones = row_iota(16)
     for c in range(16):
@@ -512,9 +572,6 @@
         amat[128:256, lanes] = jnp.concatenate([jnp.where(k, lo, 0.0) for k in picks], axis=0).astype(jnp.bfloat16)
         owner16 = jnp.broadcast_to(own_ref[c : c + 1, :], (16, 128))
         amat[256:272, lanes] = jnp.where(owner16 == ones, wide(live, 16), 0.0).astype(jnp.bfloat16)
-        cell = jnp.broadcast_to(cell_ref[c : c + 1, :], (CELLS, 128))
-        hit = cell == row_iota(CELLS)
-        bmat[:, lanes] = jnp.where(hit, 1.0, 0.0).astype(jnp.bfloat16)
     total = lax.dot_general(
         amat[...], bmat[...], (((1,), (1,)), ((), ())), preferred_element_type=F32
     )
@@ -524,6 +581,7 @@
         for g in range(8):
             pay_out[pl.ds(2 * g + h, 16, stride=18), :] = csum[pl.ds(128 * h + g, 16, stride=8), :]
         pay_out[pl.ds(16 + h, 16, stride=18), :] = total[256:272, 128 * h : 128 * h + 128]
+    out_copy.wait()
 
 
 def gradient_table():
@@ -549,7 +607,7 @@
     return out
 
 
-def mechanics_kernel(got_ref, de_ref, st_ref, lim_ref, stress_out, force_out):
+def mechanics_kernel(got_ref, de_ref, st_ref, lim_ref, stress_hbm, force_hbm, stress_out, force_out, sems):
     sums = got_ref[0:18, :]
     for s in range(1, OWNERS):
         sums = sums + got_ref[18 * s : 18 * s + 18, :]
@@ -592,49 +650,60 @@
                     forces[c] = forces[c] + cols[d][g] * at[index[c][d]]
         for c in range(3):
             force_out[c, :, lanes] = forces[c]
+    fetch(((stress_out, stress_hbm), (force_out, force_hbm)), sems)
 
 
 def swap(first, second, axis, count):
     even = [(i, i ^ 1) for i in range(count)]
     odd = [(i, i + 1 if i % 2 else i - 1) for i in range(1, count - 1)]
-    return lax.ppermute(first, axis, even), lax.ppermute(second, axis, odd)
-
-
-def local(temps, cond, absorb, layers, owner, cell, de, st, lim):
-    rows = lambda n: pltpu.VMEM((n, 128), F32)
+    a = lax.ppermute(first, axis, even)
+    b = lax.ppermute(second, axis, odd)
+    return a, b
+
+
+def program(temps, cond, absorb, layers, owner, cell, de, st, lim):
+    vm = lambda n: pltpu.VMEM((n, 128), F32)
     sx, sy, sz = (lax.axis_size(a) for a in ("gx", "gy", "gz"))
-    temps = temps.reshape(27, 16, 128)
-    layers = layers.reshape(1)
-    cols, zpay = call(
+    cols, zpay, live = call(
         prep_kernel,
-        (rows(512), rows(32)),
-        (temps, cond.reshape(16, 128), absorb.reshape(16, 128), layers),
-        smem=(3,),
+        (vm(512), vm(32), vm(8)),
+        (temps.reshape(27, 16, 128), cond.reshape(16, 128), absorb.reshape(16, 128), layers),
+        scratch=[
+            pltpu.VMEM((27, 16, 128), F32), vm(16), vm(16), pltpu.SemaphoreType.DMA((3,)),
+        ],
+        far=(0, 1, 2, 3),
     )
     za, zb = swap(zpay, zpay, "gz", sz)
-    xf, xs, hown = call(xpay_kernel, (rows(XROWS), rows(XROWS), rows(32)), (cols, za, zb), near=(0, 1, 2))
+    xf, xs, hown = call(xpay_kernel, (vm(XROWS), vm(XROWS), vm(32)), (cols, za, zb))
     xa, xb = swap(xf, xs, "gx", sx)
-    yf, ys = call(ypay_kernel, (rows(YROWS), rows(YROWS)), (cols, xa, xb, hown), near=(0, 1, 2, 3))
+    yf, ys = call(ypay_kernel, (vm(YROWS), vm(YROWS)), (cols, xa, xb, hown))
     ya, yb = swap(yf, ys, "gy", sy)
-    vm = lambda n: pltpu.VMEM((n, 128), F32)
-    t_new, pay = call(
+    m0, h0, yz, yzh, xtab, xhtab, old, bmat, own = call(
+        pre_kernel,
+        (
+            vm(6144), vm(512), vm(144), vm(144), vm(192), vm(96), vm(128),
+            pltpu.VMEM((256, 2048), jnp.bfloat16), pltpu.VMEM((16, 128), jnp.int32),
+        ),
+        (cols, hown, xa, xb, owner.reshape(16, 128), cell.reshape(16, 128)),
+        scratch=[pltpu.VMEM((16, 128), jnp.int32), pltpu.SemaphoreType.DMA((2,))],
+        far=(4, 5),
+    )
+    t_new, pay, _, _ = call(
         main_kernel,
-        (jax.ShapeDtypeStruct((27, 16, 128), F32), rows(OWNERS * 18)),
-        (cols, hown, xa, xb, ya, yb, owner.reshape(16, 128), cell.reshape(16, 128), layers),
+        (pltpu.HBM((27, 16, 128), F32), vm(OWNERS * 18), vm(6144), vm(512)),
+        (m0, h0, yz, yzh, xtab, xhtab, old, bmat, xa, xb, ya, yb, hown, own, live),
         scratch=[
-            vm(6144), vm(6144), vm(512), vm(512),
-            vm(192), vm(192), vm(192), vm(192), vm(48), vm(144), vm(144), vm(144), vm(72), vm(128), vm(128),
-            pltpu.VMEM((272, 2048), jnp.bfloat16), pltpu.VMEM((256, 2048), jnp.bfloat16), vm(256),
+            pltpu.VMEM((27, 16, 128), F32), pltpu.SemaphoreType.DMA, vm(6144), vm(512), vm(192), vm(192), vm(192), vm(192), vm(48), vm(144), vm(72), vm(128),
+            pltpu.VMEM((272, 2048), jnp.bfloat16), vm(256),
         ],
-        smem=(8,),
-        near=(0, 1, 2, 3, 4, 5),
+        aliases={0: 2, 1: 3},
     )
     got = lax.all_to_all(pay.reshape(OWNERS, 1, 2304), "gx", 0, 0, tiled=True)
     stress, forces = call(
         mechanics_kernel,
-        (jax.ShapeDtypeStruct((6, 8, 256), F32), jax.ShapeDtypeStruct((3, 8, 256), F32)),
+        (pltpu.HBM((6, 8, 256), F32), pltpu.HBM((3, 8, 256), F32)),
         (got.reshape(OWNERS * 18, 128), de, st, lim.reshape(1, 256)),
-        near=(0,),
+        scratch=[pltpu.VMEM((6, 8, 256), F32), pltpu.VMEM((3, 8, 256), F32), pltpu.SemaphoreType.DMA((2,))],
     )
     return t_new.reshape(3, 3, 3, 4, 4, 128), stress, forces
 
@@ -644,7 +713,7 @@
     temps = P(None, None, None, "gx", "gy", "gz")
     block = P("gx", "gy", "gz")
     return jax.shard_map(
-        local,
+        program,
         mesh=mesh,
         in_specs=(
             temps, block, block, block, P("gx", "gy", "gz", None, None), P("gx", "gy", "gz", None),

time: 78.7 us -> 71.7 us (0.911)
  Pallas kernels: 14 us -> 10.3 us
  waiting for transfers between devices: 15.4 us -> 12.1 us
    pallas_call x5 -> x6, Pallas kernels: 14 us -> 10.3 us  [call(): pl.pallas_call(kernel, out_shape=outs, in_specs=[pl.BlockSpec(memory_spac...]
    ppermute x6, waiting for transfers between devices: 15.4 us -> 12.1 us  [the longest x3 8.54 us: swap(): b = lax.ppermute(second, axis, odd)]
  transfers between devices with their start and end apart: 6 -> 6, of which waited for: 5 -> 5; matrix products, arithmetic and copies ran while one was open for 0% -> 0% of each run, Pallas kernels for 0% -> 3%
where the time goes in v2:
time: 71.7 us; the launch traced here: 71.3 us
  blocking collectives  30.2 us (42%)
  starting transfers between devices  17.4 us (24%)
  waiting for transfers between devices  12.1 us (17%)
  Pallas kernels  10.3 us (14%)
  between operations  1.38 us (2%)
    all_to_all x1, blocking collectives, program(): got = lax.all_to_all(pay.reshape(OWNERS, 1, 2304), 'gx', 0, 0, tiled=True)  30.2 us
    ppermute x3, starting transfers between devices, swap(): b = lax.ppermute(second, axis, odd)  11.5 us
    pallas_call x6, Pallas kernels, call(): pl.pallas_call(kernel, out_shape=outs, in_specs=[pl.BlockSpec(memory_spac...  10.3 us
    ppermute x3, waiting for transfers between devices, swap(): b = lax.ppermute(second, axis, odd)  8.54 us
    ppermute x3, starting transfers between devices, swap(): a = lax.ppermute(first, axis, even)  5.86 us
    ppermute x3, waiting for transfers between devices, swap(): a = lax.ppermute(first, axis, even)  3.53 us
  transfers between devices with their start and end apart: 6, of which 5 were waited for; matrix products, arithmetic and copies ran while one was open for 0% of the time, Pallas kernels for 3%

profile of v2, /device:TPU:42, one launch (start us, length us, event | category | flops | bytes accessed | tf_op | source)
XLA Modules:
  0.0 71.3 jit_solution(17846606366510023551)
XLA Ops:
  1.3 1.3 %shard_map.112 = (f32[512,128]{1,0:T(8,128)S(1)}, f32[32,128]{1,0:T(8,128)S(1)}, f32[8,128]{1,0:T(8,128)S(1)}) custom-call(f32[27,16,128]{2,1,0:T(8,128)} %bitcast.12, f32[16,128]{1,0:T(8,128)} %bitcast.15, f32[16,128]{1,0:T(8,128)} %bitcast.16, s32[1,1,1]{2,1,0:T(1,128)S(6)} %copy.17.lay_ref), custom_call_target="tpu_custom_call" | custom-call | tf_op jit(solution)/shard_map/pallas_call | solution.py:51
  2.6 3.4 %collective-permute-start.1 = (f32[32,128]{1,0:T(8,128)S(1)}, f32[32,128]{1,0:T(8,128)S(1)}, u32[]{:S(2)}, u32[]{:S(2)}) collective-permute-start(f32[32,128]{1,0:T(8,128)S(1)} %get-tuple-element.25), channel_id=1, source_target_pairs={{1,2},{2,1},{5,6},{6,5},{9,10},{10,9},{13,14},{14,13},{17,18},{18,... | collective-permute-start | bytes 49160 | tf_op jit(solution)/shard_map/ppermute | solution.py:660
  6.0 1.9 %collective-permute-start = (f32[32,128]{1,0:T(8,128)S(1)}, f32[32,128]{1,0:T(8,128)S(1)}, u32[]{:S(2)}, u32[]{:S(2)}) collective-permute-start(f32[32,128]{1,0:T(8,128)S(1)} %get-tuple-element.25), channel_id=1, source_target_pairs={{0,1},{1,0},{2,3},{3,2},{4,5},{5,4},{6,7},{7,6},{8,9},{9,8},{10,11... | collective-permute-start | bytes 49160 | tf_op jit(solution)/shard_map/ppermute | solution.py:659
  7.9 0.3 collective-permute-done.1.zb_ref
  8.2 3.4 %collective-permute-done.za_ref = f32[32,128]{1,0:T(8,128)S(1)} collective-permute-done((f32[32,128]{1,0:T(8,128)S(1)}, f32[32,128]{1,0:T(8,128)S(1)}, u32[]{:S(2)}, u32[]{:S(2)}) %collective-permute-start) | collective-permute-done | bytes 16416 | tf_op jit(solution)/shard_map/ppermute | solution.py:659
  11.6 2.0 %collective-permute-start.2 = (f32[424,128]{1,0:T(8,128)S(1)}, f32[424,128]{1,0:T(8,128)S(1)}, u32[]{:S(2)}, u32[]{:S(2)}) collective-permute-start(f32[424,128]{1,0:T(8,128)S(1)} %get-tuple-element.27), channel_id=1, source_target_pairs={{0,32},{32,0},{64,96},{96,64},{128,160},{160,128},{192,224},{224,1... | collective-permute-start | bytes 651272 | tf_op jit(solution)/shard_map/ppermute | solution.py:659
  13.7 5.6 %collective-permute-start.3 = (f32[424,128]{1,0:T(8,128)S(1)}, f32[424,128]{1,0:T(8,128)S(1)}, u32[]{:S(2)}, u32[]{:S(2)}) collective-permute-start(f32[424,128]{1,0:T(8,128)S(1)} %get-tuple-element.28), channel_id=1, source_target_pairs={{32,64},{64,32},{96,128},{128,96},{160,192},{192,160},{224,256},{2... | collective-permute-start | bytes 651272 | tf_op jit(solution)/shard_map/ppermute | solution.py:660
  19.3 0.1 collective-permute-done.2.xa_ref
  19.4 3.7 %collective-permute-done.3.xb_ref = f32[424,128]{1,0:T(8,128)S(1)} collective-permute-done((f32[424,128]{1,0:T(8,128)S(1)}, f32[424,128]{1,0:T(8,128)S(1)}, u32[]{:S(2)}, u32[]{:S(2)}) %collective-permute-start.3) | collective-permute-done | bytes 217120 | tf_op jit(solution)/shard_map/ppermute | solution.py:660
  23.2 0.1 shard_map.115
  23.3 1.9 %collective-permute-start.4 = (f32[720,128]{1,0:T(8,128)S(1)}, f32[720,128]{1,0:T(8,128)S(1)}, u32[]{:S(2)}, u32[]{:S(2)}) collective-permute-start(f32[720,128]{1,0:T(8,128)S(1)} %get-tuple-element.37), channel_id=1, source_target_pairs={{0,4},{4,0},{8,12},{12,8},{16,20},{20,16},{24,28},{28,24},{1,5},{5... | collective-permute-start | bytes 1105928 | tf_op jit(solution)/shard_map/ppermute | solution.py:659
  25.2 2.5 %collective-permute-start.5 = (f32[720,128]{1,0:T(8,128)S(1)}, f32[720,128]{1,0:T(8,128)S(1)}, u32[]{:S(2)}, u32[]{:S(2)}) collective-permute-start(f32[720,128]{1,0:T(8,128)S(1)} %get-tuple-element.38), channel_id=1, source_target_pairs={{4,8},{8,4},{12,16},{16,12},{20,24},{24,20},{5,9},{9,5},{13,17},{1... | collective-permute-start | bytes 1105928 | tf_op jit(solution)/shard_map/ppermute | solution.py:660
  27.7 1.8 %shard_map.114 = (f32[6144,128]{1,0:T(8,128)S(1)}, f32[512,128]{1,0:T(8,128)S(1)}, f32[144,128]{1,0:T(8,128)S(1)}, f32[144,128]{1,0:T(8,128)S(1)}, f32[192,128]{...) custom-call(f32[512,128]{1,0:T(8,128)S(1)} %get-tuple-element.24.col, ...), custom_call_target="tpu_custom_call" | custom-call | tf_op jit(solution)/shard_map/pallas_call | solution.py:51
  29.5 0.0 collective-permute-done.4.ya_ref
  29.5 4.5 %collective-permute-done.5.yb_ref = f32[720,128]{1,0:T(8,128)S(1)} collective-permute-done((f32[720,128]{1,0:T(8,128)S(1)}, f32[720,128]{1,0:T(8,128)S(1)}, u32[]{:S(2)}, u32[]{:S(2)}) %collective-permute-start.5) | collective-permute-done | bytes 368672 | tf_op jit(solution)/shard_map/ppermute | solution.py:660
  34.0 0.0 copy-start
  34.1 0.0 copy-start.1
  34.1 0.0 copy-start.2
  34.1 6.2 %shard_map.116 = (f32[27,16,128]{2,1,0:T(8,128)}, f32[288,128]{1,0:T(8,128)S(1)}, f32[6144,128]{1,0:T(8,128)S(1)}, f32[512,128]{1,0:T(8,128)S(1)}) custom-call(f32[6144,128]{1,0:T(8,128)S(1)} %get-tuple-element.29.m0_in, f32[512,128]{1,0:T(8,128)S(1)} %get-tuple-element.30.h0_in, ...), custom_call_target="tpu_custom_call", output_to_operand_aliasing={{2}: (0, {}), {3}: (1, {})} | custom-call | tf_op jit(solution)/shard_map/pallas_call | solution.py:51
  40.3 30.2 %all_to_all.5 = f32[16,1,2304]{2,1,0:T(1,128)S(1)} all-to-all(f32[16,1,2304]{2,1,0:T(1,128)S(1)} %bitcast.10), channel_id=1, replica_groups=mesh['gx'=16,'gy'=8,'gz'=4] {'gx'}, dimensions={0} | all-to-all | bytes 294912 | tf_op jit(solution)/shard_map/all_to_all | solution.py:701
  70.5 0.0 copy-done
  70.5 0.0 copy-done.1
  70.5 0.0 copy-done.2
  70.5 0.8 %shard_map.117 = (f32[6,8,256]{2,1,0:T(8,128)}, f32[3,8,256]{2,1,0:T(8,128)}) custom-call(f32[288,128]{1,0:T(8,128)S(1)} %bitcast.9, f32[6,8,256]{2,1,0:T(8,128)S(1)} %copy-done, f32[6,8,256]{2,1,0:T(8,128)S(1)} %copy-done.1, f32[1,256]{1,0:T(1,128)S(1)} %bitcast.11), custom_call_target="tpu_custom_call" | custom-call | tf_op jit(solution)/shard_map/pallas_call | solution.py:51
  (1 shorter events, 0.0 us)
Async XLA Ops:
  2.6 5.6 %collective-permute-start.1 = (f32[32,128]{1,0:T(8,128)S(1)}, f32[32,128]{1,0:T(8,128)S(1)}, u32[]{:S(2)}, u32[]{:S(2)}) collective-permute-start(f32[32,128]{1,0:T(8,128)S(1)} %get-tuple-element.25), channel_id=1, source_target_pairs={{1,2},{2,1},{5,6},{6,5},{9,10},{10,9},{13,14},{14,13},{17,18},{18,... | collective-permute-start | bytes 49160 | tf_op jit(solution)/shard_map/ppermute | solution.py:660
  6.0 5.6 %collective-permute-start = (f32[32,128]{1,0:T(8,128)S(1)}, f32[32,128]{1,0:T(8,128)S(1)}, u32[]{:S(2)}, u32[]{:S(2)}) collective-permute-start(f32[32,128]{1,0:T(8,128)S(1)} %get-tuple-element.25), channel_id=1, source_target_pairs={{0,1},{1,0},{2,3},{3,2},{4,5},{5,4},{6,7},{7,6},{8,9},{9,8},{10,11... | collective-permute-start | bytes 49160 | tf_op jit(solution)/shard_map/ppermute | solution.py:659
  11.6 7.8 %collective-permute-start.2 = (f32[424,128]{1,0:T(8,128)S(1)}, f32[424,128]{1,0:T(8,128)S(1)}, u32[]{:S(2)}, u32[]{:S(2)}) collective-permute-start(f32[424,128]{1,0:T(8,128)S(1)} %get-tuple-element.27), channel_id=1, source_target_pairs={{0,32},{32,0},{64,96},{96,64},{128,160},{160,128},{192,224},{224,1... | collective-permute-start | bytes 651272 | tf_op jit(solution)/shard_map/ppermute | solution.py:659
  13.7 9.5 %collective-permute-start.3 = (f32[424,128]{1,0:T(8,128)S(1)}, f32[424,128]{1,0:T(8,128)S(1)}, u32[]{:S(2)}, u32[]{:S(2)}) collective-permute-start(f32[424,128]{1,0:T(8,128)S(1)} %get-tuple-element.28), channel_id=1, source_target_pairs={{32,64},{64,32},{96,128},{128,96},{160,192},{192,160},{224,256},{2... | collective-permute-start | bytes 651272 | tf_op jit(solution)/shard_map/ppermute | solution.py:660
  23.3 6.2 %collective-permute-start.4 = (f32[720,128]{1,0:T(8,128)S(1)}, f32[720,128]{1,0:T(8,128)S(1)}, u32[]{:S(2)}, u32[]{:S(2)}) collective-permute-start(f32[720,128]{1,0:T(8,128)S(1)} %get-tuple-element.37), channel_id=1, source_target_pairs={{0,4},{4,0},{8,12},{12,8},{16,20},{20,16},{24,28},{28,24},{1,5},{5... | collective-permute-start | bytes 1105928 | tf_op jit(solution)/shard_map/ppermute | solution.py:659
  25.2 8.8 %collective-permute-start.5 = (f32[720,128]{1,0:T(8,128)S(1)}, f32[720,128]{1,0:T(8,128)S(1)}, u32[]{:S(2)}, u32[]{:S(2)}) collective-permute-start(f32[720,128]{1,0:T(8,128)S(1)} %get-tuple-element.38), channel_id=1, source_target_pairs={{4,8},{8,4},{12,16},{16,12},{20,24},{24,20},{5,9},{9,5},{13,17},{1... | collective-permute-start | bytes 1105928 | tf_op jit(solution)/shard_map/ppermute | solution.py:660
  34.0 36.5 %copy-start = (f32[6,8,256]{2,1,0:T(8,128)S(1)}, f32[6,8,256]{2,1,0:T(8,128)}, u32[]{:S(2)}) copy-start(f32[6,8,256]{2,1,0:T(8,128)} %de_ref.1) | copy-start | bytes 147460
  34.1 36.5 %copy-start.1 = (f32[6,8,256]{2,1,0:T(8,128)S(1)}, f32[6,8,256]{2,1,0:T(8,128)}, u32[]{:S(2)}) copy-start(f32[6,8,256]{2,1,0:T(8,128)} %st_ref.1) | copy-start | bytes 147460
  34.1 36.5 %copy-start.2 = (f32[256]{0:T(256)S(1)}, f32[256]{0:T(256)}, u32[]{:S(2)}) copy-start(f32[256]{0:T(256)} %param.17) | copy-start | bytes 3076

commit v3 on v2

--- a/solution.py
+++ b/solution.py
@@ -21,6 +21,7 @@
 NX, NY, NZ = 64, 32, 512
 PX, PY, PZ = 4, 4, 128
 OWNERS, CELLS = 16, 256
+FIRST = 8
 F32 = jnp.float32
 
 LAM = (0.0, 12.0, 24.0)
@@ -131,8 +132,13 @@
     zpay_ref[...] = acc
 
 
+def upper_first(axis):
+    at = lax.axis_index(axis)
+    return (at + lax.axis_index("gy") if axis == "gx" else at) % 2 == 0
+
+
 def by_parity(axis, write, first, second):
-    even = lax.axis_index(axis) % 2 == 0
+    even = upper_first(axis)
 
     @pl.when(even)
     def _():
@@ -169,7 +175,7 @@
 
 
 def xpay_kernel(cols_ref, za_ref, zb_ref, first_ref, second_ref, h_ref):
-    even = lax.axis_index("gz") % 2 == 0
+    even = upper_first("gz")
     idx = lane_iota(32) % 8
     za, zb = za_ref[...], zb_ref[...]
     upper = jnp.where(even, za, zb)
@@ -192,7 +198,7 @@
 
 
 def ypay_kernel(cols_ref, xa_ref, xb_ref, h_ref, first_ref, second_ref):
-    halo = functools.partial(xhalo_block, lax.axis_index("gx") % 2 == 0, xa_ref, xb_ref)
+    halo = functools.partial(xhalo_block, upper_first("gx"), xa_ref, xb_ref)
 
     def corner(side, at, ysign):
         xsign = 1.0 if side == 0 else -1.0
@@ -254,6 +260,21 @@
         if base // stride % 3 == 0:
             e = values[base] + values[base + 2 * stride]
             out.append((e - values[base + stride], e + values[base + stride]))
+    return out
+
+
+def bounded(inner, outer, c, c_outer):
+    rows = row_iota(8)
+    top, bottom = rows == 7, rows == 0
+    turn = jnp.where(bottom, -1.0, 1.0)
+    c_below = pltpu.roll(c_outer, 1, axis=0)
+    out = []
+    for n, (low, high) in enumerate(line_faces(inner, 3)):
+        base = n // 3 * 9 + n % 3
+        beside = outer[base] + outer[base + 6] + turn * outer[base + 3]
+        up = c * (high - jnp.where(top, pltpu.roll(beside, 7, axis=0), pltpu.roll(low, 7, axis=0)))
+        down = jnp.where(bottom, c_below * (pltpu.roll(beside, 1, axis=0) - low), pltpu.roll(up, 1, axis=0))
+        out.append((down, up))
     return out
 
 
@@ -320,7 +341,7 @@
     cell_ref, sems,
 ):
     gx, gy, gz = lax.axis_index("gx"), lax.axis_index("gy"), lax.axis_index("gz")
-    even_x = gx % 2 == 0
+    even_x = upper_first("gx")
     fetch(((own_in, own_out), (cell_in, cell_ref)), sems)
 
     def clear(n, _):
@@ -384,7 +405,7 @@
     t_out, sem, m1, h1, cx, cy, czu, czd, ch, gs, q_ref, inc, amat, csum,
 ):
     del m0_in, h0_in
-    even_y = lax.axis_index("gy") % 2 == 0
+    even_y = upper_first("gy")
     lane8 = lane_iota(8)
     zeros8 = jnp.zeros((8, 128), F32)
 
@@ -449,15 +470,30 @@
         return [ref[16 * t : 16 * t + n, :] for t in range(9)]
 
     groups = [
-        [(1, 3, 8), (3, 9, 16), (9, 11, 8)],
-        [(2, 4, 8), (4, 8, 16), (8, 10, 8)],
-        [(3, 9, 8)],
-        [(4, 8, 8)],
+        [(1, 3, 8, False), (3, 4, 8, True), (4, 8, 16, False), (8, 9, 8, True), (9, 11, 8, False)],
+        [(2, 4, 8, False), (4, 8, 8, True), (8, 10, 8, False)],
+        [(3, 9, 8, False)],
+        [(4, 6, 8, False), (6, 8, 8, False)],
     ]
+    live = live_ref[...]
+    out_copies = [
+        pltpu.make_async_copy(t_out.at[:, 8 * p : 8 * p + 8, :], t_hbm.at[:, 8 * p : 8 * p + 8, :], sem.at[p])
+        for p in range(2)
+    ]
+
+    def finish(ref, p):
+        modes = [pair(ref, p, m) for m in range(27)]
+        for n, v in enumerate(nodal_grid(modes)):
+            t_out[n, 8 * p : 8 * p + 8, :] = v
+        out_copies[p].start()
+        for g, m in enumerate(LOW):
+            at = 16 * g + 8 * p
+            inc[at : at + 8, :] = (modes[m] - old[at : at + 8, :]) * live
+
     src, dst, hsrc, hdst = m0, m1, h0, h1
     for step in range(STEPS):
         last = step == STEPS - 1
-        hn = 16 if step < 2 else 8
+        hn = 16 if step == 0 else 8
         hv = [hsrc[16 * m : 16 * m + hn, :] for m in range(27)]
         lane_h = lane_iota(hn)
         idx_h = lane_h % 8
@@ -468,14 +504,14 @@
             for t in range(9):
                 q_ref[8 * t : 8 * t + 8, :] = zeros8
 
-        for first, end, n in groups[step]:
+        for first, end, n, beyond in groups[step]:
             lane_n = lane_iota(n)
 
             def xflux(here, there, xi, n=n):
                 c = at_x(cx, xi, n)
                 return tuple(c * (a[1] - b[0]) for a, b in zip(line_faces(here, 9), line_faces(there, 9)))
 
-            def body(xi, carry, n=n, src=src, dst=dst, step=step, last=last, lane_n=lane_n):
+            def body(xi, carry, n=n, src=src, dst=dst, step=step, last=last, lane_n=lane_n, beyond=beyond):
                 left = carry
                 values = rows_of(src, xi, n)
                 following = rows_of(src, xi + 1, n)
@@ -485,10 +521,14 @@
                 xm = [xtab[pl.ds((3 * step + t) * 16 + xi, 1), :] for t in range(3)]
                 heats = [heat * jnp.broadcast_to(v, (n, 128)) for v in xm]
                 c = at_x(cy, xi, n)
-                yf = []
-                for low, high in line_faces(values, 3):
-                    up = c * (high - shift_rows(low, True))
-                    yf.append((shift_rows(up, False), up))
+                if beyond:
+                    outer = [src[pl.ds(pl.multiple_of(xi * 512 + 16 * m + 8, 8), 8), :] for m in range(27)]
+                    yf = bounded(values, outer, c, cy[pl.ds(pl.multiple_of(xi * 16 + 8, 8), 8), :])
+                else:
+                    yf = []
+                    for low, high in line_faces(values, 3):
+                        up = c * (high - shift_rows(low, True))
+                        yf.append((shift_rows(up, False), up))
                 cu, cd = at_x(czu, xi, n), at_x(czd, xi, n)
                 zf = []
                 shift = 123 - xi * 8
@@ -513,65 +553,59 @@
                 return m0[pl.ds(pl.multiple_of(xi * 512 + 28 * 16, 8), n), :]
 
             left = xflux(rows_of(src, first - 1, n), rows_of(src, first, n), first - 1, n)
-            if end - first == 2:
-                body(first + 1, body(first, left))
+            if end - first <= 2:
+                for xi in range(first, end):
+                    left = body(xi, left)
+                if last:
+                    finish(dst, first // 2 - 2)
             else:
                 lax.fori_loop(0, (end - first) // 2, lambda t, c: body(first + 2 * t + 1, body(first + 2 * t, c)), left)
 
         if not last:
-            n = 16 if step == 0 else 8
-            hv = [v[0:n] for v in hv]
+            n = 8
+            inner = [v[0:8] for v in hv]
             idx_n = lane_iota(n) % 8
             xm = [xhtab[(3 * step + t) * 8 : (3 * step + t) * 8 + 8, :] for t in range(3)]
             heat = h0[28 * 16 : 28 * 16 + n, :]
             heats = [heat * wide(v, n) for v in xm]
             c = ch[0:n, :]
             xf = []
-            for low, high in line_faces(hv, 9):
+            for low, high in line_faces(inner, 9):
                 up = c * (high - roll_lanes(low, 120))
                 xf.append((roll_lanes(up, 8), up))
             c = ch[16 : 16 + n, :]
-            yf = []
-            for low, high in line_faces(hv, 3):
-                up = c * (high - shift_rows(low, True))
-                yf.append((shift_rows(up, False), up))
+            if step == 0:
+                yf = bounded(inner, [v[8:16] for v in hv], c, ch[24:32, :])
+            else:
+                yf = []
+                for low, high in line_faces(inner, 3):
+                    up = c * (high - shift_rows(low, True))
+                    yf.append((shift_rows(up, False), up))
             c = ch[32 : 32 + n, :]
             zf = []
-            for t, (low, high) in enumerate(line_faces(hv, 1)):
+            for t, (low, high) in enumerate(line_faces(inner, 1)):
                 up = c * (high - roll_lanes(low, 127))
                 q = wide(q_ref[8 * t : 8 * t + 8, :], n)
                 down = jnp.where(idx_n == 4, q, roll_lanes(up, 1))
                 zf.append((down, jnp.where(idx_n == 3, roll_lanes(q, 126), up)))
             kappa = DT * h0[27 * 16 : 27 * 16 + n, :]
-            out = advance(hv, kappa, heats, table(yzh, n), (xf, yf, zf))
+            out = advance(inner, kappa, heats, table(yzh, n), (xf, yf, zf))
             for m, v in enumerate(out):
                 hdst[16 * m : 16 * m + n, :] = v
         src, dst, hsrc, hdst = dst, src, hdst, hsrc
 
-    live = live_ref[...]
-    for p in range(2):
-        modes = [pair(src, p, m) for m in range(27)]
-        for g, m in enumerate(LOW):
-            at = 16 * g + 8 * p
-            inc[at : at + 8, :] = (modes[m] - old[at : at + 8, :]) * live
-        for n, v in enumerate(nodal_grid(modes)):
-            t_out[n, 8 * p : 8 * p + 8, :] = v
-
-    out_copy = pltpu.make_async_copy(t_out, t_hbm, sem)
-    out_copy.start()
-
-    ones = row_iota(16)
+    slots = (row_iota(16) + FIRST) % OWNERS
     for c in range(16):
         lanes = slice(128 * c, 128 * c + 128)
         v = inc[pl.ds(c, 8, stride=16), :]
         hi = v.astype(jnp.bfloat16).astype(F32)
         lo = v - hi
         owner = jnp.broadcast_to(own_ref[c : c + 1, :], (8, 128))
-        picks = [owner == o for o in range(OWNERS)]
+        picks = [owner == (o + FIRST) % OWNERS for o in range(OWNERS)]
         amat[0:128, lanes] = jnp.concatenate([jnp.where(k, hi, 0.0) for k in picks], axis=0).astype(jnp.bfloat16)
         amat[128:256, lanes] = jnp.concatenate([jnp.where(k, lo, 0.0) for k in picks], axis=0).astype(jnp.bfloat16)
         owner16 = jnp.broadcast_to(own_ref[c : c + 1, :], (16, 128))
-        amat[256:272, lanes] = jnp.where(owner16 == ones, wide(live, 16), 0.0).astype(jnp.bfloat16)
+        amat[256:272, lanes] = jnp.where(owner16 == slots, wide(live, 16), 0.0).astype(jnp.bfloat16)
     total = lax.dot_general(
         amat[...], bmat[...], (((1,), (1,)), ((), ())), preferred_element_type=F32
     )
@@ -581,7 +615,8 @@
         for g in range(8):
             pay_out[pl.ds(2 * g + h, 16, stride=18), :] = csum[pl.ds(128 * h + g, 16, stride=8), :]
         pay_out[pl.ds(16 + h, 16, stride=18), :] = total[256:272, 128 * h : 128 * h + 128]
-    out_copy.wait()
+    for c in out_copies:
+        c.wait()
 
 
 def gradient_table():
@@ -656,6 +691,13 @@
 def swap(first, second, axis, count):
     even = [(i, i ^ 1) for i in range(count)]
     odd = [(i, i + 1 if i % 2 else i - 1) for i in range(1, count - 1)]
+    if axis == "gx":
+        turns = lax.axis_size("gy")
+        even, odd = (
+            [(a * turns + t, b * turns + t) for t in range(turns) for a, b in (one, two)[t % 2]]
+            for one, two in ((even, odd), (odd, even))
+        )
+        axis = ("gx", "gy")
     a = lax.ppermute(first, axis, even)
     b = lax.ppermute(second, axis, odd)
     return a, b
@@ -693,12 +735,13 @@
         (pltpu.HBM((27, 16, 128), F32), vm(OWNERS * 18), vm(6144), vm(512)),
         (m0, h0, yz, yzh, xtab, xhtab, old, bmat, xa, xb, ya, yb, hown, own, live),
         scratch=[
-            pltpu.VMEM((27, 16, 128), F32), pltpu.SemaphoreType.DMA, vm(6144), vm(512), vm(192), vm(192), vm(192), vm(192), vm(48), vm(144), vm(72), vm(128),
+            pltpu.VMEM((27, 16, 128), F32), pltpu.SemaphoreType.DMA((2,)), vm(6144), vm(512), vm(192), vm(192), vm(192), vm(192), vm(48), vm(144), vm(72), vm(128),
             pltpu.VMEM((272, 2048), jnp.bfloat16), vm(256),
         ],
         aliases={0: 2, 1: 3},
     )
-    got = lax.all_to_all(pay.reshape(OWNERS, 1, 2304), "gx", 0, 0, tiled=True)
+    group = [(o + FIRST) % OWNERS for o in range(OWNERS)]
+    got = lax.all_to_all(pay.reshape(OWNERS, 1, 2304), "gx", 0, 0, axis_index_groups=[group], tiled=True)
     stress, forces = call(
         mechanics_kernel,
         (pltpu.HBM((6, 8, 256), F32), pltpu.HBM((3, 8, 256), F32)),

time: 71.7 us -> 66.6 us (0.929)
  the two profiles are of different devices: /device:TPU:42 before, /device:TPU:19 now
where the time goes in v3:
time: 66.6 us; the launch traced here: 66.2 us
  blocking collectives  27 us (41%)
  starting transfers between devices  17.3 us (26%)
  waiting for transfers between devices  10.7 us (16%)
  Pallas kernels  9.73 us (15%)
  between operations  1.39 us (2%)
    all_to_all x1, blocking collectives, program(): lax.all_to_all(pay.reshape(OWNERS, 1, 2304), 'gx', 0, 0, axis_index_group...  27 us
    ppermute x3, starting transfers between devices, swap(): b = lax.ppermute(second, axis, odd)  12.8 us
    pallas_call x6, Pallas kernels, call(): pl.pallas_call(kernel, out_shape=outs, in_specs=[pl.BlockSpec(memory_spac...  9.73 us
    ppermute x3, waiting for transfers between devices, swap(): b = lax.ppermute(second, axis, odd)  8.19 us
    ppermute x3, starting transfers between devices, swap(): a = lax.ppermute(first, axis, even)  4.52 us
    ppermute x3, waiting for transfers between devices, swap(): a = lax.ppermute(first, axis, even)  2.55 us
  transfers between devices with their start and end apart: 6, of which 3 were waited for; matrix products, arithmetic and copies ran while one was open for 0% of the time, Pallas kernels for 3%

profile of v3, /device:TPU:19, one launch (start us, length us, event | category | flops | bytes accessed | tf_op | source)
XLA Modules:
  0.0 66.2 jit_solution(6504442939498841989)
XLA Ops:
  1.3 1.3 %shard_map.112 = (f32[512,128]{1,0:T(8,128)S(1)}, f32[32,128]{1,0:T(8,128)S(1)}, f32[8,128]{1,0:T(8,128)S(1)}) custom-call(f32[27,16,128]{2,1,0:T(8,128)} %bitcast.12, f32[16,128]{1,0:T(8,128)} %bitcast.15, f32[16,128]{1,0:T(8,128)} %bitcast.16, s32[1,1,1]{2,1,0:T(1,128)S(6)} %copy.17.lay_ref), custom_call_target="tpu_custom_call" | custom-call | tf_op jit(solution)/shard_map/pallas_call | solution.py:52
  2.6 3.1 %collective-permute-start.1 = (f32[32,128]{1,0:T(8,128)S(1)}, f32[32,128]{1,0:T(8,128)S(1)}, u32[]{:S(2)}, u32[]{:S(2)}) collective-permute-start(f32[32,128]{1,0:T(8,128)S(1)} %get-tuple-element.25), channel_id=1, source_target_pairs={{1,2},{2,1},{5,6},{6,5},{9,10},{10,9},{13,14},{14,13},{17,18},{18,... | collective-permute-start | bytes 49160 | tf_op jit(solution)/shard_map/ppermute | solution.py:702
  5.7 1.9 %collective-permute-start = (f32[32,128]{1,0:T(8,128)S(1)}, f32[32,128]{1,0:T(8,128)S(1)}, u32[]{:S(2)}, u32[]{:S(2)}) collective-permute-start(f32[32,128]{1,0:T(8,128)S(1)} %get-tuple-element.25), channel_id=1, source_target_pairs={{0,1},{1,0},{2,3},{3,2},{4,5},{5,4},{6,7},{7,6},{8,9},{9,8},{10,11... | collective-permute-start | bytes 49160 | tf_op jit(solution)/shard_map/ppermute | solution.py:701
  7.6 0.0 collective-permute-done.1.zb_ref
  7.6 2.5 %collective-permute-done.za_ref = f32[32,128]{1,0:T(8,128)S(1)} collective-permute-done((f32[32,128]{1,0:T(8,128)S(1)}, f32[32,128]{1,0:T(8,128)S(1)}, u32[]{:S(2)}, u32[]{:S(2)}) %collective-permute-start) | collective-permute-done | bytes 16416 | tf_op jit(solution)/shard_map/ppermute | solution.py:701
  10.2 0.7 %collective-permute-start.2 = (f32[424,128]{1,0:T(8,128)S(1)}, f32[424,128]{1,0:T(8,128)S(1)}, u32[]{:S(2)}, u32[]{:S(2)}) collective-permute-start(f32[424,128]{1,0:T(8,128)S(1)} %get-tuple-element.27), channel_id=1, source_target_pairs={{0,32},{32,0},{64,96},{96,64},{128,160},{160,128},{192,224},{224,1... | collective-permute-start | bytes 651272 | tf_op jit(solution)/shard_map/ppermute | solution.py:701
  10.9 6.4 %collective-permute-start.3 = (f32[424,128]{1,0:T(8,128)S(1)}, f32[424,128]{1,0:T(8,128)S(1)}, u32[]{:S(2)}, u32[]{:S(2)}) collective-permute-start(f32[424,128]{1,0:T(8,128)S(1)} %get-tuple-element.28), channel_id=1, source_target_pairs={{32,64},{64,32},{96,128},{128,96},{160,192},{192,160},{224,256},{2... | collective-permute-start | bytes 651272 | tf_op jit(solution)/shard_map/ppermute | solution.py:702
  17.3 0.0 collective-permute-done.2.xa_ref
  17.3 4.4 %collective-permute-done.3.xb_ref = f32[424,128]{1,0:T(8,128)S(1)} collective-permute-done((f32[424,128]{1,0:T(8,128)S(1)}, f32[424,128]{1,0:T(8,128)S(1)}, u32[]{:S(2)}, u32[]{:S(2)}) %collective-permute-start.3) | collective-permute-done | bytes 217120 | tf_op jit(solution)/shard_map/ppermute | solution.py:702
  21.7 0.1 shard_map.115
  21.9 1.9 %collective-permute-start.4 = (f32[720,128]{1,0:T(8,128)S(1)}, f32[720,128]{1,0:T(8,128)S(1)}, u32[]{:S(2)}, u32[]{:S(2)}) collective-permute-start(f32[720,128]{1,0:T(8,128)S(1)} %get-tuple-element.37), channel_id=1, source_target_pairs={{0,4},{4,0},{8,12},{12,8},{16,20},{20,16},{24,28},{28,24},{1,5},{5... | collective-permute-start | bytes 1105928 | tf_op jit(solution)/shard_map/ppermute | solution.py:701
  23.8 3.3 %collective-permute-start.5 = (f32[720,128]{1,0:T(8,128)S(1)}, f32[720,128]{1,0:T(8,128)S(1)}, u32[]{:S(2)}, u32[]{:S(2)}) collective-permute-start(f32[720,128]{1,0:T(8,128)S(1)} %get-tuple-element.38), channel_id=1, source_target_pairs={{4,8},{8,4},{12,16},{16,12},{20,24},{24,20},{5,9},{9,5},{13,17},{1... | collective-permute-start | bytes 1105928 | tf_op jit(solution)/shard_map/ppermute | solution.py:702
  27.1 1.8 %shard_map.114 = (f32[6144,128]{1,0:T(8,128)S(1)}, f32[512,128]{1,0:T(8,128)S(1)}, f32[144,128]{1,0:T(8,128)S(1)}, f32[144,128]{1,0:T(8,128)S(1)}, f32[192,128]{...) custom-call(f32[512,128]{1,0:T(8,128)S(1)} %get-tuple-element.24.col, ...), custom_call_target="tpu_custom_call" | custom-call | tf_op jit(solution)/shard_map/pallas_call | solution.py:52
  28.9 0.0 collective-permute-done.4.ya_ref
  28.9 3.8 %collective-permute-done.5.yb_ref = f32[720,128]{1,0:T(8,128)S(1)} collective-permute-done((f32[720,128]{1,0:T(8,128)S(1)}, f32[720,128]{1,0:T(8,128)S(1)}, u32[]{:S(2)}, u32[]{:S(2)}) %collective-permute-start.5) | collective-permute-done | bytes 368672 | tf_op jit(solution)/shard_map/ppermute | solution.py:702
  32.7 0.0 copy-start
  32.7 0.0 copy-start.1
  32.7 0.0 copy-start.2
  32.7 5.7 %shard_map.116 = (f32[27,16,128]{2,1,0:T(8,128)}, f32[288,128]{1,0:T(8,128)S(1)}, f32[6144,128]{1,0:T(8,128)S(1)}, f32[512,128]{1,0:T(8,128)S(1)}) custom-call(f32[6144,128]{1,0:T(8,128)S(1)} %get-tuple-element.29.m0_in, f32[512,128]{1,0:T(8,128)S(1)} %get-tuple-element.30.h0_in, ...), custom_call_target="tpu_custom_call", output_to_operand_aliasing={{2}: (0, {}), {3}: (1, {})} | custom-call | tf_op jit(solution)/shard_map/pallas_call | solution.py:52
  38.4 27.0 %all_to_all.5 = f32[16,1,2304]{2,1,0:T(1,128)S(1)} all-to-all(f32[16,1,2304]{2,1,0:T(1,128)S(1)} %bitcast.10), channel_id=1, replica_groups={{256,288,320,352,384,416,448,480,0,32,64,96,128,160,192,224},{257,289,3..., dimensions={0} | all-to-all | bytes 294912 | tf_op jit(solution)/shard_map/all_to_all | solution.py:744
  65.4 0.0 copy-done
  65.4 0.0 copy-done.1
  65.4 0.0 copy-done.2
  65.4 0.8 %shard_map.117 = (f32[6,8,256]{2,1,0:T(8,128)}, f32[3,8,256]{2,1,0:T(8,128)}) custom-call(f32[288,128]{1,0:T(8,128)S(1)} %bitcast.9, f32[6,8,256]{2,1,0:T(8,128)S(1)} %copy-done, f32[6,8,256]{2,1,0:T(8,128)S(1)} %copy-done.1, f32[1,256]{1,0:T(1,128)S(1)} %bitcast.11), custom_call_target="tpu_custom_call" | custom-call | tf_op jit(solution)/shard_map/pallas_call | solution.py:52
  (1 shorter events, 0.0 us)
Async XLA Ops:
  2.6 5.1 %collective-permute-start.1 = (f32[32,128]{1,0:T(8,128)S(1)}, f32[32,128]{1,0:T(8,128)S(1)}, u32[]{:S(2)}, u32[]{:S(2)}) collective-permute-start(f32[32,128]{1,0:T(8,128)S(1)} %get-tuple-element.25), channel_id=1, source_target_pairs={{1,2},{2,1},{5,6},{6,5},{9,10},{10,9},{13,14},{14,13},{17,18},{18,... | collective-permute-start | bytes 49160 | tf_op jit(solution)/shard_map/ppermute | solution.py:702
  5.7 4.5 %collective-permute-start = (f32[32,128]{1,0:T(8,128)S(1)}, f32[32,128]{1,0:T(8,128)S(1)}, u32[]{:S(2)}, u32[]{:S(2)}) collective-permute-start(f32[32,128]{1,0:T(8,128)S(1)} %get-tuple-element.25), channel_id=1, source_target_pairs={{0,1},{1,0},{2,3},{3,2},{4,5},{5,4},{6,7},{7,6},{8,9},{9,8},{10,11... | collective-permute-start | bytes 49160 | tf_op jit(solution)/shard_map/ppermute | solution.py:701
  10.2 7.1 %collective-permute-start.2 = (f32[424,128]{1,0:T(8,128)S(1)}, f32[424,128]{1,0:T(8,128)S(1)}, u32[]{:S(2)}, u32[]{:S(2)}) collective-permute-start(f32[424,128]{1,0:T(8,128)S(1)} %get-tuple-element.27), channel_id=1, source_target_pairs={{0,32},{32,0},{64,96},{96,64},{128,160},{160,128},{192,224},{224,1... | collective-permute-start | bytes 651272 | tf_op jit(solution)/shard_map/ppermute | solution.py:701
  10.9 10.8 %collective-permute-start.3 = (f32[424,128]{1,0:T(8,128)S(1)}, f32[424,128]{1,0:T(8,128)S(1)}, u32[]{:S(2)}, u32[]{:S(2)}) collective-permute-start(f32[424,128]{1,0:T(8,128)S(1)} %get-tuple-element.28), channel_id=1, source_target_pairs={{32,64},{64,32},{96,128},{128,96},{160,192},{192,160},{224,256},{2... | collective-permute-start | bytes 651272 | tf_op jit(solution)/shard_map/ppermute | solution.py:702
  21.9 7.1 %collective-permute-start.4 = (f32[720,128]{1,0:T(8,128)S(1)}, f32[720,128]{1,0:T(8,128)S(1)}, u32[]{:S(2)}, u32[]{:S(2)}) collective-permute-start(f32[720,128]{1,0:T(8,128)S(1)} %get-tuple-element.37), channel_id=1, source_target_pairs={{0,4},{4,0},{8,12},{12,8},{16,20},{20,16},{24,28},{28,24},{1,5},{5... | collective-permute-start | bytes 1105928 | tf_op jit(solution)/shard_map/ppermute | solution.py:701
  23.8 8.9 %collective-permute-start.5 = (f32[720,128]{1,0:T(8,128)S(1)}, f32[720,128]{1,0:T(8,128)S(1)}, u32[]{:S(2)}, u32[]{:S(2)}) collective-permute-start(f32[720,128]{1,0:T(8,128)S(1)} %get-tuple-element.38), channel_id=1, source_target_pairs={{4,8},{8,4},{12,16},{16,12},{20,24},{24,20},{5,9},{9,5},{13,17},{1... | collective-permute-start | bytes 1105928 | tf_op jit(solution)/shard_map/ppermute | solution.py:702
  32.7 32.7 %copy-start = (f32[6,8,256]{2,1,0:T(8,128)S(1)}, f32[6,8,256]{2,1,0:T(8,128)}, u32[]{:S(2)}) copy-start(f32[6,8,256]{2,1,0:T(8,128)} %de_ref.1) | copy-start | bytes 147460
  32.7 32.7 %copy-start.1 = (f32[6,8,256]{2,1,0:T(8,128)S(1)}, f32[6,8,256]{2,1,0:T(8,128)}, u32[]{:S(2)}) copy-start(f32[6,8,256]{2,1,0:T(8,128)} %st_ref.1) | copy-start | bytes 147460
  32.7 32.7 %copy-start.2 = (f32[256]{0:T(256)S(1)}, f32[256]{0:T(256)}, u32[]{:S(2)}) copy-start(f32[256]{0:T(256)} %param.17) | copy-start | bytes 3076

commit v4 on v3

--- a/solution.py
+++ b/solution.py
@@ -26,19 +26,17 @@
 
 LAM = (0.0, 12.0, 24.0)
 ROWS = 29
-
-XFULL = {(d, y): ((d - 1) * 4 + y) * ROWS for d in (1, 2, 3) for y in range(4)}
-XFACE = [12 * ROWS + 10 * y for y in range(4)]
-XH = 12 * ROWS + 40
-XROWS = 424
-YFULL = {(d, x): ((d - 1) * 4 + x) * ROWS for d in (1, 2, 3) for x in range(4)}
-YFACE = [12 * ROWS + 10 * x for x in range(4)]
-NEAR = [(side, xd, d) for side in (0, 1) for xd in (1, 2) for d in range(1, 4 - xd)]
-EDGE = [(side, xd, 4 - xd) for side in (0, 1) for xd in (1, 2, 3)]
-YNEAR = [12 * ROWS + 40 + ROWS * n for n in range(6)]
-YEDGE = [18 * ROWS + 40 + 16 * n for n in range(6)]
-YH = [18 * ROWS + 136, 19 * ROWS + 136]
-YROWS = 720
+FAR = 20
+
+X1 = [ROWS * y for y in range(4)]
+X2 = [4 * ROWS + FAR * y for y in range(4)]
+XH = 4 * ROWS + 4 * FAR
+XROWS = 232
+Y1, Y2 = X1, X2
+NEAR = [(0, XH), (1, XH + ROWS)]
+EDGE = [(side, xd, 3 - xd, XH + 2 * ROWS + 4 * (2 * side + xd - 1)) for side in (0, 1) for xd in (1, 2)]
+YH = [XH + 2 * ROWS + 16, XH + 3 * ROWS + 16]
+YROWS = 328
 
 
 def mode(i, j, l):
@@ -149,24 +147,22 @@
         write(second, first)
 
 
-def face_rows(cols_ref, c, axis, sign):
-    base = c * 32
+def put(dst, at, parts):
+    for part in parts:
+        dst[at : at + part.shape[0], :] = part
+        at += part.shape[0]
+
+
+def far_modes(column, axis, sign):
+    half = 0.5 * sign
     if axis == 0:
-        parts = [cols_ref[base + 9 * i : base + 9 * i + 9, :] for i in range(3)]
-        return [parts[0] + parts[2] + sign * parts[1]]
+        odd = half * column[9:18]
+        return [column[0:9] + odd, column[18:27] + odd, column[27:29]]
     out = []
     for i in range(3):
-        parts = [cols_ref[base + 9 * i + 3 * j : base + 9 * i + 3 * j + 3, :] for j in range(3)]
-        out.append(parts[0] + parts[2] + sign * parts[1])
-    return out
-
-
-def put_faces(dst, at, cols_ref, c, axis, sign):
-    row = at
-    for part in face_rows(cols_ref, c, axis, sign):
-        dst[row : row + part.shape[0], :] = part
-        row += part.shape[0]
-    dst[row : row + 1, :] = cols_ref[c * 32 + 27 : c * 32 + 28, :]
+        odd = half * column[9 * i + 3 : 9 * i + 6]
+        out += [column[9 * i : 9 * i + 3] + odd, column[9 * i + 6 : 9 * i + 9] + odd]
+    return out + [column[27:29]]
 
 
 def xhalo_block(even, xa_ref, xb_ref, side, at, rows):
@@ -184,13 +180,12 @@
     h_ref[...] = own
 
     def write(upper_ref, lower_ref):
-        for (d, y), at in XFULL.items():
-            up, down = ((4 - d) * 4 + y) * 32, ((d - 1) * 4 + y) * 32
-            upper_ref[at : at + ROWS, :] = cols_ref[up : up + ROWS, :]
-            lower_ref[at : at + ROWS, :] = cols_ref[down : down + ROWS, :]
         for y in range(4):
-            put_faces(upper_ref, XFACE[y], cols_ref, y, 0, 1.0)
-            put_faces(lower_ref, XFACE[y], cols_ref, 12 + y, 0, -1.0)
+            column = [cols_ref[(x * 4 + y) * 32 : (x * 4 + y) * 32 + ROWS, :] for x in range(4)]
+            put(upper_ref, X1[y], [column[3]])
+            put(lower_ref, X1[y], [column[0]])
+            put(upper_ref, X2[y], far_modes(column[2], 0, 1.0))
+            put(lower_ref, X2[y], far_modes(column[1], 0, -1.0))
         for ref in (upper_ref, lower_ref):
             ref[XH : XH + ROWS, :] = own[0:ROWS]
 
@@ -200,30 +195,27 @@
 def ypay_kernel(cols_ref, xa_ref, xb_ref, h_ref, first_ref, second_ref):
     halo = functools.partial(xhalo_block, upper_first("gx"), xa_ref, xb_ref)
 
-    def corner(side, at, ysign):
-        xsign = 1.0 if side == 0 else -1.0
-        c = [halo(side, at + 9 * i, 9) for i in range(3)]
-        xface = c[0] + c[2] + xsign * c[1]
-        yface = [v[0:3] + v[6:9] + ysign * v[3:6] for v in c[1:]]
-        return (xface[0:3] - xsign * yface[0] - yface[1], xface[3:9], yface[0], yface[1], halo(side, at + 27, 1))
+    def edge(side, xd, y, ysign):
+        if xd == 1:
+            c = [halo(side, X1[y] + 9 * i, 9) for i in range(3)]
+            face, k = c[0] + c[2] + (1.0 if side == 0 else -1.0) * c[1], halo(side, X1[y] + 27, 1)
+        else:
+            face, k = halo(side, X2[y], 9) + halo(side, X2[y] + 9, 9), halo(side, X2[y] + 18, 1)
+        return [face[0:3] + face[6:9] + ysign * face[3:6], k]
 
     def write(upper_ref, lower_ref):
-        for (d, x), at in YFULL.items():
-            up, down = (x * 4 + 4 - d) * 32, (x * 4 + d - 1) * 32
-            upper_ref[at : at + ROWS, :] = cols_ref[up : up + ROWS, :]
-            lower_ref[at : at + ROWS, :] = cols_ref[down : down + ROWS, :]
         for x in range(4):
-            put_faces(upper_ref, YFACE[x], cols_ref, x * 4, 1, 1.0)
-            put_faces(lower_ref, YFACE[x], cols_ref, x * 4 + 3, 1, -1.0)
-        for (side, xd, d), at in zip(NEAR, YNEAR):
-            upper_ref[at : at + ROWS, :] = halo(side, XFULL[xd, 4 - d], ROWS)
-            lower_ref[at : at + ROWS, :] = halo(side, XFULL[xd, d - 1], ROWS)
-        for (side, xd, d), at in zip(EDGE, YEDGE):
-            for ref, y, sign in ((upper_ref, 4 - d, 1.0), (lower_ref, d - 1, -1.0)):
-                row = at
-                for part in corner(side, XFULL[xd, y], sign):
-                    ref[row : row + part.shape[0], :] = part
-                    row += part.shape[0]
+            column = [cols_ref[(x * 4 + y) * 32 : (x * 4 + y) * 32 + ROWS, :] for y in range(4)]
+            put(upper_ref, Y1[x], [column[3]])
+            put(lower_ref, Y1[x], [column[0]])
+            put(upper_ref, Y2[x], far_modes(column[2], 1, 1.0))
+            put(lower_ref, Y2[x], far_modes(column[1], 1, -1.0))
+        for side, at in NEAR:
+            put(upper_ref, at, [halo(side, X1[3], ROWS)])
+            put(lower_ref, at, [halo(side, X1[0], ROWS)])
+        for side, xd, d, at in EDGE:
+            put(upper_ref, at, edge(side, xd, 4 - d, 1.0))
+            put(lower_ref, at, edge(side, xd, d - 1, -1.0))
         beside = jnp.where(lane_iota(ROWS) // 8 % 4 < 2, halo(1, XH, ROWS), halo(0, XH, ROWS))
         for ref in (upper_ref, lower_ref):
             ref[YH[0] : YH[0] + ROWS, :] = h_ref[0:ROWS, :]
@@ -245,13 +237,7 @@
 
 
 def shift_rows(v, up):
-    n = v.shape[0]
-    amount, edge = (7, 7) if up else (1, 0)
-    if n == 8:
-        return pltpu.roll(v, amount, axis=0)
-    a, b = pltpu.roll(v[0:8], amount, axis=0), pltpu.roll(v[8:16], amount, axis=0)
-    take = row_iota(8) == edge
-    return jnp.concatenate([jnp.where(take, b, a), jnp.where(take, a, b)], axis=0)
+    return pltpu.roll(v, 7 if up else 1, axis=0)
 
 
 def line_faces(values, stride):
@@ -260,21 +246,6 @@
         if base // stride % 3 == 0:
             e = values[base] + values[base + 2 * stride]
             out.append((e - values[base + stride], e + values[base + stride]))
-    return out
-
-
-def bounded(inner, outer, c, c_outer):
-    rows = row_iota(8)
-    top, bottom = rows == 7, rows == 0
-    turn = jnp.where(bottom, -1.0, 1.0)
-    c_below = pltpu.roll(c_outer, 1, axis=0)
-    out = []
-    for n, (low, high) in enumerate(line_faces(inner, 3)):
-        base = n // 3 * 9 + n % 3
-        beside = outer[base] + outer[base + 6] + turn * outer[base + 3]
-        up = c * (high - jnp.where(top, pltpu.roll(beside, 7, axis=0), pltpu.roll(low, 7, axis=0)))
-        down = jnp.where(bottom, c_below * (pltpu.roll(beside, 1, axis=0) - low), pltpu.roll(up, 1, axis=0))
-        out.append((down, up))
     return out
 
 
@@ -344,27 +315,23 @@
     even_x = upper_first("gx")
     fetch(((own_in, own_out), (cell_in, cell_ref)), sems)
 
-    def clear(n, _):
-        m0[pl.ds(pl.multiple_of(n * 128, 128), 128), :] = jnp.zeros((128, 128), F32)
+    def clear(xi, _):
+        for m in range(ROWS):
+            m0[pl.ds(pl.multiple_of(xi * 512 + 16 * m, 16), 8), :] = jnp.zeros((8, 128), F32)
         return 0
 
-    lax.fori_loop(0, 48, clear, 0)
+    lax.fori_loop(1, 11, clear, 0)
     h0[...] = jnp.zeros((512, 128), F32)
     xhalo = functools.partial(xhalo_block, even_x, xa_ref, xb_ref)
     for c in range(16):
         place(m0, c // 4, c % 4, cols_ref[c * 32 : c * 32 + ROWS, :])
     for side in (0, 1):
-        for d in range(1, 4):
-            x = -d if side == 0 else 3 + d
-            for y in range(4):
-                place(m0, x, y, xhalo(side, XFULL[d, y], ROWS))
-        x = -4 if side == 0 else 7
         for y in range(4):
-            block = xhalo(side, XFACE[y], 10)
-            at = (x + 4) * 512 + slot(y)
-            m0[pl.ds(at, 8, stride=16), :] = block[0:8]
-            m0[pl.ds(at + 8 * 16, 1), :] = block[8:9]
-            m0[pl.ds(at + 27 * 16, 1), :] = block[9:10]
+            place(m0, -1 if side == 0 else 4, y, xhalo(side, X1[y], ROWS))
+            block = xhalo(side, X2[y], FAR)
+            at = (2 if side == 0 else 9) * 512 + slot(y)
+            m0[pl.ds(at, 9, stride=16), :] = block[0:9]
+            m0[pl.ds(at + 18 * 16, 11, stride=16), :] = block[9:20]
     blocks = [xhalo(0, XH, ROWS), h_ref[0:ROWS, :], xhalo(1, XH, ROWS)]
     for y in range(4):
         place_h(h0, slot(y), y, blocks)
@@ -414,50 +381,44 @@
         return jnp.where(even_y, b, a) if side == 0 else jnp.where(even_y, a, b)
 
     for side in (0, 1):
-        out = [-d if side == 0 else 3 + d for d in range(5)]
-        for (d, x), at in YFULL.items():
-            place(m0, x, out[d], yhalo(side, at, ROWS))
+        out = [-d if side == 0 else 3 + d for d in range(3)]
         for x in range(4):
-            block = yhalo(side, YFACE[x], 10)
-            at = (x + 4) * 512 + slot(out[4])
+            place(m0, x, out[1], yhalo(side, Y1[x], ROWS))
+            block = yhalo(side, Y2[x], FAR)
+            at = (x + 4) * 512 + slot(out[2])
             for i in range(3):
-                for l in range(3):
-                    m0[pl.ds(at + mode(i, 0, l) * 16, 1), :] = block[3 * i + l : 3 * i + l + 1]
-            m0[pl.ds(at + 27 * 16, 1), :] = block[9:10]
-        for (xside, xd, d), at in zip(NEAR, YNEAR):
-            place(m0, -xd if xside == 0 else 3 + xd, out[d], yhalo(side, at, ROWS))
-        for (xside, xd, d), at in zip(EDGE, YEDGE):
-            block = yhalo(side, at, 16)
+                for j in (0, 1):
+                    row = 6 * i + 3 * j
+                    m0[pl.ds(at + (9 * i + 6 * j) * 16, 3, stride=16), :] = block[row : row + 3]
+            m0[pl.ds(at + 27 * 16, 2, stride=16), :] = block[18:20]
+        for xside, at in NEAR:
+            place(m0, -1 if xside == 0 else 4, out[1], yhalo(side, at, ROWS))
+        for xside, xd, d, at in EDGE:
+            block = yhalo(side, at, 4)
             to = ((-xd if xside == 0 else 3 + xd) + 4) * 512 + slot(out[d])
-            m0[pl.ds(to, 8, stride=16), :] = block[0:8]
-            for row, m in enumerate((8, 9, 10, 11, 18, 19, 20, 27), 8):
-                m0[pl.ds(to + 16 * m, 1), :] = block[row : row + 1]
+            m0[pl.ds(to, 3, stride=16), :] = block[0:3]
+            m0[pl.ds(to + 27 * 16, 1), :] = block[3:4]
         beside = yhalo(side, YH[1], ROWS)
         blocks = [beside, yhalo(side, YH[0], ROWS), beside]
-        for y in range(4):
-            place_h(h0, slot(8 * side - 4 + y), y, blocks)
-
-    lane16 = lane_iota(16)
-    idx16 = lane16 % 8
-    kh = h0[27 * 16 : 28 * 16, :]
-    gk_src = jnp.where(idx16 == 5, roll_lanes(kh, 2), kh)
-    ch[0:16, :] = couple(kh, roll_lanes(kh, 120))
-    ch[16:32, :] = couple(kh, shift_rows(kh, True))
-    ch[32:48, :] = jnp.where((idx16 == 3) | (idx16 == 7), 0.0, couple(kh, roll_lanes(kh, 127)))
-
-    def kof(xi, n):
-        return m0[xi * 512 + 27 * 16 : xi * 512 + 27 * 16 + n, :]
-
-    for xi in range(11):
-        n = 16 if 2 <= xi < 9 else 8
-        at = slice(xi * 16, xi * 16 + n)
-        k = kof(xi, n)
-        cx[at, :] = couple(k, kof(xi + 1, n))
-        if xi == 0:
+        for d in (1, 2):
+            place_h(h0, slot(out[d]), out[d] % 4, blocks)
+
+    idx8 = lane8 % 8
+    kh = h0[27 * 16 : 27 * 16 + 8, :]
+    last_row = row_iota(8) == 7
+    gk_src = jnp.where(idx8 == 5, roll_lanes(kh, 2), kh)
+    ch[0:8, :] = couple(kh, roll_lanes(kh, 120))
+    ch[16:24, :] = jnp.where(last_row, 0.0, couple(kh, shift_rows(kh, True)))
+    ch[32:40, :] = jnp.where((idx8 == 3) | (idx8 == 7), 0.0, couple(kh, roll_lanes(kh, 127)))
+    ks = [m0[xi * 512 + 27 * 16 : xi * 512 + 27 * 16 + 8, :] for xi in range(1, 11)]
+    for xi in range(1, 10):
+        k, at = ks[xi - 1], slice(xi * 16, xi * 16 + 8)
+        cx[at, :] = couple(k, ks[xi])
+        if xi == 1:
             continue
-        gk = roll_lanes(gk_src[0:n], (123 - xi * 8) % 128)
-        cy[at, :] = couple(k, shift_rows(k, True))
-        czu[at, :] = couple(k, jnp.where(lane_iota(n) == 127, gk, roll_lanes(k, 127)))
+        gk = roll_lanes(gk_src, 123 - xi * 8)
+        cy[at, :] = jnp.where(last_row, 0.0, couple(k, shift_rows(k, True)))
+        czu[at, :] = couple(k, jnp.where(lane8 == 127, gk, roll_lanes(k, 127)))
         czd[at, :] = couple(k, gk)
 
     def rows_of(ref, xi, n):
@@ -470,10 +431,10 @@
         return [ref[16 * t : 16 * t + n, :] for t in range(9)]
 
     groups = [
-        [(1, 3, 8, False), (3, 4, 8, True), (4, 8, 16, False), (8, 9, 8, True), (9, 11, 8, False)],
-        [(2, 4, 8, False), (4, 8, 8, True), (8, 10, 8, False)],
-        [(3, 9, 8, False)],
-        [(4, 6, 8, False), (6, 8, 8, False)],
+        [(2, 10)],
+        [(3, 9)],
+        [(3, 9)],
+        [(4, 6), (6, 8)],
     ]
     live = live_ref[...]
     out_copies = [
@@ -493,7 +454,7 @@
     src, dst, hsrc, hdst = m0, m1, h0, h1
     for step in range(STEPS):
         last = step == STEPS - 1
-        hn = 16 if step == 0 else 8
+        hn = 8
         hv = [hsrc[16 * m : 16 * m + hn, :] for m in range(27)]
         lane_h = lane_iota(hn)
         idx_h = lane_h % 8
@@ -504,14 +465,15 @@
             for t in range(9):
                 q_ref[8 * t : 8 * t + 8, :] = zeros8
 
-        for first, end, n, beyond in groups[step]:
+        n = 8
+        for first, end in groups[step]:
             lane_n = lane_iota(n)
 
             def xflux(here, there, xi, n=n):
                 c = at_x(cx, xi, n)
                 return tuple(c * (a[1] - b[0]) for a, b in zip(line_faces(here, 9), line_faces(there, 9)))
 
-            def body(xi, carry, n=n, src=src, dst=dst, step=step, last=last, lane_n=lane_n, beyond=beyond):
+            def body(xi, carry, n=n, src=src, dst=dst, step=step, last=last, lane_n=lane_n):
                 left = carry
                 values = rows_of(src, xi, n)
                 following = rows_of(src, xi + 1, n)
@@ -521,14 +483,10 @@
                 xm = [xtab[pl.ds((3 * step + t) * 16 + xi, 1), :] for t in range(3)]
                 heats = [heat * jnp.broadcast_to(v, (n, 128)) for v in xm]
                 c = at_x(cy, xi, n)
-                if beyond:
-                    outer = [src[pl.ds(pl.multiple_of(xi * 512 + 16 * m + 8, 8), 8), :] for m in range(27)]
-                    yf = bounded(values, outer, c, cy[pl.ds(pl.multiple_of(xi * 16 + 8, 8), 8), :])
-                else:
-                    yf = []
-                    for low, high in line_faces(values, 3):
-                        up = c * (high - shift_rows(low, True))
-                        yf.append((shift_rows(up, False), up))
+                yf = []
+                for low, high in line_faces(values, 3):
+                    up = c * (high - shift_rows(low, True))
+                    yf.append((shift_rows(up, False), up))
                 cu, cd = at_x(czu, xi, n), at_x(czd, xi, n)
                 zf = []
                 shift = 123 - xi * 8
@@ -574,13 +532,10 @@
                 up = c * (high - roll_lanes(low, 120))
                 xf.append((roll_lanes(up, 8), up))
             c = ch[16 : 16 + n, :]
-            if step == 0:
-                yf = bounded(inner, [v[8:16] for v in hv], c, ch[24:32, :])
-            else:
-                yf = []
-                for low, high in line_faces(inner, 3):
-                    up = c * (high - shift_rows(low, True))
-                    yf.append((shift_rows(up, False), up))
+            yf = []
+            for low, high in line_faces(inner, 3):
+                up = c * (high - shift_rows(low, True))
+                yf.append((shift_rows(up, False), up))
             c = ch[32 : 32 + n, :]
             zf = []
             for t, (low, high) in enumerate(line_faces(inner, 1)):

time: 66.6 us -> 63 us (0.946)
  the two profiles are of different devices: /device:TPU:19 before, /device:TPU:11 now
where the time goes in v4:
time: 63 us; the launch traced here: 62.6 us
  blocking collectives  27.9 us (44%)
  starting transfers between devices  17.8 us (28%)
  Pallas kernels  8.85 us (14%)
  waiting for transfers between devices  6.57 us (10%)
  between operations  1.41 us (2%)
    all_to_all x1, blocking collectives, program(): lax.all_to_all(pay.reshape(OWNERS, 1, 2304), 'gx', 0, 0, axis_index_group...  27.9 us
    ppermute x3, starting transfers between devices, swap(): b = lax.ppermute(second, axis, odd)  13.1 us
    pallas_call x6, Pallas kernels, call(): pl.pallas_call(kernel, out_shape=outs, in_specs=[pl.BlockSpec(memory_spac...  8.85 us
    ppermute x3, starting transfers between devices, swap(): a = lax.ppermute(first, axis, even)  4.64 us
    ppermute x3, waiting for transfers between devices, swap(): b = lax.ppermute(second, axis, odd)  4.02 us
    ppermute x3, waiting for transfers between devices, swap(): a = lax.ppermute(first, axis, even)  2.55 us
  transfers between devices with their start and end apart: 6, of which 3 were waited for; matrix products, arithmetic and copies ran while one was open for 0% of the time, Pallas kernels for 2%

profile of v4, /device:TPU:11, one launch (start us, length us, event | category | flops | bytes accessed | tf_op | source)
XLA Modules:
  0.0 62.6 jit_solution(14368513240464438204)
XLA Ops:
  1.3 1.3 %shard_map.112 = (f32[512,128]{1,0:T(8,128)S(1)}, f32[32,128]{1,0:T(8,128)S(1)}, f32[8,128]{1,0:T(8,128)S(1)}) custom-call(f32[27,16,128]{2,1,0:T(8,128)} %bitcast.12, f32[16,128]{1,0:T(8,128)} %bitcast.15, f32[16,128]{1,0:T(8,128)} %bitcast.16, s32[1,1,1]{2,1,0:T(1,128)S(6)} %copy.17.lay_ref), custom_call_target="tpu_custom_call" | custom-call | tf_op jit(solution)/shard_map/pallas_call | solution.py:50
  2.6 3.1 %collective-permute-start.1 = (f32[32,128]{1,0:T(8,128)S(1)}, f32[32,128]{1,0:T(8,128)S(1)}, u32[]{:S(2)}, u32[]{:S(2)}) collective-permute-start(f32[32,128]{1,0:T(8,128)S(1)} %get-tuple-element.25), channel_id=1, source_target_pairs={{1,2},{2,1},{5,6},{6,5},{9,10},{10,9},{13,14},{14,13},{17,18},{18,... | collective-permute-start | bytes 49160 | tf_op jit(solution)/shard_map/ppermute | solution.py:657
  5.7 1.9 %collective-permute-start = (f32[32,128]{1,0:T(8,128)S(1)}, f32[32,128]{1,0:T(8,128)S(1)}, u32[]{:S(2)}, u32[]{:S(2)}) collective-permute-start(f32[32,128]{1,0:T(8,128)S(1)} %get-tuple-element.25), channel_id=1, source_target_pairs={{0,1},{1,0},{2,3},{3,2},{4,5},{5,4},{6,7},{7,6},{8,9},{9,8},{10,11... | collective-permute-start | bytes 49160 | tf_op jit(solution)/shard_map/ppermute | solution.py:656
  7.6 0.0 collective-permute-done.1.zb_ref
  7.6 2.5 %collective-permute-done.za_ref = f32[32,128]{1,0:T(8,128)S(1)} collective-permute-done((f32[32,128]{1,0:T(8,128)S(1)}, f32[32,128]{1,0:T(8,128)S(1)}, u32[]{:S(2)}, u32[]{:S(2)}) %collective-permute-start) | collective-permute-done | bytes 16416 | tf_op jit(solution)/shard_map/ppermute | solution.py:656
  10.2 0.7 %collective-permute-start.2 = (f32[232,128]{1,0:T(8,128)S(1)}, f32[232,128]{1,0:T(8,128)S(1)}, u32[]{:S(2)}, u32[]{:S(2)}) collective-permute-start(f32[232,128]{1,0:T(8,128)S(1)} %get-tuple-element.27), channel_id=1, source_target_pairs={{0,32},{32,0},{64,96},{96,64},{128,160},{160,128},{192,224},{224,1... | collective-permute-start | bytes 356360 | tf_op jit(solution)/shard_map/ppermute | solution.py:656
  10.9 6.4 %collective-permute-start.3 = (f32[232,128]{1,0:T(8,128)S(1)}, f32[232,128]{1,0:T(8,128)S(1)}, u32[]{:S(2)}, u32[]{:S(2)}) collective-permute-start(f32[232,128]{1,0:T(8,128)S(1)} %get-tuple-element.28), channel_id=1, source_target_pairs={{32,64},{64,32},{96,128},{128,96},{160,192},{192,160},{224,256},{2... | collective-permute-start | bytes 356360 | tf_op jit(solution)/shard_map/ppermute | solution.py:657
  17.3 0.0 collective-permute-done.2.xa_ref
  17.3 2.3 %collective-permute-done.3.xb_ref = f32[232,128]{1,0:T(8,128)S(1)} collective-permute-done((f32[232,128]{1,0:T(8,128)S(1)}, f32[232,128]{1,0:T(8,128)S(1)}, u32[]{:S(2)}, u32[]{:S(2)}) %collective-permute-start.3) | collective-permute-done | bytes 118816 | tf_op jit(solution)/shard_map/ppermute | solution.py:657
  19.6 0.1 shard_map.115
  19.7 0.0 copy-start
  19.7 0.0 copy-start.1
  19.7 0.0 copy-start.2
  19.7 2.1 %collective-permute-start.4 = (f32[328,128]{1,0:T(8,128)S(1)}, f32[328,128]{1,0:T(8,128)S(1)}, u32[]{:S(2)}, u32[]{:S(2)}) collective-permute-start(f32[328,128]{1,0:T(8,128)S(1)} %get-tuple-element.37), channel_id=1, source_target_pairs={{0,4},{4,0},{8,12},{12,8},{16,20},{20,16},{24,28},{28,24},{1,5},{5... | collective-permute-start | bytes 503816 | tf_op jit(solution)/shard_map/ppermute | solution.py:656
  21.8 3.6 %collective-permute-start.5 = (f32[328,128]{1,0:T(8,128)S(1)}, f32[328,128]{1,0:T(8,128)S(1)}, u32[]{:S(2)}, u32[]{:S(2)}) collective-permute-start(f32[328,128]{1,0:T(8,128)S(1)} %get-tuple-element.38), channel_id=1, source_target_pairs={{4,8},{8,4},{12,16},{16,12},{20,24},{24,20},{5,9},{9,5},{13,17},{1... | collective-permute-start | bytes 503816 | tf_op jit(solution)/shard_map/ppermute | solution.py:657
  25.4 1.6 %shard_map.114 = (f32[6144,128]{1,0:T(8,128)S(1)}, f32[512,128]{1,0:T(8,128)S(1)}, f32[144,128]{1,0:T(8,128)S(1)}, f32[144,128]{1,0:T(8,128)S(1)}, f32[192,128]{...) custom-call(f32[512,128]{1,0:T(8,128)S(1)} %get-tuple-element.24.col, ...), custom_call_target="tpu_custom_call" | custom-call | tf_op jit(solution)/shard_map/pallas_call | solution.py:50
  27.0 0.0 collective-permute-done.4.ya_ref
  27.0 1.7 %collective-permute-done.5.yb_ref = f32[328,128]{1,0:T(8,128)S(1)} collective-permute-done((f32[328,128]{1,0:T(8,128)S(1)}, f32[328,128]{1,0:T(8,128)S(1)}, u32[]{:S(2)}, u32[]{:S(2)}) %collective-permute-start.5) | collective-permute-done | bytes 167968 | tf_op jit(solution)/shard_map/ppermute | solution.py:657
  28.7 5.2 %shard_map.116 = (f32[27,16,128]{2,1,0:T(8,128)}, f32[288,128]{1,0:T(8,128)S(1)}, f32[6144,128]{1,0:T(8,128)S(1)}, f32[512,128]{1,0:T(8,128)S(1)}) custom-call(f32[6144,128]{1,0:T(8,128)S(1)} %get-tuple-element.29.m0_in, f32[512,128]{1,0:T(8,128)S(1)} %get-tuple-element.30.h0_in, ...), custom_call_target="tpu_custom_call", output_to_operand_aliasing={{2}: (0, {}), {3}: (1, {})} | custom-call | tf_op jit(solution)/shard_map/pallas_call | solution.py:50
  33.9 27.9 %all_to_all.5 = f32[16,1,2304]{2,1,0:T(1,128)S(1)} all-to-all(f32[16,1,2304]{2,1,0:T(1,128)S(1)} %bitcast.10), channel_id=1, replica_groups={{256,288,320,352,384,416,448,480,0,32,64,96,128,160,192,224},{257,289,3..., dimensions={0} | all-to-all | bytes 294912 | tf_op jit(solution)/shard_map/all_to_all | solution.py:699
  61.8 0.0 copy-done
  61.8 0.0 copy-done.1
  61.8 0.0 copy-done.2
  61.8 0.8 %shard_map.117 = (f32[6,8,256]{2,1,0:T(8,128)}, f32[3,8,256]{2,1,0:T(8,128)}) custom-call(f32[288,128]{1,0:T(8,128)S(1)} %bitcast.9, f32[6,8,256]{2,1,0:T(8,128)S(1)} %copy-done, f32[6,8,256]{2,1,0:T(8,128)S(1)} %copy-done.1, f32[1,256]{1,0:T(1,128)S(1)} %bitcast.11), custom_call_target="tpu_custom_call" | custom-call | tf_op jit(solution)/shard_map/pallas_call | solution.py:50
  (1 shorter events, 0.0 us)
Async XLA Ops:
  2.6 5.1 %collective-permute-start.1 = (f32[32,128]{1,0:T(8,128)S(1)}, f32[32,128]{1,0:T(8,128)S(1)}, u32[]{:S(2)}, u32[]{:S(2)}) collective-permute-start(f32[32,128]{1,0:T(8,128)S(1)} %get-tuple-element.25), channel_id=1, source_target_pairs={{1,2},{2,1},{5,6},{6,5},{9,10},{10,9},{13,14},{14,13},{17,18},{18,... | collective-permute-start | bytes 49160 | tf_op jit(solution)/shard_map/ppermute | solution.py:657
  5.7 4.5 %collective-permute-start = (f32[32,128]{1,0:T(8,128)S(1)}, f32[32,128]{1,0:T(8,128)S(1)}, u32[]{:S(2)}, u32[]{:S(2)}) collective-permute-start(f32[32,128]{1,0:T(8,128)S(1)} %get-tuple-element.25), channel_id=1, source_target_pairs={{0,1},{1,0},{2,3},{3,2},{4,5},{5,4},{6,7},{7,6},{8,9},{9,8},{10,11... | collective-permute-start | bytes 49160 | tf_op jit(solution)/shard_map/ppermute | solution.py:656
  10.2 7.1 %collective-permute-start.2 = (f32[232,128]{1,0:T(8,128)S(1)}, f32[232,128]{1,0:T(8,128)S(1)}, u32[]{:S(2)}, u32[]{:S(2)}) collective-permute-start(f32[232,128]{1,0:T(8,128)S(1)} %get-tuple-element.27), channel_id=1, source_target_pairs={{0,32},{32,0},{64,96},{96,64},{128,160},{160,128},{192,224},{224,1... | collective-permute-start | bytes 356360 | tf_op jit(solution)/shard_map/ppermute | solution.py:656
  10.9 8.7 %collective-permute-start.3 = (f32[232,128]{1,0:T(8,128)S(1)}, f32[232,128]{1,0:T(8,128)S(1)}, u32[]{:S(2)}, u32[]{:S(2)}) collective-permute-start(f32[232,128]{1,0:T(8,128)S(1)} %get-tuple-element.28), channel_id=1, source_target_pairs={{32,64},{64,32},{96,128},{128,96},{160,192},{192,160},{224,256},{2... | collective-permute-start | bytes 356360 | tf_op jit(solution)/shard_map/ppermute | solution.py:657
  19.7 42.1 %copy-start = (f32[6,8,256]{2,1,0:T(8,128)S(1)}, f32[6,8,256]{2,1,0:T(8,128)}, u32[]{:S(2)}) copy-start(f32[6,8,256]{2,1,0:T(8,128)} %de_ref.1) | copy-start | bytes 147460
  19.7 42.1 %copy-start.1 = (f32[6,8,256]{2,1,0:T(8,128)S(1)}, f32[6,8,256]{2,1,0:T(8,128)}, u32[]{:S(2)}) copy-start(f32[6,8,256]{2,1,0:T(8,128)} %st_ref.1) | copy-start | bytes 147460
  19.7 42.1 %copy-start.2 = (f32[256]{0:T(256)S(1)}, f32[256]{0:T(256)}, u32[]{:S(2)}) copy-start(f32[256]{0:T(256)} %param.17) | copy-start | bytes 3076
  19.7 7.2 %collective-permute-start.4 = (f32[328,128]{1,0:T(8,128)S(1)}, f32[328,128]{1,0:T(8,128)S(1)}, u32[]{:S(2)}, u32[]{:S(2)}) collective-permute-start(f32[328,128]{1,0:T(8,128)S(1)} %get-tuple-element.37), channel_id=1, source_target_pairs={{0,4},{4,0},{8,12},{12,8},{16,20},{20,16},{24,28},{28,24},{1,5},{5... | collective-permute-start | bytes 503816 | tf_op jit(solution)/shard_map/ppermute | solution.py:656
  21.8 6.9 %collective-permute-start.5 = (f32[328,128]{1,0:T(8,128)S(1)}, f32[328,128]{1,0:T(8,128)S(1)}, u32[]{:S(2)}, u32[]{:S(2)}) collective-permute-start(f32[328,128]{1,0:T(8,128)S(1)} %get-tuple-element.38), channel_id=1, source_target_pairs={{4,8},{8,4},{12,16},{16,12},{20,24},{24,20},{5,9},{9,5},{13,17},{1... | collective-permute-start | bytes 503816 | tf_op jit(solution)/shard_map/ppermute | solution.py:657

commit v5 on v4

--- a/solution.py
+++ b/solution.py
@@ -368,8 +368,8 @@
 
 def main_kernel(
     m0_in, h0_in, yz, yzh, xtab, xhtab, old, bmat, xa_ref, xb_ref, ya_ref, yb_ref, h_ref, own_ref, live_ref,
-    t_hbm, pay_out, m0, h0,
-    t_out, sem, m1, h1, cx, cy, czu, czd, ch, gs, q_ref, inc, amat, csum,
+    t_out, pay_out, m0, h0,
+    m1, h1, cx, cy, czu, czd, ch, gs, q_ref, inc, amat, csum,
 ):
     del m0_in, h0_in
     even_y = upper_first("gy")
@@ -437,16 +437,11 @@
         [(4, 6), (6, 8)],
     ]
     live = live_ref[...]
-    out_copies = [
-        pltpu.make_async_copy(t_out.at[:, 8 * p : 8 * p + 8, :], t_hbm.at[:, 8 * p : 8 * p + 8, :], sem.at[p])
-        for p in range(2)
-    ]
 
     def finish(ref, p):
         modes = [pair(ref, p, m) for m in range(27)]
         for n, v in enumerate(nodal_grid(modes)):
             t_out[n, 8 * p : 8 * p + 8, :] = v
-        out_copies[p].start()
         for g, m in enumerate(LOW):
             at = 16 * g + 8 * p
             inc[at : at + 8, :] = (modes[m] - old[at : at + 8, :]) * live
@@ -511,7 +506,7 @@
                 return m0[pl.ds(pl.multiple_of(xi * 512 + 28 * 16, 8), n), :]
 
             left = xflux(rows_of(src, first - 1, n), rows_of(src, first, n), first - 1, n)
-            if end - first <= 2:
+            if end - first <= 8:
                 for xi in range(first, end):
                     left = body(xi, left)
                 if last:
@@ -570,8 +565,6 @@
         for g in range(8):
             pay_out[pl.ds(2 * g + h, 16, stride=18), :] = csum[pl.ds(128 * h + g, 16, stride=8), :]
         pay_out[pl.ds(16 + h, 16, stride=18), :] = total[256:272, 128 * h : 128 * h + 128]
-    for c in out_copies:
-        c.wait()
 
 
 def gradient_table():
@@ -597,7 +590,11 @@
     return out
 
 
-def mechanics_kernel(got_ref, de_ref, st_ref, lim_ref, stress_hbm, force_hbm, stress_out, force_out, sems):
+def mechanics_kernel(
+    got_ref, de_ref, st_ref, lim_ref, t_ref, stress_hbm, force_hbm, t_hbm, stress_out, force_out, sems, t_sem
+):
+    t_copy = pltpu.make_async_copy(t_ref, t_hbm, t_sem)
+    t_copy.start()
     sums = got_ref[0:18, :]
     for s in range(1, OWNERS):
         sums = sums + got_ref[18 * s : 18 * s + 18, :]
@@ -641,6 +638,7 @@
         for c in range(3):
             force_out[c, :, lanes] = forces[c]
     fetch(((stress_out, stress_hbm), (force_out, force_hbm)), sems)
+    t_copy.wait()
 
 
 def swap(first, second, axis, count):
@@ -687,21 +685,24 @@
     )
     t_new, pay, _, _ = call(
         main_kernel,
-        (pltpu.HBM((27, 16, 128), F32), vm(OWNERS * 18), vm(6144), vm(512)),
+        (pltpu.VMEM((27, 16, 128), F32), vm(OWNERS * 18), vm(6144), vm(512)),
         (m0, h0, yz, yzh, xtab, xhtab, old, bmat, xa, xb, ya, yb, hown, own, live),
         scratch=[
-            pltpu.VMEM((27, 16, 128), F32), pltpu.SemaphoreType.DMA((2,)), vm(6144), vm(512), vm(192), vm(192), vm(192), vm(192), vm(48), vm(144), vm(72), vm(128),
+            vm(6144), vm(512), vm(192), vm(192), vm(192), vm(192), vm(48), vm(144), vm(72), vm(128),
             pltpu.VMEM((272, 2048), jnp.bfloat16), vm(256),
         ],
         aliases={0: 2, 1: 3},
     )
     group = [(o + FIRST) % OWNERS for o in range(OWNERS)]
     got = lax.all_to_all(pay.reshape(OWNERS, 1, 2304), "gx", 0, 0, axis_index_groups=[group], tiled=True)
-    stress, forces = call(
+    stress, forces, t_new = call(
         mechanics_kernel,
-        (pltpu.HBM((6, 8, 256), F32), pltpu.HBM((3, 8, 256), F32)),
-        (got.reshape(OWNERS * 18, 128), de, st, lim.reshape(1, 256)),
-        scratch=[pltpu.VMEM((6, 8, 256), F32), pltpu.VMEM((3, 8, 256), F32), pltpu.SemaphoreType.DMA((2,))],
+        (pltpu.HBM((6, 8, 256), F32), pltpu.HBM((3, 8, 256), F32), pltpu.HBM((27, 16, 128), F32)),
+        (got.reshape(OWNERS * 18, 128), de, st, lim.reshape(1, 256), t_new),
+        scratch=[
+            pltpu.VMEM((6, 8, 256), F32), pltpu.VMEM((3, 8, 256), F32),
+            pltpu.SemaphoreType.DMA((2,)), pltpu.SemaphoreType.DMA,
+        ],
     )
     return t_new.reshape(3, 3, 3, 4, 4, 128), stress, forces
 

time: 63 us -> 61.2 us (0.971)
  Pallas kernels: 8.85 us -> 7.1 us
    pallas_call x6, Pallas kernels: 8.85 us -> 7.1 us  [call(): pl.pallas_call(kernel, out_shape=outs, in_specs=[pl.BlockSpec(memory_spac...]
  transfers between devices with their start and end apart: 6 -> 6, of which waited for: 3 -> 3; matrix products, arithmetic and copies ran while one was open for 0% -> 0% of each run, Pallas kernels for 2% -> 3%
where the time goes in v5:
time: 61.2 us; the launch traced here: 60.8 us
  blocking collectives  27.9 us (46%)
  starting transfers between devices  17.8 us (29%)
  Pallas kernels  7.1 us (12%)
  waiting for transfers between devices  6.57 us (11%)
  between operations  1.41 us (2%)
    all_to_all x1, blocking collectives, program(): lax.all_to_all(pay.reshape(OWNERS, 1, 2304), 'gx', 0, 0, axis_index_group...  27.9 us
    ppermute x3, starting transfers between devices, swap(): b = lax.ppermute(second, axis, odd)  13.1 us
    pallas_call x6, Pallas kernels, call(): pl.pallas_call(kernel, out_shape=outs, in_specs=[pl.BlockSpec(memory_spac...  7.1 us
    ppermute x3, starting transfers between devices, swap(): a = lax.ppermute(first, axis, even)  4.64 us
    ppermute x3, waiting for transfers between devices, swap(): b = lax.ppermute(second, axis, odd)  4.02 us
    ppermute x3, waiting for transfers between devices, swap(): a = lax.ppermute(first, axis, even)  2.55 us
  transfers between devices with their start and end apart: 6, of which 3 were waited for; matrix products, arithmetic and copies ran while one was open for 0% of the time, Pallas kernels for 3%

profile of v5, /device:TPU:11, one launch (start us, length us, event | category | flops | bytes accessed | tf_op | source)
XLA Modules:
  0.0 60.8 jit_solution(4333079027428513787)
XLA Ops:
  1.3 1.3 %shard_map.112 = (f32[512,128]{1,0:T(8,128)S(1)}, f32[32,128]{1,0:T(8,128)S(1)}, f32[8,128]{1,0:T(8,128)S(1)}) custom-call(f32[27,16,128]{2,1,0:T(8,128)} %bitcast.12, f32[16,128]{1,0:T(8,128)} %bitcast.15, f32[16,128]{1,0:T(8,128)} %bitcast.16, s32[1,1,1]{2,1,0:T(1,128)S(6)} %copy.17.lay_ref), custom_call_target="tpu_custom_call" | custom-call | tf_op jit(solution)/shard_map/pallas_call | solution.py:50
  2.6 3.1 %collective-permute-start.1 = (f32[32,128]{1,0:T(8,128)S(1)}, f32[32,128]{1,0:T(8,128)S(1)}, u32[]{:S(2)}, u32[]{:S(2)}) collective-permute-start(f32[32,128]{1,0:T(8,128)S(1)} %get-tuple-element.26), channel_id=1, source_target_pairs={{1,2},{2,1},{5,6},{6,5},{9,10},{10,9},{13,14},{14,13},{17,18},{18,... | collective-permute-start | bytes 49160 | tf_op jit(solution)/shard_map/ppermute | solution.py:655
  5.7 1.9 %collective-permute-start = (f32[32,128]{1,0:T(8,128)S(1)}, f32[32,128]{1,0:T(8,128)S(1)}, u32[]{:S(2)}, u32[]{:S(2)}) collective-permute-start(f32[32,128]{1,0:T(8,128)S(1)} %get-tuple-element.26), channel_id=1, source_target_pairs={{0,1},{1,0},{2,3},{3,2},{4,5},{5,4},{6,7},{7,6},{8,9},{9,8},{10,11... | collective-permute-start | bytes 49160 | tf_op jit(solution)/shard_map/ppermute | solution.py:654
  7.6 0.0 collective-permute-done.1.zb_ref
  7.6 2.5 %collective-permute-done.za_ref = f32[32,128]{1,0:T(8,128)S(1)} collective-permute-done((f32[32,128]{1,0:T(8,128)S(1)}, f32[32,128]{1,0:T(8,128)S(1)}, u32[]{:S(2)}, u32[]{:S(2)}) %collective-permute-start) | collective-permute-done | bytes 16416 | tf_op jit(solution)/shard_map/ppermute | solution.py:654
  10.2 0.7 %collective-permute-start.2 = (f32[232,128]{1,0:T(8,128)S(1)}, f32[232,128]{1,0:T(8,128)S(1)}, u32[]{:S(2)}, u32[]{:S(2)}) collective-permute-start(f32[232,128]{1,0:T(8,128)S(1)} %get-tuple-element.28), channel_id=1, source_target_pairs={{0,32},{32,0},{64,96},{96,64},{128,160},{160,128},{192,224},{224,1... | collective-permute-start | bytes 356360 | tf_op jit(solution)/shard_map/ppermute | solution.py:654
  10.9 6.4 %collective-permute-start.3 = (f32[232,128]{1,0:T(8,128)S(1)}, f32[232,128]{1,0:T(8,128)S(1)}, u32[]{:S(2)}, u32[]{:S(2)}) collective-permute-start(f32[232,128]{1,0:T(8,128)S(1)} %get-tuple-element.29), channel_id=1, source_target_pairs={{32,64},{64,32},{96,128},{128,96},{160,192},{192,160},{224,256},{2... | collective-permute-start | bytes 356360 | tf_op jit(solution)/shard_map/ppermute | solution.py:655
  17.3 0.0 collective-permute-done.2.xa_ref
  17.3 2.3 %collective-permute-done.3.xb_ref = f32[232,128]{1,0:T(8,128)S(1)} collective-permute-done((f32[232,128]{1,0:T(8,128)S(1)}, f32[232,128]{1,0:T(8,128)S(1)}, u32[]{:S(2)}, u32[]{:S(2)}) %collective-permute-start.3) | collective-permute-done | bytes 118816 | tf_op jit(solution)/shard_map/ppermute | solution.py:655
  19.6 0.1 shard_map.115
  19.7 0.0 copy-start
  19.7 0.0 copy-start.1
  19.7 0.0 copy-start.2
  19.7 2.1 %collective-permute-start.4 = (f32[328,128]{1,0:T(8,128)S(1)}, f32[328,128]{1,0:T(8,128)S(1)}, u32[]{:S(2)}, u32[]{:S(2)}) collective-permute-start(f32[328,128]{1,0:T(8,128)S(1)} %get-tuple-element.38), channel_id=1, source_target_pairs={{0,4},{4,0},{8,12},{12,8},{16,20},{20,16},{24,28},{28,24},{1,5},{5... | collective-permute-start | bytes 503816 | tf_op jit(solution)/shard_map/ppermute | solution.py:654
  21.8 3.6 %collective-permute-start.5 = (f32[328,128]{1,0:T(8,128)S(1)}, f32[328,128]{1,0:T(8,128)S(1)}, u32[]{:S(2)}, u32[]{:S(2)}) collective-permute-start(f32[328,128]{1,0:T(8,128)S(1)} %get-tuple-element.39), channel_id=1, source_target_pairs={{4,8},{8,4},{12,16},{16,12},{20,24},{24,20},{5,9},{9,5},{13,17},{1... | collective-permute-start | bytes 503816 | tf_op jit(solution)/shard_map/ppermute | solution.py:655
  25.4 1.6 %shard_map.114 = (f32[6144,128]{1,0:T(8,128)S(1)}, f32[512,128]{1,0:T(8,128)S(1)}, f32[144,128]{1,0:T(8,128)S(1)}, f32[144,128]{1,0:T(8,128)S(1)}, f32[192,128]{...) custom-call(f32[512,128]{1,0:T(8,128)S(1)} %get-tuple-element.25.col, ...), custom_call_target="tpu_custom_call" | custom-call | tf_op jit(solution)/shard_map/pallas_call | solution.py:50
  27.0 0.0 collective-permute-done.4.ya_ref
  27.0 1.7 %collective-permute-done.5.yb_ref = f32[328,128]{1,0:T(8,128)S(1)} collective-permute-done((f32[328,128]{1,0:T(8,128)S(1)}, f32[328,128]{1,0:T(8,128)S(1)}, u32[]{:S(2)}, u32[]{:S(2)}) %collective-permute-start.5) | collective-permute-done | bytes 167968 | tf_op jit(solution)/shard_map/ppermute | solution.py:655
  28.7 3.4 %shard_map.116 = (f32[27,16,128]{2,1,0:T(8,128)S(1)}, f32[288,128]{1,0:T(8,128)S(1)}, f32[6144,128]{1,0:T(8,128)S(1)}, f32[512,128]{1,0:T(8,128)S(1)}) custom-call(f32[6144,128]{1,0:T(8,128)S(1)} %get-tuple-element.30.m0_in, f32[512,128]{1,0:T(8,128)S(1)} %get-tuple-element.31.h0_in, ...), custom_call_target="tpu_custom_call", output_to_operand_aliasing={{2}: (0, {}), {3}: (1, {})} | custom-call | tf_op jit(solution)/shard_map/pallas_call | solution.py:50
  32.1 27.9 %all_to_all.5 = f32[16,1,2304]{2,1,0:T(1,128)S(1)} all-to-all(f32[16,1,2304]{2,1,0:T(1,128)S(1)} %bitcast.10), channel_id=1, replica_groups={{256,288,320,352,384,416,448,480,0,32,64,96,128,160,192,224},{257,289,3..., dimensions={0} | all-to-all | bytes 294912 | tf_op jit(solution)/shard_map/all_to_all | solution.py:697
  60.0 0.0 copy-done
  60.0 0.0 copy-done.1
  60.0 0.0 copy-done.2
  60.0 0.8 %shard_map.117 = (f32[6,8,256]{2,1,0:T(8,128)}, f32[3,8,256]{2,1,0:T(8,128)}, f32[27,16,128]{2,1,0:T(8,128)}) custom-call(f32[288,128]{1,0:T(8,128)S(1)} %bitcast.9, f32[6,8,256]{2,1,0:T(8,128)S(1)} %copy-done, f32[6,8,256]{2,1,0:T(8,128)S(1)} %copy-done.1, f32[1,256]{1,0:T(1,128)S(1)} %bitcast.11, f32[27,16,128]{2,1,0:T(8,128)S(1)} %get-tuple-element.43.t_ref), custom_call_target="tpu_custom_call" | custom-call | tf_op jit(solution)/shard_map/pallas_call | solution.py:50
  (1 shorter events, 0.0 us)
Async XLA Ops:
  2.6 5.1 %collective-permute-start.1 = (f32[32,128]{1,0:T(8,128)S(1)}, f32[32,128]{1,0:T(8,128)S(1)}, u32[]{:S(2)}, u32[]{:S(2)}) collective-permute-start(f32[32,128]{1,0:T(8,128)S(1)} %get-tuple-element.26), channel_id=1, source_target_pairs={{1,2},{2,1},{5,6},{6,5},{9,10},{10,9},{13,14},{14,13},{17,18},{18,... | collective-permute-start | bytes 49160 | tf_op jit(solution)/shard_map/ppermute | solution.py:655
  5.7 4.5 %collective-permute-start = (f32[32,128]{1,0:T(8,128)S(1)}, f32[32,128]{1,0:T(8,128)S(1)}, u32[]{:S(2)}, u32[]{:S(2)}) collective-permute-start(f32[32,128]{1,0:T(8,128)S(1)} %get-tuple-element.26), channel_id=1, source_target_pairs={{0,1},{1,0},{2,3},{3,2},{4,5},{5,4},{6,7},{7,6},{8,9},{9,8},{10,11... | collective-permute-start | bytes 49160 | tf_op jit(solution)/shard_map/ppermute | solution.py:654
  10.2 7.1 %collective-permute-start.2 = (f32[232,128]{1,0:T(8,128)S(1)}, f32[232,128]{1,0:T(8,128)S(1)}, u32[]{:S(2)}, u32[]{:S(2)}) collective-permute-start(f32[232,128]{1,0:T(8,128)S(1)} %get-tuple-element.28), channel_id=1, source_target_pairs={{0,32},{32,0},{64,96},{96,64},{128,160},{160,128},{192,224},{224,1... | collective-permute-start | bytes 356360 | tf_op jit(solution)/shard_map/ppermute | solution.py:654
  10.9 8.7 %collective-permute-start.3 = (f32[232,128]{1,0:T(8,128)S(1)}, f32[232,128]{1,0:T(8,128)S(1)}, u32[]{:S(2)}, u32[]{:S(2)}) collective-permute-start(f32[232,128]{1,0:T(8,128)S(1)} %get-tuple-element.29), channel_id=1, source_target_pairs={{32,64},{64,32},{96,128},{128,96},{160,192},{192,160},{224,256},{2... | collective-permute-start | bytes 356360 | tf_op jit(solution)/shard_map/ppermute | solution.py:655
  19.7 40.3 %copy-start = (f32[6,8,256]{2,1,0:T(8,128)S(1)}, f32[6,8,256]{2,1,0:T(8,128)}, u32[]{:S(2)}) copy-start(f32[6,8,256]{2,1,0:T(8,128)} %de_ref.1) | copy-start | bytes 147460
  19.7 40.3 %copy-start.1 = (f32[6,8,256]{2,1,0:T(8,128)S(1)}, f32[6,8,256]{2,1,0:T(8,128)}, u32[]{:S(2)}) copy-start(f32[6,8,256]{2,1,0:T(8,128)} %st_ref.1) | copy-start | bytes 147460
  19.7 40.3 %copy-start.2 = (f32[256]{0:T(256)S(1)}, f32[256]{0:T(256)}, u32[]{:S(2)}) copy-start(f32[256]{0:T(256)} %param.17) | copy-start | bytes 3076
  19.7 7.2 %collective-permute-start.4 = (f32[328,128]{1,0:T(8,128)S(1)}, f32[328,128]{1,0:T(8,128)S(1)}, u32[]{:S(2)}, u32[]{:S(2)}) collective-permute-start(f32[328,128]{1,0:T(8,128)S(1)} %get-tuple-element.38), channel_id=1, source_target_pairs={{0,4},{4,0},{8,12},{12,8},{16,20},{20,16},{24,28},{28,24},{1,5},{5... | collective-permute-start | bytes 503816 | tf_op jit(solution)/shard_map/ppermute | solution.py:654
  21.8 6.9 %collective-permute-start.5 = (f32[328,128]{1,0:T(8,128)S(1)}, f32[328,128]{1,0:T(8,128)S(1)}, u32[]{:S(2)}, u32[]{:S(2)}) collective-permute-start(f32[328,128]{1,0:T(8,128)S(1)} %get-tuple-element.39), channel_id=1, source_target_pairs={{4,8},{8,4},{12,16},{16,12},{20,24},{24,20},{5,9},{9,5},{13,17},{1... | collective-permute-start | bytes 503816 | tf_op jit(solution)/shard_map/ppermute | solution.py:655
